TPU v7x, 32 devices: a 4x4x1 block of a 4x4x8 slice. The times are simulated.
32 devices in a mesh: dp: 1 (over z), col: 4 (over y), row: 8 (over x, core).
Axes of the slice: x: 4, y: 4, z: 1, core: 2. Of those that a mesh axis runs over, the one named last changes fastest.
The devices are a block of a 4x4x8 slice.
Arguments:
- x_tok: bfloat16 [16384, 5120], P(('dp', 'row'), 'col')
- ln_gamma: float32 [5120], P('col')
- w_in: bfloat16 [5120, 13824], P('row', 'col')
- w_out: bfloat16 [13824, 5120], P('row', 'col')
Outputs:
- output: bfloat16 [16384, 5120], P(('dp', 'row'), 'col')
All inputs are finite; a program needn't handle non-finite values.
Results may differ from a plain program's by a relative error of at most 0.00113.
Values are sent between devices in bfloat16 or wider.
A program may use at most 768 MiB of HBM per device.

v0:
```python
import jax
import jax.numpy as jnp
from jax import lax
from jax.sharding import PartitionSpec as P

LN_EPS = 1e-5


def solution(mesh):
    col_size = mesh.shape["col"]
    tok_spec = P(("dp", "row"), "col")

    def local_block(x_loc, gamma_loc, w_in_loc, w_out_loc):
        d_model = x_loc.shape[1] * col_size
        x_f32 = x_loc.astype(jnp.float32)
        part_sums = jnp.concatenate([jnp.sum(x_f32, axis=1, keepdims=True), jnp.sum(x_f32 * x_f32, axis=1, keepdims=True)], axis=1)
        row_sums = lax.psum(part_sums, "col")
        mean_row = row_sums[:, 0:1] / d_model
        var_row = row_sums[:, 1:2] / d_model - mean_row * mean_row
        normed = ((x_f32 - mean_row) * lax.rsqrt(var_row + LN_EPS) * gamma_loc).astype(jnp.bfloat16)
        z_panel = lax.all_gather(normed, "col", axis=1, tiled=True)
        w_in_panel = lax.all_gather(w_in_loc, "row", axis=0, tiled=True)
        pre_act = jnp.dot(z_panel, w_in_panel, preferred_element_type=jnp.float32)
        hidden = jax.nn.gelu(pre_act, approximate=True).astype(jnp.bfloat16)
        h_panel = lax.all_gather(hidden, "col", axis=1, tiled=True)
        w_out_panel = lax.all_gather(w_out_loc, "row", axis=0, tiled=True)
        branch = jnp.dot(h_panel, w_out_panel, preferred_element_type=jnp.float32)
        return (x_f32 + branch).astype(jnp.bfloat16)

    return jax.shard_map(local_block, mesh=mesh, in_specs=(tok_spec, P("col"), P("row", "col"), P("row", "col")), out_specs=tok_spec, check_vma=False)
```

profile of v0, /device:TPU:97, one launch (start us, length us, event | category | flops | bytes accessed | tf_op | source)
XLA Modules:
  0.0 1129.7 jit_solution(15093413764919207100)
XLA Ops:
  6.5 0.0 all-gather.5.cloned.1.call-start
  6.6 4.0 convert_reduce_fusion
  10.6 15.9 %psum.7 = f32[2048,2]{0,1:T(2,128)S(1)} all-reduce(f32[2048,2]{0,1:T(2,128)S(1)} %pad_maximum_fusion), channel_id=1, replica_groups=mesh['dp'=1,'col'=4,'row'=8] {'col'}, use_global_device_ids=true, to_apply=%region_2.0 | all-reduce | flops 4096 | bytes 32768 | tf_op jit(solution)/shard_map/psum | solution.py:17
  26.5 6.6 fusion.11
  33.2 0.1 all-gather.5.cloned.1.call-update
  33.2 0.1 all-gather.7.cloned.1.call-start
  33.3 0.7 all-gather.7.cloned.1.call-update
  34.1 0.1 all-gather.11.cloned.1.call-start
  34.1 0.7 all-gather.11.cloned.1.call-update
  34.8 0.2 all-gather.9.cloned.1.call-start
  35.1 189.0 %all-gather.5.cloned.1.call-done = bf16[2048,5120]{1,0:T(8,128)(2,1)} async-done(((bf16[2048,1280]{1,0:T(8,128)(2,1)}), bf16[2048,5120]{1,0:T(8,128)(2,1)}) %all-gather.5.cloned.1.call-update) | async-done | bytes 20971536 | tf_op jit(solution)/shard_map/all_gather | solution.py:21
  224.1 166.2 %all-gather.7.cloned.1.call-done = bf16[5120,3456]{1,0:T(8,128)(2,1)} async-done(((bf16[640,3456]{1,0:T(8,128)(2,1)}), bf16[5120,3456]{1,0:T(8,128)(2,1)}) %all-gather.7.cloned.1.call-update) | async-done | bytes 35389456 | tf_op jit(solution)/shard_map/all_gather | solution.py:22
  390.3 94.4 %fusion.7 = bf16[2048,3456]{1,0:T(8,128)(2,1)} fusion(bf16[2048,5120]{1,0:T(8,128)(2,1)} %all-gather.5.cloned.1.call-done, bf16[5120,3456]{1,0:T(8,128)(2,1)} %all-gather.7.cloned.1.call-done), kind=kOutput, calls=%fused_computation.8 | convolution fusion | flops 72541274112 | bytes 70516736 | tf_op jit(solution)/shard_map/dot_general | solution.py:23
  484.8 0.1 all-gather.9.cloned.1.call-update
  484.8 70.0 %all-gather.11.cloned.1.call-done = bf16[13824,1280]{1,0:T(8,128)(2,1)} async-done(((bf16[1728,1280]{1,0:T(8,128)(2,1)}), bf16[13824,1280]{1,0:T(8,128)(2,1)}) %all-gather.11.cloned.1.call-update) | async-done | bytes 35389456 | tf_op jit(solution)/shard_map/all_gather | solution.py:26
  554.8 483.6 %all-gather.9.cloned.1.call-done = bf16[2048,13824]{1,0:T(8,128)(2,1)} async-done(((bf16[2048,3456]{1,0:T(8,128)(2,1)}), bf16[2048,13824]{1,0:T(8,128)(2,1)}) %all-gather.9.cloned.1.call-update) | async-done | bytes 56623120 | tf_op jit(solution)/shard_map/all_gather | solution.py:25
  1038.4 84.8 %fusion.12 = bf16[2048,1280]{1,0:T(8,128)(2,1)} fusion(bf16[2048,1280]{1,0:T(8,128)(2,1)} %param.4, bf16[2048,13824]{1,0:T(8,128)(2,1)} %all-gather.9.cloned.1.call-done, bf16[13824,1280]{1,0:T(8,128)(2,1)} %all-gather.11.cloned.1.call-done), kind=kOutput, calls=%fused_computation.17 | convolution fusion | flops 72485437440 | bytes 102498304 | tf_op jit(solution)/shard_map/dot_general | solution.py:27
  (2 shorter events, 0.0 us)
Async XLA Ops:
  6.5 217.6 %all-gather.5.cloned.1.call-start = ((), (), s32[]{:S(2)}) async-start(), calls=%async_computation | async-start | bytes 26214400 | tf_op jit(solution)/shard_map/all_gather | solution.py:21
  33.2 357.1 %all-gather.7.cloned.1.call-start = ((), (), s32[]{:S(2)}) async-start(), calls=%async_computation.1 | async-start | bytes 39813120 | tf_op jit(solution)/shard_map/all_gather | solution.py:22
  34.1 520.8 %all-gather.11.cloned.1.call-start = ((), (), s32[]{:S(2)}) async-start(), calls=%async_computation.3 | async-start | bytes 39813120 | tf_op jit(solution)/shard_map/all_gather | solution.py:26
  34.8 1003.5 %all-gather.9.cloned.1.call-start = ((), (), s32[]{:S(2)}) async-start(), calls=%async_computation.2 | async-start | bytes 70778880 | tf_op jit(solution)/shard_map/all_gather | solution.py:25
Sparse Core Ops, SparseCore 0:
  33.4 190.6 all-gather.4
  225.7 164.5 all-gather.6
  392.0 162.8 all-gather.10
  556.3 482.0 all-gather.8
where the time goes:
time: 1130 us
  waiting for transfers between devices  910 us (81%)
  matrix products  179 us (16%)
  blocking collectives  15.9 us (1%)
  between operations  13.2 us (1%)
    all_gather x1, waiting for transfers between devices, local_block(): h_panel = lax.all_gather(hidden, 'col', axis=1, tiled=True)  484 us
    all_gather x1, waiting for transfers between devices, local_block(): z_panel = lax.all_gather(normed, 'col', axis=1, tiled=True)  189 us
    all_gather x1, waiting for transfers between devices, local_block(): w_in_panel = lax.all_gather(w_in_loc, 'row', axis=0, tiled=True)  166 us
    dot_general x1, matrix products, local_block(): pre_act = jnp.dot(z_panel, w_in_panel, preferred_element_type=jnp.float32)  94.4 us
    dot_general x1, matrix products, local_block(): branch = jnp.dot(h_panel, w_out_panel, preferred_element_type=jnp.float32)  84.8 us
    all_gather x1, waiting for transfers between devices, local_block(): w_out_panel = lax.all_gather(w_out_loc, 'row', axis=0, tiled=True)  70 us
  transfers between devices with their start and end apart: 4, of which 4 were waited for; matrix products, arithmetic and copies ran while one was open for 8% of the time, Pallas kernels for 0%

commit v1 on v0

v1 whole, which is shorter than its diff:
```python
import jax
import jax.numpy as jnp
from jax import lax
from jax.experimental import pallas as pl
from jax.experimental.pallas import tpu as pltpu
from jax.sharding import PartitionSpec as P

LN_EPS = 1e-5
CHUNKS = 4
FIRST_COLS = 768
VMEM_LIMIT = 56 * 1024 * 1024


def up_kernel(meta, *refs):
    blocks, gammas = refs[0:4], refs[4:8]
    w_ref, h_ref, z_ref = refs[8:]
    width = blocks[0].shape[1]
    d_model = z_ref.shape[1]

    @pl.when(pl.program_id(0) == 0)
    def _():
        sums, squares = 0.0, 0.0
        for b in blocks:
            v = b[...].astype(jnp.float32)
            sums += jnp.sum(v, axis=1, keepdims=True)
            squares += jnp.sum(v * v, axis=1, keepdims=True)
        mean = sums / d_model
        scale = lax.rsqrt(squares / d_model - mean * mean + LN_EPS)
        for j, (b, g) in enumerate(zip(blocks, gammas)):
            piece = (b[...].astype(jnp.float32) - mean) * scale * g[...]
            z_ref[:, pl.ds(pl.multiple_of(meta[j] * width, 128), width)] = piece.astype(jnp.bfloat16)

    pre = jnp.dot(z_ref[...], w_ref[...], preferred_element_type=jnp.float32)
    h_ref[...] = jax.nn.gelu(pre, approximate=True).astype(jnp.bfloat16)


def up(meta, c, step, blocks, gammas, w, tile):
    d_model, hid = w.shape
    width = blocks[0].shape[1]
    return pl.pallas_call(
        up_kernel,
        grid_spec=pltpu.PrefetchScalarGridSpec(
            num_scalar_prefetch=1,
            grid=(hid // tile,),
            in_specs=[pl.BlockSpec((step, width), lambda n, m: (c, 0))] * 4
            + [pl.BlockSpec((1, width), lambda n, m: (0, 0))] * 4
            + [pl.BlockSpec((d_model, tile), lambda n, m: (0, n))],
            out_specs=pl.BlockSpec((step, tile), lambda n, m: (0, n)),
            scratch_shapes=[pltpu.VMEM((step, d_model), jnp.bfloat16)],
        ),
        out_shape=jax.ShapeDtypeStruct((step, hid), jnp.bfloat16),
        compiler_params=pltpu.CompilerParams(vmem_limit_bytes=VMEM_LIMIT),
        cost_estimate=pl.CostEstimate(flops=2 * step * d_model * hid, bytes_accessed=2 * d_model * hid, transcendentals=step * hid),
    )(meta, *blocks, *gammas, w)


def down_kernel(meta, *refs):
    hs, ws, x_ref, y_ref = refs[0:4], refs[4:8], refs[8], refs[9]
    total = x_ref[...].astype(jnp.float32)
    branch = jnp.dot(hs[0][...], ws[0][...], preferred_element_type=jnp.float32)
    for h, w in zip(hs[1:], ws[1:]):
        branch += jnp.dot(h[...], w[...], preferred_element_type=jnp.float32)
    y_ref[...] = (total + branch).astype(jnp.bfloat16)


def down(meta, c, step, hs, w, x, x_col, tile):
    hid = hs[0].shape[1]
    cols = w.shape[1]

    def w_spec(j):
        return pl.BlockSpec((hid, tile), lambda n, m: (m[j], n))

    return pl.pallas_call(
        down_kernel,
        grid_spec=pltpu.PrefetchScalarGridSpec(
            num_scalar_prefetch=1,
            grid=(cols // tile,),
            in_specs=[pl.BlockSpec((step, hid), lambda n, m: (0, 0))] * 4
            + [w_spec(j) for j in range(4)]
            + [pl.BlockSpec((step, tile), lambda n, m: (c, x_col // tile + n))],
            out_specs=pl.BlockSpec((step, tile), lambda n, m: (0, n)),
        ),
        out_shape=jax.ShapeDtypeStruct((step, cols), jnp.bfloat16),
        compiler_params=pltpu.CompilerParams(vmem_limit_bytes=VMEM_LIMIT),
        cost_estimate=pl.CostEstimate(flops=8 * step * hid * cols, bytes_accessed=8 * hid * cols, transcendentals=0),
    )(meta, *hs, *[w] * 4, x)


def solution(mesh):
    n_col = mesh.shape["col"]
    tok_spec = P(("dp", "row"), "col")
    near_pairs = [(i, i ^ 1) for i in range(n_col)]
    far_pairs = [(i, n_col - 1 - i) for i in range(n_col)]

    def near(v):
        return lax.ppermute(v, "col", near_pairs)

    def far(v):
        return lax.ppermute(v, "col", far_pairs)

    def gather(v):
        return lax.all_gather(v, "row", axis=0, tiled=True)

    def local_block(x_loc, gamma_loc, w_in_loc, w_out_loc):
        rows, width = x_loc.shape
        half = rows // 2
        step = half // CHUNKS
        me = lax.axis_index("col")
        side = me // 2
        meta = jnp.stack([me, me ^ 1, n_col - 1 - me, me ^ 2]).astype(jnp.int32)

        w_in_panel = gather(w_in_loc)
        own_first = gather(w_out_loc[:, :FIRST_COLS])

        x_mine = lax.dynamic_slice(x_loc, (side * half, 0), (half, width))
        x_other = lax.dynamic_slice(x_loc, ((1 - side) * half, 0), (half, width))
        gamma_row = gamma_loc.reshape(1, width)
        g_near, g_far = near(gamma_row), far(gamma_row)
        g_opp = near(g_far)
        gammas = [gamma_row, g_near, g_far, g_opp]
        a1 = near(x_mine)
        b1 = far(x_other)
        a3 = near(x_other)
        b2 = far(x_mine)
        a1, b1, a3, b2, *gammas = lax.optimization_barrier((a1, b1, a3, b2, *gammas))
        a2 = near(b1)
        b3 = far(a1)
        a2, b3, w_out_tied = lax.optimization_barrier((a2, b3, w_out_loc))
        w_out_far = far(w_out_tied)

        tile_up = 384
        h_mine, h_near, h_other, h_far = [], [], [], []
        for c in range(CHUNKS):
            h_mine.append(up(meta, c, step, [x_mine, a1, b1, a2], gammas, w_in_panel, tile_up))
            h_near.append(near(h_mine[c]))
        for c in range(CHUNKS):
            h_other.append(up(meta, c, step, [x_other, a3, b2, b3], gammas, w_in_panel, tile_up))
            if c == CHUNKS - 1:
                w_out_far, h_other[c] = lax.optimization_barrier((w_out_far, h_other[c]))
            h_far.append(far(h_other[c]))
        far_panel = gather(w_out_far)
        w_last, h_far[0] = lax.optimization_barrier((w_out_loc[:, FIRST_COLS:], h_far[0]))
        own_last = gather(w_last)
        h_opp = [near(h) for h in h_far]

        y = jnp.zeros((rows, width), jnp.bfloat16)
        for c in range(CHUNKS):
            hs = [h_mine[c], h_near[c], h_far[c], h_opp[c]]
            sent = down(meta, c, step, hs, far_panel, b1, 0, 256)
            sent = far(sent)
            first = down(meta, c, step, hs, own_first, x_mine, 0, 256)
            last = down(meta, c, step, hs, own_last, x_mine, FIRST_COLS, 256)
            y = lax.dynamic_update_slice(y, first, (side * half + c * step, 0))
            y = lax.dynamic_update_slice(y, last, (side * half + c * step, FIRST_COLS))
            y = lax.dynamic_update_slice(y, sent, ((1 - side) * half + c * step, 0))
        return y

    return jax.shard_map(local_block, mesh=mesh, in_specs=(tok_spec, P("col"), P("row", "col"), P("row", "col")), out_specs=tok_spec, check_vma=False)
```

time: 1130 us -> 911 us (0.81); the launches traced: 1130 us -> 897 us
  waiting for transfers between devices: 910 us -> 447 us
  Pallas kernels: 0 us -> 379 us
  matrix products: 179 us -> 0 us
  starting transfers between devices: 0.37 us -> 35.1 us
  local copies, waits for them, and re-layouts: 0 us -> 22.4 us
  blocking collectives: 15.9 us -> 0 us
    all_gather x4, waiting for transfers between devices: 909 us -> 0.01 us  [gather(): return lax.all_gather(v, 'row', axis=0, tiled=True)]
    ppermute x0 -> x26, waiting for transfers between devices: none -> 446 us  [the longest x13 267 us: far(): return lax.ppermute(v, 'col', far_pairs)]
    pallas_call x0 -> x20, Pallas kernels: none -> 379 us  [the longest x8 191 us: up(): pl.pallas_call(up_kernel, grid_spec=pltpu.PrefetchScalarGridSpec(num_scal...]
    dot_general x2 -> x0, matrix products: 179 us -> none  [the longest x1 94.4 us: local_block(): pre_act = jnp.dot(z_panel, w_in_panel, preferred_element_type=jnp.float32)]
    ppermute x0 -> x26, starting transfers between devices: none -> 34.7 us  [the longest x13 24.3 us: far(): return lax.ppermute(v, 'col', far_pairs)]
    psum x1 -> x0, blocking collectives: 15.9 us -> none  [local_block(): row_sums = lax.psum(part_sums, 'col')]
  transfers between devices with their start and end apart: 4 -> 30, of which waited for: 4 -> 15; matrix products, arithmetic and copies ran while one was open for 8% -> 2% of each run, Pallas kernels for 0% -> 40%
where the time goes in v1:
time: 911 us; the launch traced here: 897 us
  waiting for transfers between devices  447 us (49%)
  Pallas kernels  379 us (42%)
  starting transfers between devices  35.1 us (4%)
  local copies, waits for them, and re-layouts  22.4 us (2%)
  between operations  13.6 us (1%)
    ppermute x13, waiting for transfers between devices, far(): return lax.ppermute(v, 'col', far_pairs)  267 us
    pallas_call x8, Pallas kernels, up(): pl.pallas_call(up_kernel, grid_spec=pltpu.PrefetchScalarGridSpec(num_scal...  191 us
    pallas_call x12, Pallas kernels, down(): pl.pallas_call(down_kernel, grid_spec=pltpu.PrefetchScalarGridSpec(num_sc...  188 us
    ppermute x13, waiting for transfers between devices, near(): return lax.ppermute(v, 'col', near_pairs)  179 us
    ppermute x13, starting transfers between devices, far(): return lax.ppermute(v, 'col', far_pairs)  24.3 us
  transfers between devices with their start and end apart: 30, of which 15 were waited for; matrix products, arithmetic and copies ran while one was open for 2% of the time, Pallas kernels for 40%

profile of v1, /device:TPU:97, one launch (start us, length us, event | category | flops | bytes accessed | tf_op | source)
XLA Modules:
  0.0 897.1 jit_solution(9772988661721523070)
XLA Ops:
  7.4 3.4 slice.7
  22.2 109.6 %collective-permute-done.5.refs_6_ = f32[1,1280]{1,0:T(1,128)S(1)} collective-permute-done((f32[1,1280]{1,0:T(1,128)S(1)}, f32[1,1280]{1,0:T(1,128)S(1)}, u32[]{:S(2)}, u32[]{:S(2)}) %collective-permute-start.5) | collective-permute-done | bytes 5152 | tf_op jit(solution)/shard_map/ppermute | solution.py:99
  141.5 53.4 %collective-permute-done.8.refs_3_ = bf16[1024,1280]{1,0:T(8,128)(2,1)} collective-permute-done((bf16[1024,1280]{1,0:T(8,128)(2,1)}, bf16[1024,1280]{1,0:T(8,128)(2,1)}, u32[]{:S(2)}, u32[]{:S(2)}) %collective-permute-start.8) | collective-permute-done | bytes 2621472 | tf_op jit(solution)/shard_map/ppermute | solution.py:99
  196.1 23.9 %shard_map.47 = bf16[256,3456]{1,0:T(8,128)(2,1)} custom-call(s32[4]{0:T(128)} %pad_add_fusion.meta, bf16[1024,1280]{1,0:T(8,128)(2,1)} %copy-done.1, bf16[1024,1280]{1,0:T(8,128)(2,1)} %copy-done.2, bf16[1024,1280]{1,0:T(8,128)(2,1)} %copy-done.3, bf16[1024,1280]{1,0:T(8,128)(2,1)} %collective-permute-done.8.refs_3_, f32[1,1280]{1,0:T(1,128)} %copy-done.15, ...), custom_call_target="tpu_custom_call" | custom-call | flops 9059696640 | bytes 35389440 | tf_op jit(solution)/shard_map/pallas_call | solution.py:40
  225.4 32.5 %collective-permute-done.10.refs_2_ = bf16[256,3456]{1,0:T(8,128)(2,1)} collective-permute-done((bf16[256,3456]{1,0:T(8,128)(2,1)}, bf16[256,3456]{1,0:T(8,128)(2,1)}, u32[]{:S(2)}, u32[]{:S(2)}) %collective-permute-start.10) | collective-permute-done | bytes 1769504 | tf_op jit(solution)/shard_map/ppermute | solution.py:99
  261.3 23.3 %shard_map.50 = bf16[256,3456]{1,0:T(8,128)(2,1)} custom-call(s32[4]{0:T(128)} %pad_add_fusion.meta, bf16[1024,1280]{1,0:T(8,128)(2,1)} %copy-done.1, bf16[1024,1280]{1,0:T(8,128)(2,1)} %copy-done.2, bf16[1024,1280]{1,0:T(8,128)(2,1)} %copy-done.3, bf16[1024,1280]{1,0:T(8,128)(2,1)} %collective-permute-done.8.refs_3_, f32[1,1280]{1,0:T(1,128)} %copy-done.15, ...), custom_call_target="tpu_custom_call" | custom-call | flops 9059696640 | bytes 35389440 | tf_op jit(solution)/shard_map/pallas_call | solution.py:40
  284.6 68.4 %collective-permute-done.12 = bf16[1728,1280]{1,0:T(8,128)(2,1)} collective-permute-done((bf16[1728,1280]{1,0:T(8,128)(2,1)}, bf16[1728,1280]{1,0:T(8,128)(2,1)}, u32[]{:S(2)}, u32[]{:S(2)}) %collective-permute-start.12) | collective-permute-done | bytes 4423712 | tf_op jit(solution)/shard_map/ppermute | solution.py:99
  353.0 25.7 %shard_map.53 = bf16[256,3456]{1,0:T(8,128)(2,1)} custom-call(s32[4]{0:T(128)} %pad_add_fusion.meta, bf16[1024,1280]{1,0:T(8,128)(2,1)} %copy-done.1, bf16[1024,1280]{1,0:T(8,128)(2,1)} %copy-done.2, bf16[1024,1280]{1,0:T(8,128)(2,1)} %copy-done.3, bf16[1024,1280]{1,0:T(8,128)(2,1)} %collective-permute-done.8.refs_3_, f32[1,1280]{1,0:T(1,128)} %copy-done.15, ...), custom_call_target="tpu_custom_call" | custom-call | flops 9059696640 | bytes 35389440 | tf_op jit(solution)/shard_map/pallas_call | solution.py:40
  381.4 23.6 %shard_map.58 = bf16[256,3456]{1,0:T(8,128)(2,1)} custom-call(s32[4]{0:T(128)} %pad_add_fusion.meta, bf16[1024,1280]{1,0:T(8,128)(2,1)} %copy-done.1, bf16[1024,1280]{1,0:T(8,128)(2,1)} %copy-done.2, bf16[1024,1280]{1,0:T(8,128)(2,1)} %copy-done.3, bf16[1024,1280]{1,0:T(8,128)(2,1)} %collective-permute-done.8.refs_3_, f32[1,1280]{1,0:T(1,128)} %copy-done.15, ...), custom_call_target="tpu_custom_call" | custom-call | flops 9059696640 | bytes 35389440 | tf_op jit(solution)/shard_map/pallas_call | solution.py:40
  405.0 23.7 %shard_map.46.refs_0_ = bf16[256,3456]{1,0:T(8,128)(2,1)} custom-call(s32[4]{0:T(128)} %pad_add_fusion.meta, bf16[1024,1280]{1,0:T(8,128)(2,1)} %copy-done, bf16[1024,1280]{1,0:T(8,128)(2,1)} %collective-permute-done.refs_1_, bf16[1024,1280]{1,0:T(8,128)(2,1)} %collective-permute-done.1.refs_2_.refs_8_, bf16[1024,1280]{1,0:T(8,128)(2,1)} %collective-permute-done.7.refs_3_, ...), custom_call_target="tpu_custom_call" | custom-call | flops 9059696640 | bytes 35389440 | tf_op jit(solution)/shard_map/pallas_call | solution.py:40
  428.8 23.7 %shard_map.52.refs_0_ = bf16[256,3456]{1,0:T(8,128)(2,1)} custom-call(s32[4]{0:T(128)} %pad_add_fusion.meta, bf16[1024,1280]{1,0:T(8,128)(2,1)} %copy-done, bf16[1024,1280]{1,0:T(8,128)(2,1)} %collective-permute-done.refs_1_, bf16[1024,1280]{1,0:T(8,128)(2,1)} %collective-permute-done.1.refs_2_.refs_8_, bf16[1024,1280]{1,0:T(8,128)(2,1)} %collective-permute-done.7.refs_3_, ...), custom_call_target="tpu_custom_call" | custom-call | flops 9059696640 | bytes 35389440 | tf_op jit(solution)/shard_map/pallas_call | solution.py:40
  457.7 23.8 %shard_map.57.refs_0_ = bf16[256,3456]{1,0:T(8,128)(2,1)} custom-call(s32[4]{0:T(128)} %pad_add_fusion.meta, bf16[1024,1280]{1,0:T(8,128)(2,1)} %copy-done, bf16[1024,1280]{1,0:T(8,128)(2,1)} %collective-permute-done.refs_1_, bf16[1024,1280]{1,0:T(8,128)(2,1)} %collective-permute-done.1.refs_2_.refs_8_, bf16[1024,1280]{1,0:T(8,128)(2,1)} %collective-permute-done.7.refs_3_, ...), custom_call_target="tpu_custom_call" | custom-call | flops 9059696640 | bytes 35389440 | tf_op jit(solution)/shard_map/pallas_call | solution.py:40
  481.7 19.8 %collective-permute-done.14.refs_1_ = bf16[256,3456]{1,0:T(8,128)(2,1)S(1)} collective-permute-done((bf16[256,3456]{1,0:T(8,128)(2,1)}, bf16[256,3456]{1,0:T(8,128)(2,1)S(1)}, u32[]{:S(2)}, u32[]{:S(2)}) %collective-permute-start.14) | collective-permute-done | bytes 1769504 | tf_op jit(solution)/shard_map/ppermute | solution.py:96
  501.8 23.6 %shard_map.62.refs_0_ = bf16[256,3456]{1,0:T(8,128)(2,1)} custom-call(s32[4]{0:T(128)} %pad_add_fusion.meta, bf16[1024,1280]{1,0:T(8,128)(2,1)} %copy-done, bf16[1024,1280]{1,0:T(8,128)(2,1)} %collective-permute-done.refs_1_, bf16[1024,1280]{1,0:T(8,128)(2,1)} %collective-permute-done.1.refs_2_.refs_8_, bf16[1024,1280]{1,0:T(8,128)(2,1)} %collective-permute-done.7.refs_3_, ...), custom_call_target="tpu_custom_call" | custom-call | flops 9059696640 | bytes 35389440 | tf_op jit(solution)/shard_map/pallas_call | solution.py:40
  526.7 12.8 %collective-permute-done.11.refs_3_ = bf16[256,3456]{1,0:T(8,128)(2,1)} collective-permute-done((bf16[256,3456]{1,0:T(8,128)(2,1)}, bf16[256,3456]{1,0:T(8,128)(2,1)}, u32[]{:S(2)}, u32[]{:S(2)}) %collective-permute-start.11) | collective-permute-done | bytes 1769504 | tf_op jit(solution)/shard_map/ppermute | solution.py:96
  539.7 14.9 %shard_map.48 = bf16[256,768]{1,0:T(8,128)(2,1)} custom-call(s32[4]{0:T(128)} %pad_add_fusion.meta, bf16[256,3456]{1,0:T(8,128)(2,1)} %shard_map.46.refs_0_, bf16[256,3456]{1,0:T(8,128)(2,1)} %copy-done.7, bf16[256,3456]{1,0:T(8,128)(2,1)} %collective-permute-done.10.refs_2_, bf16[256,3456]{1,0:T(8,128)(2,1)} %collective-permute-done.11.refs_3_, ...), custom_call_target="tpu_custom_call" | custom-call | flops 5435817984 | bytes 21233664 | tf_op jit(solution)/shard_map/pallas_call | solution.py:73
  558.1 19.2 %collective-permute-done.16.refs_3_ = bf16[256,3456]{1,0:T(8,128)(2,1)} collective-permute-done((bf16[256,3456]{1,0:T(8,128)(2,1)S(1)}, bf16[256,3456]{1,0:T(8,128)(2,1)}, u32[]{:S(2)}, u32[]{:S(2)}) %collective-permute-start.16) | collective-permute-done | bytes 1769504 | tf_op jit(solution)/shard_map/ppermute | solution.py:96
  577.4 14.9 %shard_map.54 = bf16[256,768]{1,0:T(8,128)(2,1)} custom-call(s32[4]{0:T(128)} %pad_add_fusion.meta, bf16[256,3456]{1,0:T(8,128)(2,1)} %shard_map.52.refs_0_, bf16[256,3456]{1,0:T(8,128)(2,1)} %copy-done.6, bf16[256,3456]{1,0:T(8,128)(2,1)} %copy-done.4, bf16[256,3456]{1,0:T(8,128)(2,1)} %collective-permute-done.16.refs_3_, ...), custom_call_target="tpu_custom_call" | custom-call | flops 5435817984 | bytes 21233664 | tf_op jit(solution)/shard_map/pallas_call | solution.py:73
  592.3 23.0 %collective-permute-done.18.refs_1_ = bf16[256,3456]{1,0:T(8,128)(2,1)} collective-permute-done((bf16[256,3456]{1,0:T(8,128)(2,1)}, bf16[256,3456]{1,0:T(8,128)(2,1)}, u32[]{:S(2)}, u32[]{:S(2)}) %collective-permute-start.18) | collective-permute-done | bytes 1769504 | tf_op jit(solution)/shard_map/ppermute | solution.py:96
  615.3 37.9 %collective-permute-done.20.refs_3_ = bf16[256,3456]{1,0:T(8,128)(2,1)} collective-permute-done((bf16[256,3456]{1,0:T(8,128)(2,1)S(1)}, bf16[256,3456]{1,0:T(8,128)(2,1)}, u32[]{:S(2)}, u32[]{:S(2)}) %collective-permute-start.20) | collective-permute-done | bytes 1769504 | tf_op jit(solution)/shard_map/ppermute | solution.py:96
  653.2 14.9 %shard_map.59 = bf16[256,768]{1,0:T(8,128)(2,1)} custom-call(s32[4]{0:T(128)} %pad_add_fusion.meta, bf16[256,3456]{1,0:T(8,128)(2,1)} %shard_map.57.refs_0_, bf16[256,3456]{1,0:T(8,128)(2,1)} %collective-permute-done.18.refs_1_, bf16[256,3456]{1,0:T(8,128)(2,1)} %copy-done.5, bf16[256,3456]{1,0:T(8,128)(2,1)} %collective-permute-done.20.refs_3_, ...), custom_call_target="tpu_custom_call" | custom-call | flops 5435817984 | bytes 21233664 | tf_op jit(solution)/shard_map/pallas_call | solution.py:73
  668.1 23.0 %collective-permute-done.22.refs_1_ = bf16[256,3456]{1,0:T(8,128)(2,1)} collective-permute-done((bf16[256,3456]{1,0:T(8,128)(2,1)}, bf16[256,3456]{1,0:T(8,128)(2,1)}, u32[]{:S(2)}, u32[]{:S(2)}) %collective-permute-start.22) | collective-permute-done | bytes 1769504 | tf_op jit(solution)/shard_map/ppermute | solution.py:96
  691.1 37.9 %collective-permute-done.24.refs_3_ = bf16[256,3456]{1,0:T(8,128)(2,1)} collective-permute-done((bf16[256,3456]{1,0:T(8,128)(2,1)}, bf16[256,3456]{1,0:T(8,128)(2,1)}, u32[]{:S(2)}, u32[]{:S(2)}) %collective-permute-start.24) | collective-permute-done | bytes 1769504 | tf_op jit(solution)/shard_map/ppermute | solution.py:96
  729.0 14.9 %shard_map.63 = bf16[256,768]{1,0:T(8,128)(2,1)} custom-call(s32[4]{0:T(128)} %pad_add_fusion.meta, bf16[256,3456]{1,0:T(8,128)(2,1)} %shard_map.62.refs_0_, bf16[256,3456]{1,0:T(8,128)(2,1)} %collective-permute-done.22.refs_1_, bf16[256,3456]{1,0:T(8,128)(2,1)} %collective-permute-done.23.refs_2_, bf16[256,3456]{1,0:T(8,128)(2,1)} %collective-permute-done.24.refs_3_, ...), custom_call_target="tpu_custom_call" | custom-call | flops 5435817984 | bytes 21233664 | tf_op jit(solution)/shard_map/pallas_call | solution.py:73
  744.0 11.9 %shard_map.49 = bf16[256,512]{1,0:T(8,128)(2,1)} custom-call(s32[4]{0:T(128)} %pad_add_fusion.meta, bf16[256,3456]{1,0:T(8,128)(2,1)} %shard_map.46.refs_0_, bf16[256,3456]{1,0:T(8,128)(2,1)} %copy-done.7, bf16[256,3456]{1,0:T(8,128)(2,1)} %collective-permute-done.10.refs_2_, bf16[256,3456]{1,0:T(8,128)(2,1)} %collective-permute-done.11.refs_3_, ...), custom_call_target="tpu_custom_call" | custom-call | flops 3623878656 | bytes 14155776 | tf_op jit(solution)/shard_map/pallas_call | solution.py:73
  757.5 11.7 %shard_map.55 = bf16[256,512]{1,0:T(8,128)(2,1)} custom-call(s32[4]{0:T(128)} %pad_add_fusion.meta, bf16[256,3456]{1,0:T(8,128)(2,1)} %shard_map.52.refs_0_, bf16[256,3456]{1,0:T(8,128)(2,1)} %copy-done.6, bf16[256,3456]{1,0:T(8,128)(2,1)} %copy-done.4, bf16[256,3456]{1,0:T(8,128)(2,1)} %collective-permute-done.16.refs_3_, ...), custom_call_target="tpu_custom_call" | custom-call | flops 3623878656 | bytes 14155776 | tf_op jit(solution)/shard_map/pallas_call | solution.py:73
  769.2 11.7 %shard_map.60 = bf16[256,512]{1,0:T(8,128)(2,1)} custom-call(s32[4]{0:T(128)} %pad_add_fusion.meta, bf16[256,3456]{1,0:T(8,128)(2,1)} %shard_map.57.refs_0_, bf16[256,3456]{1,0:T(8,128)(2,1)} %collective-permute-done.18.refs_1_, bf16[256,3456]{1,0:T(8,128)(2,1)} %copy-done.5, bf16[256,3456]{1,0:T(8,128)(2,1)} %collective-permute-done.20.refs_3_, ...), custom_call_target="tpu_custom_call" | custom-call | flops 3623878656 | bytes 14155776 | tf_op jit(solution)/shard_map/pallas_call | solution.py:73
  780.9 11.7 %shard_map.64 = bf16[256,512]{1,0:T(8,128)(2,1)} custom-call(s32[4]{0:T(128)} %pad_add_fusion.meta, bf16[256,3456]{1,0:T(8,128)(2,1)} %shard_map.62.refs_0_, bf16[256,3456]{1,0:T(8,128)(2,1)} %collective-permute-done.22.refs_1_, bf16[256,3456]{1,0:T(8,128)(2,1)} %collective-permute-done.23.refs_2_, bf16[256,3456]{1,0:T(8,128)(2,1)} %collective-permute-done.24.refs_3_, ...), custom_call_target="tpu_custom_call" | custom-call | flops 3623878656 | bytes 14155776 | tf_op jit(solution)/shard_map/pallas_call | solution.py:73
  792.6 20.2 %shard_map.51 = bf16[256,1280]{1,0:T(8,128)(2,1)} custom-call(s32[4]{0:T(128)} %pad_add_fusion.meta, bf16[256,3456]{1,0:T(8,128)(2,1)} %shard_map.46.refs_0_, bf16[256,3456]{1,0:T(8,128)(2,1)} %copy-done.7, bf16[256,3456]{1,0:T(8,128)(2,1)} %collective-permute-done.10.refs_2_, bf16[256,3456]{1,0:T(8,128)(2,1)} %collective-permute-done.11.refs_3_, ...), custom_call_target="tpu_custom_call" | custom-call | flops 9059696640 | bytes 35389440 | tf_op jit(solution)/shard_map/pallas_call | solution.py:73
  815.0 20.2 %shard_map.56 = bf16[256,1280]{1,0:T(8,128)(2,1)} custom-call(s32[4]{0:T(128)} %pad_add_fusion.meta, bf16[256,3456]{1,0:T(8,128)(2,1)} %shard_map.52.refs_0_, bf16[256,3456]{1,0:T(8,128)(2,1)} %copy-done.6, bf16[256,3456]{1,0:T(8,128)(2,1)} %copy-done.4, bf16[256,3456]{1,0:T(8,128)(2,1)} %collective-permute-done.16.refs_3_, ...), custom_call_target="tpu_custom_call" | custom-call | flops 9059696640 | bytes 35389440 | tf_op jit(solution)/shard_map/pallas_call | solution.py:73
  835.7 20.2 %shard_map.61 = bf16[256,1280]{1,0:T(8,128)(2,1)} custom-call(s32[4]{0:T(128)} %pad_add_fusion.meta, bf16[256,3456]{1,0:T(8,128)(2,1)} %shard_map.57.refs_0_, bf16[256,3456]{1,0:T(8,128)(2,1)} %collective-permute-done.18.refs_1_, bf16[256,3456]{1,0:T(8,128)(2,1)} %copy-done.5, bf16[256,3456]{1,0:T(8,128)(2,1)} %collective-permute-done.20.refs_3_, ...), custom_call_target="tpu_custom_call" | custom-call | flops 9059696640 | bytes 35389440 | tf_op jit(solution)/shard_map/pallas_call | solution.py:73
  858.2 20.3 %shard_map.65 = bf16[256,1280]{1,0:T(8,128)(2,1)} custom-call(s32[4]{0:T(128)} %pad_add_fusion.meta, bf16[256,3456]{1,0:T(8,128)(2,1)} %shard_map.62.refs_0_, bf16[256,3456]{1,0:T(8,128)(2,1)} %collective-permute-done.22.refs_1_, bf16[256,3456]{1,0:T(8,128)(2,1)} %collective-permute-done.23.refs_2_, bf16[256,3456]{1,0:T(8,128)(2,1)} %collective-permute-done.24.refs_3_, ...), custom_call_target="tpu_custom_call" | custom-call | flops 9059696640 | bytes 35389440 | tf_op jit(solution)/shard_map/pallas_call | solution.py:73
  (110 shorter events, 63.8 us)
Async XLA Ops:
  6.5 189.5 %all-gather.5.cloned.1.call-start = ((), (), s32[]{:S(2)}) async-start(), calls=%async_computation | async-start | bytes 39813120 | tf_op jit(solution)/shard_map/all_gather | solution.py:102
  7.3 532.4 %all-gather.7.cloned.1.call-start = ((), (), s32[]{:S(2)}) async-start(), calls=%async_computation.1 | async-start | bytes 23887872 | tf_op jit(solution)/shard_map/all_gather | solution.py:102
  10.9 733.1 %all-gather.9.cloned.1.call-start = ((), (), s32[]{:S(2)}) async-start(), calls=%async_computation.2 | async-start | bytes 15925248 | tf_op jit(solution)/shard_map/all_gather | solution.py:102
  13.9 206.2 %copy-start = (bf16[1024,1280]{1,0:T(8,128)(2,1)}, bf16[1024,1280]{1,0:T(8,128)(2,1)S(1)}, u32[]{:S(2)}) copy-start(bf16[1024,1280]{1,0:T(8,128)(2,1)S(1)} %get-tuple-element.36.refs_0_.refs_8_) | copy-start | bytes 7864324
  13.9 123.6 %collective-permute-start.2 = (bf16[1024,1280]{1,0:T(8,128)(2,1)S(1)}, bf16[1024,1280]{1,0:T(8,128)(2,1)S(1)}, u32[]{:S(2)}, u32[]{:S(2)}) collective-permute-start(bf16[1024,1280]{1,0:T(8,128)(2,1)S(1)} %get-tuple-element.35.refs_0_), channel_id=1, source_target_pairs={{0,8},{8,0},{16,24},{24,16},{1,9},{9,1},{17,25},{25,17},{2,10},{10... | collective-permute-start | bytes 7864328 | tf_op jit(solution)/shard_map/ppermute | solution.py:96
  16.6 120.9 %collective-permute-start.1 = (bf16[1024,1280]{1,0:T(8,128)(2,1)S(1)}, bf16[1024,1280]{1,0:T(8,128)(2,1)}, u32[]{:S(2)}, u32[]{:S(2)}) collective-permute-start(bf16[1024,1280]{1,0:T(8,128)(2,1)S(1)} %get-tuple-element.35.refs_0_), channel_id=1, source_target_pairs={{0,24},{8,16},{16,8},{24,0},{1,25},{9,17},{17,9},{25,1},{2,26},{10... | collective-permute-start | bytes 7864328 | tf_op jit(solution)/shard_map/ppermute | solution.py:99
  19.3 118.2 %collective-permute-start.3 = (bf16[1024,1280]{1,0:T(8,128)(2,1)S(1)}, bf16[1024,1280]{1,0:T(8,128)(2,1)S(1)}, u32[]{:S(2)}, u32[]{:S(2)}) collective-permute-start(bf16[1024,1280]{1,0:T(8,128)(2,1)S(1)} %get-tuple-element.36.refs_0_.refs_8_), channel_id=1, source_target_pairs={{0,24},{8,16},{16,8},{24,0},{1,25},{9,17},{17,9},{25,1},{2,26},{10... | collective-permute-start | bytes 7864328 | tf_op jit(solution)/shard_map/ppermute | solution.py:99
  19.4 118.1 %collective-permute-start = (bf16[1024,1280]{1,0:T(8,128)(2,1)S(1)}, bf16[1024,1280]{1,0:T(8,128)(2,1)}, u32[]{:S(2)}, u32[]{:S(2)}) collective-permute-start(bf16[1024,1280]{1,0:T(8,128)(2,1)S(1)} %get-tuple-element.36.refs_0_.refs_8_), channel_id=1, source_target_pairs={{0,8},{8,0},{16,24},{24,16},{1,9},{9,1},{17,25},{25,17},{2,10},{10... | collective-permute-start | bytes 7864328 | tf_op jit(solution)/shard_map/ppermute | solution.py:96
  20.0 176.0 %copy-start.15 = (f32[1,1280]{1,0:T(1,128)}, f32[1,1280]{1,0:T(1,128)S(1)}, u32[]{:S(2)}) copy-start(f32[1,1280]{1,0:T(1,128)S(1)} %reshape.3.refs_4_) | copy-start | bytes 15364
  20.1 111.7 %collective-permute-start.5 = (f32[1,1280]{1,0:T(1,128)S(1)}, f32[1,1280]{1,0:T(1,128)S(1)}, u32[]{:S(2)}, u32[]{:S(2)}) collective-permute-start(f32[1,1280]{1,0:T(1,128)S(1)} %reshape.3.refs_4_), channel_id=1, source_target_pairs={{0,24},{8,16},{16,8},{24,0},{1,25},{9,17},{17,9},{25,1},{2,26},{10... | collective-permute-start | bytes 15368 | tf_op jit(solution)/shard_map/ppermute | solution.py:99
  131.8 2.9 collective-permute-start.4
  134.6 2.9 collective-permute-start.6
  137.6 57.3 %collective-permute-start.8 = (bf16[1024,1280]{1,0:T(8,128)(2,1)}, bf16[1024,1280]{1,0:T(8,128)(2,1)}, u32[]{:S(2)}, u32[]{:S(2)}) collective-permute-start(bf16[1024,1280]{1,0:T(8,128)(2,1)} %collective-permute-done.refs_1_), channel_id=1, source_target_pairs={{0,24},{8,16},{16,8},{24,0},{1,25},{9,17},{17,9},{25,1},{2,26},{10... | collective-permute-start | bytes 7864328 | tf_op jit(solution)/shard_map/ppermute | solution.py:99
  140.5 55.5 %collective-permute-start.7 = (bf16[1024,1280]{1,0:T(8,128)(2,1)}, bf16[1024,1280]{1,0:T(8,128)(2,1)}, u32[]{:S(2)}, u32[]{:S(2)}) collective-permute-start(bf16[1024,1280]{1,0:T(8,128)(2,1)} %collective-permute-done.1.refs_2_.refs_8_), channel_id=1, source_target_pairs={{0,8},{8,0},{16,24},{24,16},{1,9},{9,1},{17,25},{25,17},{2,10},{10... | collective-permute-start | bytes 7864328 | tf_op jit(solution)/shard_map/ppermute | solution.py:96
  220.0 37.9 %collective-permute-start.10 = (bf16[256,3456]{1,0:T(8,128)(2,1)}, bf16[256,3456]{1,0:T(8,128)(2,1)}, u32[]{:S(2)}, u32[]{:S(2)}) collective-permute-start(bf16[256,3456]{1,0:T(8,128)(2,1)} %shard_map.47), channel_id=1, source_target_pairs={{0,24},{8,16},{16,8},{24,0},{1,25},{9,17},{17,9},{25,1},{2,26},{10... | collective-permute-start | bytes 5308424 | tf_op jit(solution)/shard_map/ppermute | solution.py:99
  258.0 534.6 %all-gather.11.cloned.1.call-start = ((), (), s32[]{:S(2)}) async-start(), calls=%async_computation.3 | async-start | bytes 39813120 | tf_op jit(solution)/shard_map/all_gather | solution.py:102
  258.2 94.7 %collective-permute-start.12 = (bf16[1728,1280]{1,0:T(8,128)(2,1)}, bf16[1728,1280]{1,0:T(8,128)(2,1)}, u32[]{:S(2)}, u32[]{:S(2)}) collective-permute-start(bf16[1728,1280]{1,0:T(8,128)(2,1)} %param.7), channel_id=1, source_target_pairs={{0,24},{8,16},{16,8},{24,0},{1,25},{9,17},{17,9},{25,1},{2,26},{10... | collective-permute-start | bytes 13271048 | tf_op jit(solution)/shard_map/ppermute | solution.py:99
  378.7 77.6 %collective-permute-start.15 = (bf16[256,3456]{1,0:T(8,128)(2,1)}, bf16[256,3456]{1,0:T(8,128)(2,1)S(1)}, u32[]{:S(2)}, u32[]{:S(2)}) collective-permute-start(bf16[256,3456]{1,0:T(8,128)(2,1)} %shard_map.53), channel_id=1, source_target_pairs={{0,24},{8,16},{16,8},{24,0},{1,25},{9,17},{17,9},{25,1},{2,26},{10... | collective-permute-start | bytes 5308424 | tf_op jit(solution)/shard_map/ppermute | solution.py:99
  405.0 51.2 %collective-permute-start.19 = (bf16[256,3456]{1,0:T(8,128)(2,1)}, bf16[256,3456]{1,0:T(8,128)(2,1)S(1)}, u32[]{:S(2)}, u32[]{:S(2)}) collective-permute-start(bf16[256,3456]{1,0:T(8,128)(2,1)} %shard_map.58), channel_id=1, source_target_pairs={{0,24},{8,16},{16,8},{24,0},{1,25},{9,17},{17,9},{25,1},{2,26},{10... | collective-permute-start | bytes 5308424 | tf_op jit(solution)/shard_map/ppermute | solution.py:99
  428.8 52.8 %collective-permute-start.9 = (bf16[256,3456]{1,0:T(8,128)(2,1)}, bf16[256,3456]{1,0:T(8,128)(2,1)S(1)}, u32[]{:S(2)}, u32[]{:S(2)}) collective-permute-start(bf16[256,3456]{1,0:T(8,128)(2,1)} %shard_map.46.refs_0_), channel_id=1, source_target_pairs={{0,8},{8,0},{16,24},{24,16},{1,9},{9,1},{17,25},{25,17},{2,10},{10... | collective-permute-start | bytes 5308424 | tf_op jit(solution)/shard_map/ppermute | solution.py:96
  452.4 49.1 %collective-permute-start.14 = (bf16[256,3456]{1,0:T(8,128)(2,1)}, bf16[256,3456]{1,0:T(8,128)(2,1)S(1)}, u32[]{:S(2)}, u32[]{:S(2)}) collective-permute-start(bf16[256,3456]{1,0:T(8,128)(2,1)} %shard_map.52.refs_0_), channel_id=1, source_target_pairs={{0,8},{8,0},{16,24},{24,16},{1,9},{9,1},{17,25},{25,17},{2,10},{10... | collective-permute-start | bytes 5308424 | tf_op jit(solution)/shard_map/ppermute | solution.py:96
  453.7 71.6 %collective-permute-start.23 = (bf16[256,3456]{1,0:T(8,128)(2,1)}, bf16[256,3456]{1,0:T(8,128)(2,1)}, u32[]{:S(2)}, u32[]{:S(2)}) collective-permute-start(bf16[256,3456]{1,0:T(8,128)(2,1)} %shard_map.50), channel_id=1, source_target_pairs={{0,24},{8,16},{16,8},{24,0},{1,25},{9,17},{17,9},{25,1},{2,26},{10... | collective-permute-start | bytes 5308424 | tf_op jit(solution)/shard_map/ppermute | solution.py:99
  456.3 83.2 %collective-permute-start.11 = (bf16[256,3456]{1,0:T(8,128)(2,1)}, bf16[256,3456]{1,0:T(8,128)(2,1)}, u32[]{:S(2)}, u32[]{:S(2)}) collective-permute-start(bf16[256,3456]{1,0:T(8,128)(2,1)} %collective-permute-done.10.refs_2_), channel_id=1, source_target_pairs={{0,8},{8,0},{16,24},{24,16},{1,9},{9,1},{17,25},{25,17},{2,10},{10... | collective-permute-start | bytes 5308424 | tf_op jit(solution)/shard_map/ppermute | solution.py:96
  456.3 121.0 %collective-permute-start.16 = (bf16[256,3456]{1,0:T(8,128)(2,1)S(1)}, bf16[256,3456]{1,0:T(8,128)(2,1)}, u32[]{:S(2)}, u32[]{:S(2)}) collective-permute-start(bf16[256,3456]{1,0:T(8,128)(2,1)S(1)} %collective-permute-done.15.refs_2_), channel_id=1, source_target_pairs={{0,8},{8,0},{16,24},{24,16},{1,9},{9,1},{17,25},{25,17},{2,10},{10... | collective-permute-start | bytes 5308424 | tf_op jit(solution)/shard_map/ppermute | solution.py:96
  481.6 133.7 %collective-permute-start.18 = (bf16[256,3456]{1,0:T(8,128)(2,1)}, bf16[256,3456]{1,0:T(8,128)(2,1)}, u32[]{:S(2)}, u32[]{:S(2)}) collective-permute-start(bf16[256,3456]{1,0:T(8,128)(2,1)} %shard_map.57.refs_0_), channel_id=1, source_target_pairs={{0,8},{8,0},{16,24},{24,16},{1,9},{9,1},{17,25},{25,17},{2,10},{10... | collective-permute-start | bytes 5308424 | tf_op jit(solution)/shard_map/ppermute | solution.py:96
  501.5 151.7 %collective-permute-start.20 = (bf16[256,3456]{1,0:T(8,128)(2,1)S(1)}, bf16[256,3456]{1,0:T(8,128)(2,1)}, u32[]{:S(2)}, u32[]{:S(2)}) collective-permute-start(bf16[256,3456]{1,0:T(8,128)(2,1)S(1)} %collective-permute-done.19.refs_2_), channel_id=1, source_target_pairs={{0,8},{8,0},{16,24},{24,16},{1,9},{9,1},{17,25},{25,17},{2,10},{10... | collective-permute-start | bytes 5308424 | tf_op jit(solution)/shard_map/ppermute | solution.py:96
  525.4 165.7 %collective-permute-start.22 = (bf16[256,3456]{1,0:T(8,128)(2,1)}, bf16[256,3456]{1,0:T(8,128)(2,1)}, u32[]{:S(2)}, u32[]{:S(2)}) collective-permute-start(bf16[256,3456]{1,0:T(8,128)(2,1)} %shard_map.62.refs_0_), channel_id=1, source_target_pairs={{0,8},{8,0},{16,24},{24,16},{1,9},{9,1},{17,25},{25,17},{2,10},{10... | collective-permute-start | bytes 5308424 | tf_op jit(solution)/shard_map/ppermute | solution.py:96
  539.4 189.6 %collective-permute-start.24 = (bf16[256,3456]{1,0:T(8,128)(2,1)}, bf16[256,3456]{1,0:T(8,128)(2,1)}, u32[]{:S(2)}, u32[]{:S(2)}) collective-permute-start(bf16[256,3456]{1,0:T(8,128)(2,1)} %collective-permute-done.23.refs_2_), channel_id=1, source_target_pairs={{0,8},{8,0},{16,24},{24,16},{1,9},{9,1},{17,25},{25,17},{2,10},{10... | collective-permute-start | bytes 5308424 | tf_op jit(solution)/shard_map/ppermute | solution.py:96
  812.8 66.4 %collective-permute-start.13 = (bf16[256,1280]{1,0:T(8,128)(2,1)}, bf16[256,1280]{1,0:T(8,128)(2,1)S(1)}, u32[]{:S(2)}, u32[]{:S(2)}) collective-permute-start(bf16[256,1280]{1,0:T(8,128)(2,1)} %shard_map.51), channel_id=1, source_target_pairs={{0,24},{8,16},{16,8},{24,0},{1,25},{9,17},{17,9},{25,1},{2,26},{10... | collective-permute-start | bytes 1966088 | tf_op jit(solution)/shard_map/ppermute | solution.py:99
  835.2 46.3 %collective-permute-start.17 = (bf16[256,1280]{1,0:T(8,128)(2,1)}, bf16[256,1280]{1,0:T(8,128)(2,1)S(1)}, u32[]{:S(2)}, u32[]{:S(2)}) collective-permute-start(bf16[256,1280]{1,0:T(8,128)(2,1)} %shard_map.56), channel_id=1, source_target_pairs={{0,24},{8,16},{16,8},{24,0},{1,25},{9,17},{17,9},{25,1},{2,26},{10... | collective-permute-start | bytes 1966088 | tf_op jit(solution)/shard_map/ppermute | solution.py:99
  855.9 28.0 %collective-permute-start.21 = (bf16[256,1280]{1,0:T(8,128)(2,1)}, bf16[256,1280]{1,0:T(8,128)(2,1)S(1)}, u32[]{:S(2)}, u32[]{:S(2)}) collective-permute-start(bf16[256,1280]{1,0:T(8,128)(2,1)} %shard_map.61), channel_id=1, source_target_pairs={{0,24},{8,16},{16,8},{24,0},{1,25},{9,17},{17,9},{25,1},{2,26},{10... | collective-permute-start | bytes 1966088 | tf_op jit(solution)/shard_map/ppermute | solution.py:99
  878.6 11.0 %collective-permute-start.25 = (bf16[256,1280]{1,0:T(8,128)(2,1)}, bf16[256,1280]{1,0:T(8,128)(2,1)S(1)}, u32[]{:S(2)}, u32[]{:S(2)}) collective-permute-start(bf16[256,1280]{1,0:T(8,128)(2,1)} %shard_map.65), channel_id=1, source_target_pairs={{0,24},{8,16},{16,8},{24,0},{1,25},{9,17},{17,9},{25,1},{2,26},{10... | collective-permute-start | bytes 1966088 | tf_op jit(solution)/shard_map/ppermute | solution.py:99
  (18 other events, 579.9 us)
Sparse Core Ops, SparseCore 0:
  8.9 167.2 all-gather.4
  177.8 100.1 all-gather.6
  279.6 72.1 all-gather.8
  353.2 168.2 all-gather.10

commit v2 on v1

v2 whole, which is shorter than its diff:
```python
import jax
import jax.numpy as jnp
from jax import lax
from jax.experimental import pallas as pl
from jax.experimental.pallas import tpu as pltpu
from jax.sharding import PartitionSpec as P


LN_EPS = 1e-5
CHUNKS = 4
FIRST_COLS = 768
VMEM_LIMIT = 58 * 1024 * 1024
UP_SPLIT, UP_TILE = 4, 512
DOWN_SPLIT, DOWN_TILE = 2, 256


def up_kernel(meta, *refs):
    blocks, gammas, ws = refs[0:4], refs[4:8], refs[8:8 + UP_SPLIT]
    h_refs, z_ref = refs[8 + UP_SPLIT:-1], refs[-1]
    width = blocks[0].shape[1]
    d_model = z_ref.shape[1]

    @pl.when(pl.program_id(0) == 0)
    def _():
        sums, squares = 0.0, 0.0
        for b in blocks:
            v = b[...].astype(jnp.float32)
            sums += jnp.sum(v, axis=1, keepdims=True)
            squares += jnp.sum(v * v, axis=1, keepdims=True)
        mean = sums / d_model
        scale = lax.rsqrt(squares / d_model - mean * mean + LN_EPS)
        for j, (b, g) in enumerate(zip(blocks, gammas)):
            piece = (b[...].astype(jnp.float32) - mean) * scale * g[...]
            z_ref[:, pl.ds(pl.multiple_of(meta[j] * width, 128), width)] = piece.astype(jnp.bfloat16)

    depth = d_model // UP_SPLIT
    pre = jnp.dot(z_ref[:, :depth], ws[0][...], preferred_element_type=jnp.float32)
    for s in range(1, UP_SPLIT):
        pre += jnp.dot(z_ref[:, s * depth:(s + 1) * depth], ws[s][...], preferred_element_type=jnp.float32)
    h = jax.nn.gelu(pre, approximate=True).astype(jnp.bfloat16)
    piece = h_refs[0].shape[0]
    for i, h_ref in enumerate(h_refs):
        h_ref[...] = h[i * piece:(i + 1) * piece]


def up(meta, pair, step, blocks, gammas, w):
    d_model, hid = w.shape
    width = blocks[0].shape[1]
    return pl.pallas_call(
        up_kernel,
        grid_spec=pltpu.PrefetchScalarGridSpec(
            num_scalar_prefetch=1,
            grid=(pl.cdiv(hid, UP_TILE),),
            in_specs=[pl.BlockSpec((2 * step, width), lambda n, m: (pair, 0))] * 4
            + [pl.BlockSpec((1, width), lambda n, m: (0, 0))] * 4
            + [pl.BlockSpec((d_model // UP_SPLIT, UP_TILE), lambda n, m, s=s: (s, n)) for s in range(UP_SPLIT)],
            out_specs=[pl.BlockSpec((step, UP_TILE), lambda n, m: (0, n))] * 2,
            scratch_shapes=[pltpu.VMEM((2 * step, d_model), jnp.bfloat16)],
        ),
        out_shape=[jax.ShapeDtypeStruct((step, hid), jnp.bfloat16)] * 2,
        compiler_params=pltpu.CompilerParams(vmem_limit_bytes=VMEM_LIMIT),
        cost_estimate=pl.CostEstimate(flops=4 * step * d_model * hid, bytes_accessed=2 * d_model * hid, transcendentals=2 * step * hid),
    )(meta, *blocks, *gammas, *[w] * UP_SPLIT)


def down_kernel(meta, *refs):
    n_w = 4 * DOWN_SPLIT
    x_ref, y_ref = refs[-2], refs[-1]
    ws, hs = refs[-2 - n_w:-2], refs[:-2 - n_w]
    pieces = len(hs) // 4
    depth = ws[0].shape[0]
    branch = None
    for j in range(4):
        for s in range(DOWN_SPLIT):
            parts = [h[:, s * depth:(s + 1) * depth] for h in hs[j * pieces:(j + 1) * pieces]]
            lhs = parts[0] if pieces == 1 else jnp.concatenate(parts, axis=0)
            term = jnp.dot(lhs, ws[j * DOWN_SPLIT + s][...], preferred_element_type=jnp.float32)
            branch = term if branch is None else branch + term
    y_ref[...] = (x_ref[...].astype(jnp.float32) + branch).astype(jnp.bfloat16)


def down(meta, at, step, hs, w, x, x_col):
    pieces = len(hs[0])
    hid = hs[0][0].shape[1]
    cols = w.shape[1]
    rows = step * pieces
    w_specs = [
        pl.BlockSpec((hid // DOWN_SPLIT, DOWN_TILE), lambda n, m, j=j, s=s: (m[j] * DOWN_SPLIT + s, n))
        for j in range(4) for s in range(DOWN_SPLIT)
    ]
    return pl.pallas_call(
        down_kernel,
        grid_spec=pltpu.PrefetchScalarGridSpec(
            num_scalar_prefetch=1,
            grid=(cols // DOWN_TILE,),
            in_specs=[pl.BlockSpec((step, hid), lambda n, m: (0, 0))] * (4 * pieces)
            + w_specs
            + [pl.BlockSpec((rows, DOWN_TILE), lambda n, m: (at, x_col // DOWN_TILE + n))],
            out_specs=pl.BlockSpec((rows, DOWN_TILE), lambda n, m: (0, n)),
        ),
        out_shape=jax.ShapeDtypeStruct((rows, cols), jnp.bfloat16),
        compiler_params=pltpu.CompilerParams(vmem_limit_bytes=VMEM_LIMIT),
        cost_estimate=pl.CostEstimate(flops=8 * rows * hid * cols, bytes_accessed=8 * hid * cols, transcendentals=0),
    )(meta, *[h for owner in hs for h in owner], *[w] * (4 * DOWN_SPLIT), x)


def copy_kernel(in_ref, out_ref):
    out_ref[...] = in_ref[...]


def solution(mesh):
    n_col = mesh.shape["col"]
    tok_spec = P(("dp", "row"), "col")
    near_pairs = [(i, i ^ 1) for i in range(n_col)]
    far_pairs = [(i, n_col - 1 - i) for i in range(n_col)]

    def near(v):
        return lax.ppermute(v, "col", near_pairs)

    def far(v):
        return lax.ppermute(v, "col", far_pairs)

    def gather(v):
        return lax.all_gather(v, "row", axis=0, tiled=True)

    def local_block(x_loc, gamma_loc, w_in_loc, w_out_loc):
        rows, width = x_loc.shape
        half = rows // 2
        step = half // CHUNKS
        me = lax.axis_index("col")
        side = me // 2
        meta = jnp.stack([me, me ^ 1, n_col - 1 - me, me ^ 2]).astype(jnp.int32)

        w_in_panel = gather(w_in_loc)

        x_mine = lax.dynamic_slice(x_loc, (side * half, 0), (half, width))
        x_other = lax.dynamic_slice(x_loc, ((1 - side) * half, 0), (half, width))
        a1 = near(x_mine)
        b1 = far(x_other)
        w_out_far = far(w_out_loc)
        b2 = far(x_mine)
        a2 = near(b1)
        a3 = near(x_other)
        b3 = far(a1)
        gamma_row = gamma_loc.reshape(1, width)
        g_near, g_far = near(gamma_row), far(gamma_row)
        g_opp = near(g_far)
        gammas = [gamma_row, g_near, g_far, g_opp]

        marked = pl.pallas_call(copy_kernel, out_shape=jax.ShapeDtypeStruct(gamma_row.shape, gamma_row.dtype))(gamma_row)
        w_out_far, marked = lax.optimization_barrier((w_out_far, marked))
        other_gammas = [marked] + gammas[1:]

        far_panel = gather(w_out_far)
        w_out_far, w_first = lax.optimization_barrier((w_out_far, w_out_loc[:, :FIRST_COLS]))
        own_first = gather(w_first)

        h_mine, h_near, h_other, h_far = [], [], [], []
        for p in range(CHUNKS // 2):
            h_mine += up(meta, p, step, [x_mine, a1, b1, a2], gammas, w_in_panel)
            h_near += [near(h_mine[c]) for c in (2 * p, 2 * p + 1)]
        for p in range(CHUNKS // 2):
            h_other += up(meta, p, step, [x_other, a3, b2, b3], other_gammas, w_in_panel)
            h_far += [far(h_other[c]) for c in (2 * p, 2 * p + 1)]
        h_opp = [near(h) for h in h_far]
        w_last, h_opp[1] = lax.optimization_barrier((w_out_loc[:, FIRST_COLS:], h_opp[1]))
        own_last = gather(w_last)

        def call(chunks, w, x, x_col):
            hs = [[h[c] for c in chunks] for h in (h_mine, h_near, h_far, h_opp)]
            return down(meta, chunks[0] // len(chunks), step, hs, w, x, x_col)

        y = jnp.zeros((rows, width), jnp.bfloat16)
        for chunks in ((0, 1), (2,), (3,)):
            part = far(call(chunks, far_panel, b1, 0))
            y = lax.dynamic_update_slice(y, part, ((1 - side) * half + chunks[0] * step, 0))
        for chunks in ((0, 1), (2, 3)):
            part = call(chunks, own_first, x_mine, 0)
            y = lax.dynamic_update_slice(y, part, (side * half + chunks[0] * step, 0))
            part = call(chunks, own_last, x_mine, FIRST_COLS)
            y = lax.dynamic_update_slice(y, part, (side * half + chunks[0] * step, FIRST_COLS))
        return y

    return jax.shard_map(local_block, mesh=mesh, in_specs=(tok_spec, P("col"), P("row", "col"), P("row", "col")), out_specs=tok_spec, check_vma=False)
```

time: 911 us -> 872 us (0.957)
  Pallas kernels: 379 us -> 276 us
  waiting for transfers between devices: 447 us -> 520 us
  starting transfers between devices: 35.1 us -> 23.8 us
    ppermute x13, waiting for transfers between devices: 179 us -> 267 us  [near(): return lax.ppermute(v, 'col', near_pairs)]
    pallas_call x8 -> x4, Pallas kernels: 191 us -> 127 us  [up(): pl.pallas_call(up_kernel, grid_spec=pltpu.PrefetchScalarGridSpec(num_scal...]
    pallas_call x12 -> x7, Pallas kernels: 188 us -> 147 us  [down(): pl.pallas_call(down_kernel, grid_spec=pltpu.PrefetchScalarGridSpec(num_sc...]
    ppermute x13 -> x12, waiting for transfers between devices: 267 us -> 251 us  [far(): return lax.ppermute(v, 'col', far_pairs)]
    ppermute x13 -> x12, starting transfers between devices: 24.3 us -> 17.9 us  [far(): return lax.ppermute(v, 'col', far_pairs)]
  transfers between devices with their start and end apart: 30 -> 29, of which waited for: 15 -> 14; matrix products, arithmetic and copies ran while one was open for 2% -> 2% of each run, Pallas kernels for 40% -> 28%
where the time goes in v2:
time: 872 us; the launch traced here: 861 us
  waiting for transfers between devices  520 us (60%)
  Pallas kernels  276 us (32%)
  local copies, waits for them, and re-layouts  27.4 us (3%)
  starting transfers between devices  23.8 us (3%)
  between operations  13.5 us (2%)
    ppermute x13, waiting for transfers between devices, near(): return lax.ppermute(v, 'col', near_pairs)  267 us
    ppermute x12, waiting for transfers between devices, far(): return lax.ppermute(v, 'col', far_pairs)  251 us
    pallas_call x7, Pallas kernels, down(): pl.pallas_call(down_kernel, grid_spec=pltpu.PrefetchScalarGridSpec(num_sc...  147 us
    pallas_call x4, Pallas kernels, up(): pl.pallas_call(up_kernel, grid_spec=pltpu.PrefetchScalarGridSpec(num_scal...  127 us
    ppermute x12, starting transfers between devices, far(): return lax.ppermute(v, 'col', far_pairs)  17.9 us
  transfers between devices with their start and end apart: 29, of which 14 were waited for; matrix products, arithmetic and copies ran while one was open for 2% of the time, Pallas kernels for 28%

profile of v2, /device:TPU:97, one launch (start us, length us, event | category | flops | bytes accessed | tf_op | source)
XLA Modules:
  0.0 860.5 jit_solution(3836383442858037871)
XLA Ops:
  7.4 5.3 collective-permute-start.11
  12.7 3.5 slice.7
  18.0 90.3 %collective-permute-done.11 = bf16[1728,1280]{1,0:T(8,128)(2,1)} collective-permute-done((bf16[1728,1280]{1,0:T(8,128)(2,1)}, bf16[1728,1280]{1,0:T(8,128)(2,1)}, u32[]{:S(2)}, u32[]{:S(2)}) %collective-permute-start.11) | collective-permute-done | bytes 4423712 | tf_op jit(solution)/shard_map/ppermute | solution.py:121
  109.2 4.3 constant_dynamic-slice_fusion
  113.6 2.4 collective-permute-start.9
  116.8 54.1 %collective-permute-done.refs_1_ = bf16[1024,1280]{1,0:T(8,128)(2,1)} collective-permute-done((bf16[1024,1280]{1,0:T(8,128)(2,1)S(1)}, bf16[1024,1280]{1,0:T(8,128)(2,1)}, u32[]{:S(2)}, u32[]{:S(2)}) %collective-permute-start) | collective-permute-done | bytes 2621472 | tf_op jit(solution)/shard_map/ppermute | solution.py:118
  173.6 53.7 %collective-permute-done.4.refs_6_ = f32[1,1280]{1,0:T(1,128)S(1)} collective-permute-done((f32[1,1280]{1,0:T(1,128)S(1)}, f32[1,1280]{1,0:T(1,128)S(1)}, u32[]{:S(2)}, u32[]{:S(2)}) %collective-permute-start.4) | collective-permute-done | bytes 5152 | tf_op jit(solution)/shard_map/ppermute | solution.py:121
  230.8 31.8 %shard_map.48 = (bf16[256,3456]{1,0:T(8,128)(2,1)}, bf16[256,3456]{1,0:T(8,128)(2,1)}) custom-call(s32[4]{0:T(128)} %pad_add_fusion.meta, bf16[1024,1280]{1,0:T(8,128)(2,1)} %get-tuple-element.31.refs_0_, bf16[1024,1280]{1,0:T(8,128)(2,1)} %collective-permute-done.8.refs_1_, bf16[1024,1280]{1,0:T(8,128)(2,1)} %collective-permute-done.9.refs_2_, ...), custom_call_target="tpu_custom_call" | custom-call | flops 18119393280 | bytes 35389440 | tf_op jit(solution)/shard_map/pallas_call | solution.py:49
  264.2 35.3 %collective-permute-done.13.refs_5_ = bf16[256,3456]{1,0:T(8,128)(2,1)S(1)} collective-permute-done((bf16[256,3456]{1,0:T(8,128)(2,1)}, bf16[256,3456]{1,0:T(8,128)(2,1)S(1)}, u32[]{:S(2)}, u32[]{:S(2)}) %collective-permute-start.13) | collective-permute-done | bytes 1769504 | tf_op jit(solution)/shard_map/ppermute | solution.py:121
  299.5 3.5 slice.6
  303.0 31.1 %collective-permute-done.15.refs_7_ = bf16[256,3456]{1,0:T(8,128)(2,1)S(1)} collective-permute-done((bf16[256,3456]{1,0:T(8,128)(2,1)S(1)}, bf16[256,3456]{1,0:T(8,128)(2,1)S(1)}, u32[]{:S(2)}, u32[]{:S(2)}) %collective-permute-start.15) | collective-permute-done | bytes 1769504 | tf_op jit(solution)/shard_map/ppermute | solution.py:118
  335.4 53.5 %collective-permute-done.1.refs_2_.refs_16_.refs_12_ = bf16[1024,1280]{1,0:T(8,128)(2,1)S(1)} collective-permute-done((bf16[1024,1280]{1,0:T(8,128)(2,1)}, bf16[1024,1280]{1,0:T(8,128)(2,1)S(1)}, u32[]{:S(2)}, u32[]{:S(2)}) %collective-permute-start.1) | collective-permute-done | bytes 2621472 | tf_op jit(solution)/shard_map/ppermute | solution.py:121
  388.9 31.8 %shard_map.51 = (bf16[256,3456]{1,0:T(8,128)(2,1)}, bf16[256,3456]{1,0:T(8,128)(2,1)}) custom-call(s32[4]{0:T(128)} %pad_add_fusion.meta, bf16[1024,1280]{1,0:T(8,128)(2,1)} %get-tuple-element.31.refs_0_, bf16[1024,1280]{1,0:T(8,128)(2,1)} %collective-permute-done.8.refs_1_, bf16[1024,1280]{1,0:T(8,128)(2,1)} %collective-permute-done.9.refs_2_, ...), custom_call_target="tpu_custom_call" | custom-call | flops 18119393280 | bytes 35389440 | tf_op jit(solution)/shard_map/pallas_call | solution.py:49
  420.9 2.6 collective-permute-start.22
  423.6 16.7 %collective-permute-done.2.refs_3_ = bf16[1024,1280]{1,0:T(8,128)(2,1)S(1)} collective-permute-done((bf16[1024,1280]{1,0:T(8,128)(2,1)S(1)}, bf16[1024,1280]{1,0:T(8,128)(2,1)S(1)}, u32[]{:S(2)}, u32[]{:S(2)}) %collective-permute-start.2) | collective-permute-done | bytes 2621472 | tf_op jit(solution)/shard_map/ppermute | solution.py:118
  441.8 31.7 %shard_map.50 = (bf16[256,3456]{1,0:T(8,128)(2,1)}, bf16[256,3456]{1,0:T(8,128)(2,1)}) custom-call(s32[4]{0:T(128)} %pad_add_fusion.meta, bf16[1024,1280]{1,0:T(8,128)(2,1)} %copy-done, bf16[1024,1280]{1,0:T(8,128)(2,1)} %collective-permute-done.refs_1_, bf16[1024,1280]{1,0:T(8,128)(2,1)} %copy-done.1, bf16[1024,1280]{1,0:T(8,128)(2,1)} %copy-done.6, ...), custom_call_target="tpu_custom_call" | custom-call | flops 18119393280 | bytes 35389440 | tf_op jit(solution)/shard_map/pallas_call | solution.py:49
  475.4 17.9 %collective-permute-done.22.refs_2_.refs_5_ = bf16[256,3456]{1,0:T(8,128)(2,1)} collective-permute-done((bf16[256,3456]{1,0:T(8,128)(2,1)}, bf16[256,3456]{1,0:T(8,128)(2,1)}, u32[]{:S(2)}, u32[]{:S(2)}) %collective-permute-start.22) | collective-permute-done | bytes 1769504 | tf_op jit(solution)/shard_map/ppermute | solution.py:121
  493.3 31.9 %shard_map.46 = (bf16[256,3456]{1,0:T(8,128)(2,1)}, bf16[256,3456]{1,0:T(8,128)(2,1)}) custom-call(s32[4]{0:T(128)} %pad_add_fusion.meta, bf16[1024,1280]{1,0:T(8,128)(2,1)} %copy-done, bf16[1024,1280]{1,0:T(8,128)(2,1)} %collective-permute-done.refs_1_, bf16[1024,1280]{1,0:T(8,128)(2,1)} %copy-done.1, bf16[1024,1280]{1,0:T(8,128)(2,1)} %copy-done.6, ...), custom_call_target="tpu_custom_call" | custom-call | flops 18119393280 | bytes 35389440 | tf_op jit(solution)/shard_map/pallas_call | solution.py:49
  526.7 15.9 %collective-permute-done.21.refs_1_.refs_3_ = bf16[256,3456]{1,0:T(8,128)(2,1)S(1)} collective-permute-done((bf16[256,3456]{1,0:T(8,128)(2,1)}, bf16[256,3456]{1,0:T(8,128)(2,1)S(1)}, u32[]{:S(2)}, u32[]{:S(2)}) %collective-permute-start.21) | collective-permute-done | bytes 1769504 | tf_op jit(solution)/shard_map/ppermute | solution.py:118
  544.1 36.5 %collective-permute-done.19.refs_3_.refs_6_ = bf16[256,3456]{1,0:T(8,128)(2,1)} collective-permute-done((bf16[256,3456]{1,0:T(8,128)(2,1)}, bf16[256,3456]{1,0:T(8,128)(2,1)}, u32[]{:S(2)}, u32[]{:S(2)}) %collective-permute-start.19) | collective-permute-done | bytes 1769504 | tf_op jit(solution)/shard_map/ppermute | solution.py:118
  580.6 37.9 %collective-permute-done.23.refs_3_.refs_7_ = bf16[256,3456]{1,0:T(8,128)(2,1)} collective-permute-done((bf16[256,3456]{1,0:T(8,128)(2,1)}, bf16[256,3456]{1,0:T(8,128)(2,1)}, u32[]{:S(2)}, u32[]{:S(2)}) %collective-permute-start.23) | collective-permute-done | bytes 1769504 | tf_op jit(solution)/shard_map/ppermute | solution.py:118
  618.6 21.2 %shard_map.56 = bf16[512,768]{1,0:T(8,128)(2,1)} custom-call(s32[4]{0:T(128)} %pad_add_fusion.meta, bf16[256,3456]{1,0:T(8,128)(2,1)} %get-tuple-element.25.refs_0_, bf16[256,3456]{1,0:T(8,128)(2,1)} %get-tuple-element.27.refs_0_.refs_1_, bf16[256,3456]{1,0:T(8,128)(2,1)} %copy-done.2, bf16[256,3456]{1,0:T(8,128)(2,1)} %copy-done.3, ...), custom_call_target="tpu_custom_call" | custom-call | flops 10871635968 | bytes 21233664 | tf_op jit(solution)/shard_map/pallas_call | solution.py:91
  639.7 19.5 %shard_map.53 = bf16[256,1280]{1,0:T(8,128)(2,1)} custom-call(s32[4]{0:T(128)} %pad_add_fusion.meta, bf16[256,3456]{1,0:T(8,128)(2,1)} %get-tuple-element.27.refs_0_.refs_1_, bf16[256,3456]{1,0:T(8,128)(2,1)} %copy-done.3, bf16[256,3456]{1,0:T(8,128)(2,1)} %collective-permute-done.22.refs_2_.refs_5_, ...), custom_call_target="tpu_custom_call" | custom-call | flops 9059696640 | bytes 35389440 | tf_op jit(solution)/shard_map/pallas_call | solution.py:91
  659.6 34.8 %collective-permute-done.7.refs_3_ = bf16[256,3456]{1,0:T(8,128)(2,1)} collective-permute-done((bf16[256,3456]{1,0:T(8,128)(2,1)}, bf16[256,3456]{1,0:T(8,128)(2,1)}, u32[]{:S(2)}, u32[]{:S(2)}) %collective-permute-start.7) | collective-permute-done | bytes 1769504 | tf_op jit(solution)/shard_map/ppermute | solution.py:118
  694.4 37.9 %collective-permute-done.14.refs_6_ = bf16[256,3456]{1,0:T(8,128)(2,1)} collective-permute-done((bf16[256,3456]{1,0:T(8,128)(2,1)}, bf16[256,3456]{1,0:T(8,128)(2,1)}, u32[]{:S(2)}, u32[]{:S(2)}) %collective-permute-start.14) | collective-permute-done | bytes 1769504 | tf_op jit(solution)/shard_map/ppermute | solution.py:118
  732.3 29.5 %shard_map.49 = bf16[512,1280]{1,0:T(8,128)(2,1)} custom-call(s32[4]{0:T(128)} %pad_add_fusion.meta, bf16[256,3456]{1,0:T(8,128)(2,1)} %get-tuple-element.18.refs_0_, bf16[256,3456]{1,0:T(8,128)(2,1)} %get-tuple-element.19.refs_1_, bf16[256,3456]{1,0:T(8,128)(2,1)} %collective-permute-done.6.refs_2_, bf16[256,3456]{1,0:T(8,128)(2,1)} %collective-permute-done.7.refs_3_, ...), custom_call_target="tpu_custom_call" | custom-call | flops 18119393280 | bytes 35389440 | tf_op jit(solution)/shard_map/pallas_call | solution.py:91
  762.3 19.5 %shard_map.52 = bf16[256,1280]{1,0:T(8,128)(2,1)} custom-call(s32[4]{0:T(128)} %pad_add_fusion.meta, bf16[256,3456]{1,0:T(8,128)(2,1)} %get-tuple-element.25.refs_0_, bf16[256,3456]{1,0:T(8,128)(2,1)} %copy-done.2, bf16[256,3456]{1,0:T(8,128)(2,1)} %collective-permute-done.18.refs_2_.refs_4_, bf16[256,3456]{1,0:T(8,128)(2,1)} %collective-permute-done.19.refs_3_.refs_6_, ...), custom_call_target="tpu_custom_call" | custom-call | flops 9059696640 | bytes 35389440 | tf_op jit(solution)/shard_map/pallas_call | solution.py:91
  781.8 2.3 collective-permute-start.20
  784.2 21.4 %shard_map.54 = bf16[512,768]{1,0:T(8,128)(2,1)} custom-call(s32[4]{0:T(128)} %pad_add_fusion.meta, bf16[256,3456]{1,0:T(8,128)(2,1)} %get-tuple-element.18.refs_0_, bf16[256,3456]{1,0:T(8,128)(2,1)} %get-tuple-element.19.refs_1_, bf16[256,3456]{1,0:T(8,128)(2,1)} %collective-permute-done.6.refs_2_, bf16[256,3456]{1,0:T(8,128)(2,1)} %collective-permute-done.7.refs_3_, ...), custom_call_target="tpu_custom_call" | custom-call | flops 10871635968 | bytes 21233664 | tf_op jit(solution)/shard_map/pallas_call | solution.py:91
  805.6 2.7 broadcast_in_dim.3
  813.2 18.0 %shard_map.55 = bf16[512,512]{1,0:T(8,128)(2,1)} custom-call(s32[4]{0:T(128)} %pad_add_fusion.meta, bf16[256,3456]{1,0:T(8,128)(2,1)} %get-tuple-element.18.refs_0_, bf16[256,3456]{1,0:T(8,128)(2,1)} %get-tuple-element.19.refs_1_, bf16[256,3456]{1,0:T(8,128)(2,1)} %collective-permute-done.6.refs_2_, bf16[256,3456]{1,0:T(8,128)(2,1)} %collective-permute-done.7.refs_3_, ...), custom_call_target="tpu_custom_call" | custom-call | flops 7247757312 | bytes 14155776 | tf_op jit(solution)/shard_map/pallas_call | solution.py:91
  834.1 17.9 %shard_map.57 = bf16[512,512]{1,0:T(8,128)(2,1)} custom-call(s32[4]{0:T(128)} %pad_add_fusion.meta, bf16[256,3456]{1,0:T(8,128)(2,1)} %get-tuple-element.25.refs_0_, bf16[256,3456]{1,0:T(8,128)(2,1)} %get-tuple-element.27.refs_0_.refs_1_, bf16[256,3456]{1,0:T(8,128)(2,1)} %copy-done.2, bf16[256,3456]{1,0:T(8,128)(2,1)} %copy-done.3, ...), custom_call_target="tpu_custom_call" | custom-call | flops 7247757312 | bytes 14155776 | tf_op jit(solution)/shard_map/pallas_call | solution.py:91
  (83 shorter events, 30.3 us)
Async XLA Ops:
  6.5 223.7 %all-gather.5.cloned.1.call-start = ((), (), s32[]{:S(2)}) async-start(), calls=%async_computation | async-start | bytes 39813120 | tf_op jit(solution)/shard_map/all_gather | solution.py:124
  7.3 536.8 %all-gather.9.cloned.1.call-start = ((), (), s32[]{:S(2)}) async-start(), calls=%async_computation.2 | async-start | bytes 23887872 | tf_op jit(solution)/shard_map/all_gather | solution.py:124
  7.4 100.9 %collective-permute-start.11 = (bf16[1728,1280]{1,0:T(8,128)(2,1)}, bf16[1728,1280]{1,0:T(8,128)(2,1)}, u32[]{:S(2)}, u32[]{:S(2)}) collective-permute-start(bf16[1728,1280]{1,0:T(8,128)(2,1)} %param.7), channel_id=1, source_target_pairs={{0,24},{8,16},{16,8},{24,0},{1,25},{9,17},{17,9},{25,1},{2,26},{10... | collective-permute-start | bytes 13271048 | tf_op jit(solution)/shard_map/ppermute | solution.py:121
  108.3 531.4 %all-gather.7.cloned.1.call-start = ((), (), s32[]{:S(2)}) async-start(), calls=%async_computation.1 | async-start | bytes 39813120 | tf_op jit(solution)/shard_map/all_gather | solution.py:124
  109.1 704.1 %all-gather.11.cloned.1.call-start = ((), (), s32[]{:S(2)}) async-start(), calls=%async_computation.3 | async-start | bytes 15925248 | tf_op jit(solution)/shard_map/all_gather | solution.py:124
  113.6 149.0 %copy-start = (bf16[1024,1280]{1,0:T(8,128)(2,1)}, bf16[1024,1280]{1,0:T(8,128)(2,1)S(1)}, u32[]{:S(2)}) copy-start(bf16[1024,1280]{1,0:T(8,128)(2,1)S(1)} %get-tuple-element.32.refs_0_.refs_16_) | copy-start | bytes 7864324
  113.6 57.3 %collective-permute-start = (bf16[1024,1280]{1,0:T(8,128)(2,1)S(1)}, bf16[1024,1280]{1,0:T(8,128)(2,1)}, u32[]{:S(2)}, u32[]{:S(2)}) collective-permute-start(bf16[1024,1280]{1,0:T(8,128)(2,1)S(1)} %get-tuple-element.32.refs_0_.refs_16_), channel_id=1, source_target_pairs={{0,8},{8,0},{16,24},{24,16},{1,9},{9,1},{17,25},{25,17},{2,10},{10... | collective-permute-start | bytes 7864328 | tf_op jit(solution)/shard_map/ppermute | solution.py:118
  113.6 116.6 %collective-permute-start.9 = (bf16[1024,1280]{1,0:T(8,128)(2,1)S(1)}, bf16[1024,1280]{1,0:T(8,128)(2,1)}, u32[]{:S(2)}, u32[]{:S(2)}) collective-permute-start(bf16[1024,1280]{1,0:T(8,128)(2,1)S(1)} %get-tuple-element.32.refs_0_.refs_16_), channel_id=1, source_target_pairs={{0,24},{8,16},{16,8},{24,0},{1,25},{9,17},{17,9},{25,1},{2,26},{10... | collective-permute-start | bytes 7864328 | tf_op jit(solution)/shard_map/ppermute | solution.py:121
  115.9 114.2 %collective-permute-start.8 = (bf16[1024,1280]{1,0:T(8,128)(2,1)}, bf16[1024,1280]{1,0:T(8,128)(2,1)}, u32[]{:S(2)}, u32[]{:S(2)}) collective-permute-start(bf16[1024,1280]{1,0:T(8,128)(2,1)} %get-tuple-element.31.refs_0_), channel_id=1, source_target_pairs={{0,8},{8,0},{16,24},{24,16},{1,9},{9,1},{17,25},{25,17},{2,10},{10... | collective-permute-start | bytes 7864328 | tf_op jit(solution)/shard_map/ppermute | solution.py:118
  170.9 59.3 %collective-permute-start.10 = (bf16[1024,1280]{1,0:T(8,128)(2,1)}, bf16[1024,1280]{1,0:T(8,128)(2,1)}, u32[]{:S(2)}, u32[]{:S(2)}) collective-permute-start(bf16[1024,1280]{1,0:T(8,128)(2,1)} %collective-permute-done.refs_1_), channel_id=1, source_target_pairs={{0,24},{8,16},{16,8},{24,0},{1,25},{9,17},{17,9},{25,1},{2,26},{10... | collective-permute-start | bytes 7864328 | tf_op jit(solution)/shard_map/ppermute | solution.py:121
  173.0 54.3 %collective-permute-start.4 = (f32[1,1280]{1,0:T(1,128)S(1)}, f32[1,1280]{1,0:T(1,128)S(1)}, u32[]{:S(2)}, u32[]{:S(2)}) collective-permute-start(f32[1,1280]{1,0:T(1,128)S(1)} %copy-done.12), channel_id=1, source_target_pairs={{0,24},{8,16},{16,8},{24,0},{1,25},{9,17},{17,9},{25,1},{2,26},{10... | collective-permute-start | bytes 15368 | tf_op jit(solution)/shard_map/ppermute | solution.py:121
  173.6 54.3 %collective-permute-start.3 = (f32[1,1280]{1,0:T(1,128)S(1)}, f32[1,1280]{1,0:T(1,128)S(1)}, u32[]{:S(2)}, u32[]{:S(2)}) collective-permute-start(f32[1,1280]{1,0:T(1,128)S(1)} %copy-done.12), channel_id=1, source_target_pairs={{0,8},{8,0},{16,24},{24,16},{1,9},{9,1},{17,25},{25,17},{2,10},{10... | collective-permute-start | bytes 15368 | tf_op jit(solution)/shard_map/ppermute | solution.py:118
  227.3 2.9 collective-permute-start.5
  262.6 36.9 %collective-permute-start.13 = (bf16[256,3456]{1,0:T(8,128)(2,1)}, bf16[256,3456]{1,0:T(8,128)(2,1)S(1)}, u32[]{:S(2)}, u32[]{:S(2)}) collective-permute-start(bf16[256,3456]{1,0:T(8,128)(2,1)} %get-tuple-element.22), channel_id=1, source_target_pairs={{0,24},{8,16},{16,8},{24,0},{1,25},{9,17},{17,9},{25,1},{2,26},{10... | collective-permute-start | bytes 5308424 | tf_op jit(solution)/shard_map/ppermute | solution.py:121
  299.5 34.6 %collective-permute-start.15 = (bf16[256,3456]{1,0:T(8,128)(2,1)S(1)}, bf16[256,3456]{1,0:T(8,128)(2,1)S(1)}, u32[]{:S(2)}, u32[]{:S(2)}) collective-permute-start(bf16[256,3456]{1,0:T(8,128)(2,1)S(1)} %collective-permute-done.13.refs_5_), channel_id=1, source_target_pairs={{0,8},{8,0},{16,24},{24,16},{1,9},{9,1},{17,25},{25,17},{2,10},{10... | collective-permute-start | bytes 5308424 | tf_op jit(solution)/shard_map/ppermute | solution.py:118
  335.3 53.6 %collective-permute-start.1 = (bf16[1024,1280]{1,0:T(8,128)(2,1)}, bf16[1024,1280]{1,0:T(8,128)(2,1)S(1)}, u32[]{:S(2)}, u32[]{:S(2)}) collective-permute-start(bf16[1024,1280]{1,0:T(8,128)(2,1)} %get-tuple-element.31.refs_0_), channel_id=1, source_target_pairs={{0,24},{8,16},{16,8},{24,0},{1,25},{9,17},{17,9},{25,1},{2,26},{10... | collective-permute-start | bytes 7864328 | tf_op jit(solution)/shard_map/ppermute | solution.py:121
  388.9 51.4 %collective-permute-start.2 = (bf16[1024,1280]{1,0:T(8,128)(2,1)S(1)}, bf16[1024,1280]{1,0:T(8,128)(2,1)S(1)}, u32[]{:S(2)}, u32[]{:S(2)}) collective-permute-start(bf16[1024,1280]{1,0:T(8,128)(2,1)S(1)} %collective-permute-done.1.refs_2_.refs_16_.refs_12_), channel_id=1, source_target_pairs={{0,8},{8,0},{16,24},{24,16},{1,9},{9,1},{17,25},{25,17},{2,10},{10... | collective-permute-start | bytes 7864328 | tf_op jit(solution)/shard_map/ppermute | solution.py:118
  420.8 54.2 %collective-permute-start.18 = (bf16[256,3456]{1,0:T(8,128)(2,1)}, bf16[256,3456]{1,0:T(8,128)(2,1)}, u32[]{:S(2)}, u32[]{:S(2)}) collective-permute-start(bf16[256,3456]{1,0:T(8,128)(2,1)} %get-tuple-element.26), channel_id=1, source_target_pairs={{0,24},{8,16},{16,8},{24,0},{1,25},{9,17},{17,9},{25,1},{2,26},{10... | collective-permute-start | bytes 5308424 | tf_op jit(solution)/shard_map/ppermute | solution.py:121
  420.9 72.4 %collective-permute-start.22 = (bf16[256,3456]{1,0:T(8,128)(2,1)}, bf16[256,3456]{1,0:T(8,128)(2,1)}, u32[]{:S(2)}, u32[]{:S(2)}) collective-permute-start(bf16[256,3456]{1,0:T(8,128)(2,1)} %get-tuple-element.28), channel_id=1, source_target_pairs={{0,24},{8,16},{16,8},{24,0},{1,25},{9,17},{17,9},{25,1},{2,26},{10... | collective-permute-start | bytes 5308424 | tf_op jit(solution)/shard_map/ppermute | solution.py:121
  473.5 51.8 %collective-permute-start.17 = (bf16[256,3456]{1,0:T(8,128)(2,1)}, bf16[256,3456]{1,0:T(8,128)(2,1)S(1)}, u32[]{:S(2)}, u32[]{:S(2)}) collective-permute-start(bf16[256,3456]{1,0:T(8,128)(2,1)} %get-tuple-element.25.refs_0_), channel_id=1, source_target_pairs={{0,8},{8,0},{16,24},{24,16},{1,9},{9,1},{17,25},{25,17},{2,10},{10... | collective-permute-start | bytes 5308424 | tf_op jit(solution)/shard_map/ppermute | solution.py:118
  473.9 68.7 %collective-permute-start.21 = (bf16[256,3456]{1,0:T(8,128)(2,1)}, bf16[256,3456]{1,0:T(8,128)(2,1)S(1)}, u32[]{:S(2)}, u32[]{:S(2)}) collective-permute-start(bf16[256,3456]{1,0:T(8,128)(2,1)} %get-tuple-element.27.refs_0_.refs_1_), channel_id=1, source_target_pairs={{0,8},{8,0},{16,24},{24,16},{1,9},{9,1},{17,25},{25,17},{2,10},{10... | collective-permute-start | bytes 5308424 | tf_op jit(solution)/shard_map/ppermute | solution.py:118
  475.0 68.7 %collective-permute-start.12 = (bf16[256,3456]{1,0:T(8,128)(2,1)}, bf16[256,3456]{1,0:T(8,128)(2,1)}, u32[]{:S(2)}, u32[]{:S(2)}) collective-permute-start(bf16[256,3456]{1,0:T(8,128)(2,1)} %get-tuple-element.21), channel_id=1, source_target_pairs={{0,24},{8,16},{16,8},{24,0},{1,25},{9,17},{17,9},{25,1},{2,26},{10... | collective-permute-start | bytes 5308424 | tf_op jit(solution)/shard_map/ppermute | solution.py:121
  475.0 105.6 %collective-permute-start.19 = (bf16[256,3456]{1,0:T(8,128)(2,1)}, bf16[256,3456]{1,0:T(8,128)(2,1)}, u32[]{:S(2)}, u32[]{:S(2)}) collective-permute-start(bf16[256,3456]{1,0:T(8,128)(2,1)} %collective-permute-done.18.refs_2_.refs_4_), channel_id=1, source_target_pairs={{0,8},{8,0},{16,24},{24,16},{1,9},{9,1},{17,25},{25,17},{2,10},{10... | collective-permute-start | bytes 5308424 | tf_op jit(solution)/shard_map/ppermute | solution.py:118
  493.3 125.2 %collective-permute-start.23 = (bf16[256,3456]{1,0:T(8,128)(2,1)}, bf16[256,3456]{1,0:T(8,128)(2,1)}, u32[]{:S(2)}, u32[]{:S(2)}) collective-permute-start(bf16[256,3456]{1,0:T(8,128)(2,1)} %collective-permute-done.22.refs_2_.refs_5_), channel_id=1, source_target_pairs={{0,8},{8,0},{16,24},{24,16},{1,9},{9,1},{17,25},{25,17},{2,10},{10... | collective-permute-start | bytes 5308424 | tf_op jit(solution)/shard_map/ppermute | solution.py:118
  525.3 93.3 %copy-start.2 = (bf16[256,3456]{1,0:T(8,128)(2,1)}, bf16[256,3456]{1,0:T(8,128)(2,1)S(1)}, u32[]{:S(2)}) copy-start(bf16[256,3456]{1,0:T(8,128)(2,1)S(1)} %collective-permute-done.17.refs_1_.refs_2_) | copy-start | bytes 5308420
  525.3 134.3 %collective-permute-start.6 = (bf16[256,3456]{1,0:T(8,128)(2,1)}, bf16[256,3456]{1,0:T(8,128)(2,1)}, u32[]{:S(2)}, u32[]{:S(2)}) collective-permute-start(bf16[256,3456]{1,0:T(8,128)(2,1)} %get-tuple-element.18.refs_0_), channel_id=1, source_target_pairs={{0,8},{8,0},{16,24},{24,16},{1,9},{9,1},{17,25},{25,17},{2,10},{10... | collective-permute-start | bytes 5308424 | tf_op jit(solution)/shard_map/ppermute | solution.py:118
  542.6 75.9 %copy-start.3 = (bf16[256,3456]{1,0:T(8,128)(2,1)}, bf16[256,3456]{1,0:T(8,128)(2,1)S(1)}, u32[]{:S(2)}) copy-start(bf16[256,3456]{1,0:T(8,128)(2,1)S(1)} %collective-permute-done.21.refs_1_.refs_3_) | copy-start | bytes 5308420
  542.6 151.8 %collective-permute-start.7 = (bf16[256,3456]{1,0:T(8,128)(2,1)}, bf16[256,3456]{1,0:T(8,128)(2,1)}, u32[]{:S(2)}, u32[]{:S(2)}) collective-permute-start(bf16[256,3456]{1,0:T(8,128)(2,1)} %get-tuple-element.19.refs_1_), channel_id=1, source_target_pairs={{0,8},{8,0},{16,24},{24,16},{1,9},{9,1},{17,25},{25,17},{2,10},{10... | collective-permute-start | bytes 5308424 | tf_op jit(solution)/shard_map/ppermute | solution.py:118
  543.7 188.6 %collective-permute-start.14 = (bf16[256,3456]{1,0:T(8,128)(2,1)}, bf16[256,3456]{1,0:T(8,128)(2,1)}, u32[]{:S(2)}, u32[]{:S(2)}) collective-permute-start(bf16[256,3456]{1,0:T(8,128)(2,1)} %collective-permute-done.12.refs_4_), channel_id=1, source_target_pairs={{0,8},{8,0},{16,24},{24,16},{1,9},{9,1},{17,25},{25,17},{2,10},{10... | collective-permute-start | bytes 5308424 | tf_op jit(solution)/shard_map/ppermute | solution.py:118
  659.3 151.1 %collective-permute-start.24 = (bf16[256,1280]{1,0:T(8,128)(2,1)}, bf16[256,1280]{1,0:T(8,128)(2,1)}, u32[]{:S(2)}, u32[]{:S(2)}) collective-permute-start(bf16[256,1280]{1,0:T(8,128)(2,1)} %shard_map.53), channel_id=1, source_target_pairs={{0,24},{8,16},{16,8},{24,0},{1,25},{9,17},{17,9},{25,1},{2,26},{10... | collective-permute-start | bytes 1966088 | tf_op jit(solution)/shard_map/ppermute | solution.py:121
  761.9 43.8 %collective-permute-start.16 = (bf16[512,1280]{1,0:T(8,128)(2,1)}, bf16[512,1280]{1,0:T(8,128)(2,1)S(1)}, u32[]{:S(2)}, u32[]{:S(2)}) collective-permute-start(bf16[512,1280]{1,0:T(8,128)(2,1)} %shard_map.49), channel_id=1, source_target_pairs={{0,24},{8,16},{16,8},{24,0},{1,25},{9,17},{17,9},{25,1},{2,26},{10... | collective-permute-start | bytes 3932168 | tf_op jit(solution)/shard_map/ppermute | solution.py:121
  781.8 27.6 %collective-permute-start.20 = (bf16[256,1280]{1,0:T(8,128)(2,1)}, bf16[256,1280]{1,0:T(8,128)(2,1)S(1)}, u32[]{:S(2)}, u32[]{:S(2)}) collective-permute-start(bf16[256,1280]{1,0:T(8,128)(2,1)} %shard_map.52), channel_id=1, source_target_pairs={{0,24},{8,16},{16,8},{24,0},{1,25},{9,17},{17,9},{25,1},{2,26},{10... | collective-permute-start | bytes 1966088 | tf_op jit(solution)/shard_map/ppermute | solution.py:121
  (11 other events, 171.5 us)
Sparse Core Ops, SparseCore 0:
  8.9 167.2 all-gather.4
  177.8 100.1 all-gather.8
  279.6 163.6 all-gather.6
  444.8 70.4 all-gather.10

commit v3 on v2

v3 whole, which is shorter than its diff:
```python
import jax
import jax.numpy as jnp
from jax import lax
from jax.experimental import pallas as pl
from jax.experimental.pallas import tpu as pltpu
from jax.sharding import PartitionSpec as P


LN_EPS = 1e-5
CHUNKS = 4
FIRST_COLS = 1024
NORM_ROWS = 128
VMEM_LIMIT = 58 * 1024 * 1024
UP_SPLIT, UP_TILE = 4, 512
DOWN_SPLIT, DOWN_TILE = 2, 256


def norm_kernel(meta, *refs):
    blocks, gammas, z_ref = refs[0:4], refs[4:8], refs[8]
    width = blocks[0].shape[1]
    d_model = z_ref.shape[1]
    sums, squares = 0.0, 0.0
    for b in blocks:
        v = b[...].astype(jnp.float32)
        sums += jnp.sum(v, axis=1, keepdims=True)
        squares += jnp.sum(v * v, axis=1, keepdims=True)
    mean = sums / d_model
    scale = lax.rsqrt(squares / d_model - mean * mean + LN_EPS)
    for j, (b, g) in enumerate(zip(blocks, gammas)):
        piece = (b[...].astype(jnp.float32) - mean) * scale * g[...]
        z_ref[:, pl.ds(pl.multiple_of(meta[j] * width, 128), width)] = piece.astype(jnp.bfloat16)


def norm(meta, blocks, gammas):
    rows, width = blocks[0].shape
    d_model = width * 4
    return pl.pallas_call(
        norm_kernel,
        grid_spec=pltpu.PrefetchScalarGridSpec(
            num_scalar_prefetch=1,
            grid=(rows // NORM_ROWS,),
            in_specs=[pl.BlockSpec((NORM_ROWS, width), lambda i, m: (i, 0))] * 4
            + [pl.BlockSpec((1, width), lambda i, m: (0, 0))] * 4,
            out_specs=pl.BlockSpec((NORM_ROWS, d_model), lambda i, m: (i, 0)),
        ),
        out_shape=jax.ShapeDtypeStruct((rows, d_model), jnp.bfloat16),
        compiler_params=pltpu.CompilerParams(vmem_limit_bytes=VMEM_LIMIT),
        cost_estimate=pl.CostEstimate(flops=64 * rows * d_model, bytes_accessed=4 * rows * d_model, transcendentals=rows),
    )(meta, *blocks, *gammas)


def up_kernel(z_ref, *refs):
    ws, h_refs = refs[:UP_SPLIT], refs[UP_SPLIT:]
    depth = ws[0].shape[0]
    pre = jnp.dot(z_ref[:, :depth], ws[0][...], preferred_element_type=jnp.float32)
    for s in range(1, UP_SPLIT):
        pre += jnp.dot(z_ref[:, s * depth:(s + 1) * depth], ws[s][...], preferred_element_type=jnp.float32)
    h = jax.nn.gelu(pre, approximate=True).astype(jnp.bfloat16)
    piece = h_refs[0].shape[0]
    for i, h_ref in enumerate(h_refs):
        h_ref[...] = h[i * piece:(i + 1) * piece]


def up(pair, step, z, w):
    d_model, hid = w.shape
    return pl.pallas_call(
        up_kernel,
        grid=(pl.cdiv(hid, UP_TILE),),
        in_specs=[pl.BlockSpec((2 * step, d_model), lambda n: (pair, 0))]
        + [pl.BlockSpec((d_model // UP_SPLIT, UP_TILE), lambda n, s=s: (s, n)) for s in range(UP_SPLIT)],
        out_specs=[pl.BlockSpec((step, UP_TILE), lambda n: (0, n))] * 2,
        out_shape=[jax.ShapeDtypeStruct((step, hid), jnp.bfloat16)] * 2,
        compiler_params=pltpu.CompilerParams(vmem_limit_bytes=VMEM_LIMIT),
        cost_estimate=pl.CostEstimate(flops=4 * step * d_model * hid, bytes_accessed=2 * d_model * hid, transcendentals=2 * step * hid),
    )(z, *[w] * UP_SPLIT)


def down_kernel(meta, *refs):
    n_w = 4 * DOWN_SPLIT
    x_ref, y_ref = refs[-2], refs[-1]
    pieces = y_ref.shape[0] // refs[0].shape[0]
    hs, ws = refs[:4 * pieces], refs[4 * pieces:-2]
    depth = ws[0].shape[0]

    def product(ws):
        branch = None
        for j in range(4):
            for s in range(DOWN_SPLIT):
                parts = [h[:, s * depth:(s + 1) * depth] for h in hs[j * pieces:(j + 1) * pieces]]
                lhs = parts[0] if pieces == 1 else jnp.concatenate(parts, axis=0)
                term = jnp.dot(lhs, ws[j * DOWN_SPLIT + s][...], preferred_element_type=jnp.float32)
                branch = term if branch is None else branch + term
        y_ref[...] = (x_ref[...].astype(jnp.float32) + branch).astype(jnp.bfloat16)

    if len(ws) == n_w:
        product(ws)
    else:
        first = pl.program_id(0) < FIRST_COLS // DOWN_TILE
        pl.when(first)(lambda: product(ws[:n_w]))
        pl.when(jnp.logical_not(first))(lambda: product(ws[n_w:]))


def down(meta, at, step, hs, ws, x, x_col):
    pieces = len(hs[0])
    hid = hs[0][0].shape[1]
    rows = step * pieces
    cols = sum(w.shape[1] for w in ws)
    w_specs, operands, start = [], [], 0
    for w in ws:
        tiles = w.shape[1] // DOWN_TILE
        for j in range(4):
            for s in range(DOWN_SPLIT):
                def index(n, m, j=j, s=s, start=start, tiles=tiles):
                    return (m[j] * DOWN_SPLIT + s, jnp.clip(n - start, 0, tiles - 1))

                w_specs.append(pl.BlockSpec((hid // DOWN_SPLIT, DOWN_TILE), index))
                operands.append(w)
        start += tiles
    return pl.pallas_call(
        down_kernel,
        grid_spec=pltpu.PrefetchScalarGridSpec(
            num_scalar_prefetch=1,
            grid=(cols // DOWN_TILE,),
            in_specs=[pl.BlockSpec((step, hid), lambda n, m: (0, 0))] * (4 * pieces)
            + w_specs
            + [pl.BlockSpec((rows, DOWN_TILE), lambda n, m: (at, x_col // DOWN_TILE + n))],
            out_specs=pl.BlockSpec((rows, DOWN_TILE), lambda n, m: (0, n)),
        ),
        out_shape=jax.ShapeDtypeStruct((rows, cols), jnp.bfloat16),
        compiler_params=pltpu.CompilerParams(vmem_limit_bytes=VMEM_LIMIT),
        cost_estimate=pl.CostEstimate(flops=8 * rows * hid * cols, bytes_accessed=8 * hid * cols, transcendentals=0),
    )(meta, *[h for owner in hs for h in owner], *operands, x)


def copy_kernel(in_ref, out_ref):
    out_ref[...] = in_ref[...]


def solution(mesh):
    n_col = mesh.shape["col"]
    tok_spec = P(("dp", "row"), "col")
    near_pairs = [(i, i ^ 1) for i in range(n_col)]
    far_pairs = [(i, n_col - 1 - i) for i in range(n_col)]

    def near(v):
        return lax.ppermute(v, "col", near_pairs)

    def far(v):
        return lax.ppermute(v, "col", far_pairs)

    def gather(v):
        return lax.all_gather(v, "row", axis=0, tiled=True)

    def local_block(x_loc, gamma_loc, w_in_loc, w_out_loc):
        rows, width = x_loc.shape
        half = rows // 2
        step = half // CHUNKS
        me = lax.axis_index("col")
        side = me // 2
        meta = jnp.stack([me, me ^ 1, n_col - 1 - me, me ^ 2]).astype(jnp.int32)

        w_in_panel = gather(w_in_loc)

        x_mine = lax.dynamic_slice(x_loc, (side * half, 0), (half, width))
        x_other = lax.dynamic_slice(x_loc, ((1 - side) * half, 0), (half, width))
        gamma_row = gamma_loc.reshape(1, width)
        g_near, g_far = near(gamma_row), far(gamma_row)
        g_opp = near(g_far)
        gammas = [gamma_row, g_near, g_far, g_opp]
        a1 = near(x_mine)
        b1 = far(x_other)
        w_out_far = far(w_out_loc)
        b2 = far(x_mine)
        a2 = near(b1)
        a3 = near(x_other)
        b3 = far(a1)

        marked = pl.pallas_call(copy_kernel, out_shape=jax.ShapeDtypeStruct(gamma_row.shape, gamma_row.dtype))(gamma_row)
        w_first, w_last = w_out_loc[:, :FIRST_COLS], w_out_loc[:, FIRST_COLS:]
        w_out_far, marked, w_first, w_last = lax.optimization_barrier((w_out_far, marked, w_first, w_last))
        other_gammas = [marked] + gammas[1:]

        far_panel = gather(w_out_far)
        own_first = gather(w_first)
        own_last = gather(w_last)

        h_mine, h_near, h_other, h_far = [], [], [], []
        z_mine = norm(meta, [x_mine, a1, b1, a2], gammas)
        z_other = norm(meta, [x_other, a3, b2, b3], other_gammas)
        for p in range(CHUNKS // 2):
            h_mine += up(p, step, z_mine, w_in_panel)
            h_near += [near(h_mine[c]) for c in (2 * p, 2 * p + 1)]
        for p in range(CHUNKS // 2):
            h_other += up(p, step, z_other, w_in_panel)
            h_far += [far(h_other[c]) for c in (2 * p, 2 * p + 1)]
        h_opp = [near(h) for h in h_far]

        def call(chunks, ws, x, x_col):
            hs = [[h[c] for c in chunks] for h in (h_mine, h_near, h_far, h_opp)]
            return down(meta, chunks[0] // len(chunks), step, hs, ws, x, x_col)

        y = jnp.zeros((rows, width), jnp.bfloat16)
        for chunks in ((0, 1), (2,), (3,)):
            part = far(call(chunks, [far_panel], b1, 0))
            y = lax.dynamic_update_slice(y, part, ((1 - side) * half + chunks[0] * step, 0))
        part = call((0, 1), [own_first], x_mine, 0)
        y = lax.dynamic_update_slice(y, part, (side * half, 0))
        part = call((0, 1), [own_last], x_mine, FIRST_COLS)
        y = lax.dynamic_update_slice(y, part, (side * half, FIRST_COLS))
        part = call((2, 3), [own_first, own_last], x_mine, 0)
        y = lax.dynamic_update_slice(y, part, (side * half + 2 * step, 0))
        return y

    return jax.shard_map(local_block, mesh=mesh, in_specs=(tok_spec, P("col"), P("row", "col"), P("row", "col")), out_specs=tok_spec, check_vma=False)
```

time: 872 us -> 845 us (0.969)
  waiting for transfers between devices: 520 us -> 501 us
  local copies, waits for them, and re-layouts: 27.4 us -> 18.2 us
    ppermute x13, waiting for transfers between devices: 267 us -> 251 us  [near(): return lax.ppermute(v, 'col', near_pairs)]
    pallas_call x4 -> x6, Pallas kernels: 127 us -> 136 us  [the longest x4 108 us: up(): pl.pallas_call(up_kernel, grid=(pl.cdiv(hid, UP_TILE),), in_specs=[pl.Blo...]
    pallas_call x7 -> x6, Pallas kernels: 147 us -> 140 us  [down(): pl.pallas_call(down_kernel, grid_spec=pltpu.PrefetchScalarGridSpec(num_sc...]
  transfers between devices with their start and end apart: 29 -> 29, of which waited for: 14 -> 14; matrix products, arithmetic and copies ran while one was open for 2% -> 2% of each run, Pallas kernels for 28% -> 30%
where the time goes in v3:
time: 845 us; the launch traced here: 838 us
  waiting for transfers between devices  501 us (59%)
  Pallas kernels  278 us (33%)
  starting transfers between devices  26.9 us (3%)
  local copies, waits for them, and re-layouts  18.2 us (2%)
  between operations  13.4 us (2%)
    ppermute x13, waiting for transfers between devices, near(): return lax.ppermute(v, 'col', near_pairs)  251 us
    ppermute x12, waiting for transfers between devices, far(): return lax.ppermute(v, 'col', far_pairs)  248 us
    pallas_call x6, Pallas kernels, down(): pl.pallas_call(down_kernel, grid_spec=pltpu.PrefetchScalarGridSpec(num_sc...  140 us
    pallas_call x4, Pallas kernels, up(): pl.pallas_call(up_kernel, grid=(pl.cdiv(hid, UP_TILE),), in_specs=[pl.Blo...  108 us
    pallas_call x2, Pallas kernels, norm(): pl.pallas_call(norm_kernel, grid_spec=pltpu.PrefetchScalarGridSpec(num_sc...  28.1 us
    ppermute x12, starting transfers between devices, far(): return lax.ppermute(v, 'col', far_pairs)  20.8 us
  transfers between devices with their start and end apart: 29, of which 14 were waited for; matrix products, arithmetic and copies ran while one was open for 2% of the time, Pallas kernels for 30%

profile of v3, /device:TPU:97, one launch (start us, length us, event | category | flops | bytes accessed | tf_op | source)
XLA Modules:
  0.0 838.3 jit_solution(10397425221524762161)
XLA Ops:
  7.4 5.3 collective-permute-start.11
  12.7 4.2 slice.6
  16.8 2.2 slice.7
  20.9 87.4 %collective-permute-done.11 = bf16[1728,1280]{1,0:T(8,128)(2,1)} collective-permute-done((bf16[1728,1280]{1,0:T(8,128)(2,1)}, bf16[1728,1280]{1,0:T(8,128)(2,1)}, u32[]{:S(2)}, u32[]{:S(2)}) %collective-permute-start.11) | collective-permute-done | bytes 4423712 | tf_op jit(solution)/shard_map/ppermute | solution.py:149
  109.8 4.4 constant_dynamic-slice_fusion
  114.2 2.4 collective-permute-start.1
  118.1 53.5 %collective-permute-done.refs_1_ = bf16[1024,1280]{1,0:T(8,128)(2,1)} collective-permute-done((bf16[1024,1280]{1,0:T(8,128)(2,1)S(1)}, bf16[1024,1280]{1,0:T(8,128)(2,1)}, u32[]{:S(2)}, u32[]{:S(2)}) %collective-permute-start) | collective-permute-done | bytes 2621472 | tf_op jit(solution)/shard_map/ppermute | solution.py:146
  174.3 111.2 %collective-permute-done.4.refs_6_ = f32[1,1280]{1,0:T(1,128)S(1)} collective-permute-done((f32[1,1280]{1,0:T(1,128)S(1)}, f32[1,1280]{1,0:T(1,128)S(1)}, u32[]{:S(2)}, u32[]{:S(2)}) %collective-permute-start.4) | collective-permute-done | bytes 5152 | tf_op jit(solution)/shard_map/ppermute | solution.py:149
  285.8 2.6 collective-permute-done.3.refs_5_
  291.8 13.8 %shard_map.49.z_ref = bf16[1024,5120]{1,0:T(8,128)(2,1)} custom-call(s32[4]{0:T(128)} %pad_add_fusion.meta, bf16[1024,1280]{1,0:T(8,128)(2,1)} %get-tuple-element.29.refs_0_, bf16[1024,1280]{1,0:T(8,128)(2,1)} %collective-permute-done.8.refs_1_, bf16[1024,1280]{1,0:T(8,128)(2,1)} %collective-permute-done.9.refs_2_, ...), custom_call_target="tpu_custom_call" | custom-call | flops 335544320 | bytes 20971520 | tf_op jit(solution)/shard_map/pallas_call | solution.py:37
  305.6 26.9 %shard_map.53 = (bf16[256,3456]{1,0:T(8,128)(2,1)}, bf16[256,3456]{1,0:T(8,128)(2,1)}) custom-call(bf16[1024,5120]{1,0:T(8,128)(2,1)} %shard_map.49.z_ref, bf16[5120,3456]{1,0:T(8,128)(2,1)} %all-gather.5.cloned.1.call-done.refs_0_.refs_1_.refs_2_.refs_3_, bf16[5120,3456]{1,0:T(8,128)(2,1)} %all-gather.5.cloned.1.call-done.refs_0_.refs_1_.refs_2_.refs_3_, ...), custom_call_target="tpu_custom_call" | custom-call | flops 18119393280 | bytes 35389440 | tf_op jit(solution)/shard_map/pallas_call | solution.py:66
  332.5 2.1 collective-permute-start.18
  334.6 26.9 %shard_map.50 = (bf16[256,3456]{1,0:T(8,128)(2,1)}, bf16[256,3456]{1,0:T(8,128)(2,1)}) custom-call(bf16[1024,5120]{1,0:T(8,128)(2,1)} %shard_map.49.z_ref, bf16[5120,3456]{1,0:T(8,128)(2,1)} %all-gather.5.cloned.1.call-done.refs_0_.refs_1_.refs_2_.refs_3_, bf16[5120,3456]{1,0:T(8,128)(2,1)} %all-gather.5.cloned.1.call-done.refs_0_.refs_1_.refs_2_.refs_3_, ...), custom_call_target="tpu_custom_call" | custom-call | flops 18119393280 | bytes 35389440 | tf_op jit(solution)/shard_map/pallas_call | solution.py:66
  362.1 2.2 collective-permute-start.13
  364.2 14.3 %shard_map.46.z_ref = bf16[1024,5120]{1,0:T(8,128)(2,1)} custom-call(s32[4]{0:T(128)} %pad_add_fusion.meta, bf16[1024,1280]{1,0:T(8,128)(2,1)} %copy-done, bf16[1024,1280]{1,0:T(8,128)(2,1)} %collective-permute-done.refs_1_, bf16[1024,1280]{1,0:T(8,128)(2,1)} %collective-permute-done.1.refs_2_.refs_16_.refs_12_, ...), custom_call_target="tpu_custom_call" | custom-call | flops 335544320 | bytes 20971520 | tf_op jit(solution)/shard_map/pallas_call | solution.py:37
  379.2 26.7 %shard_map.47 = (bf16[256,3456]{1,0:T(8,128)(2,1)}, bf16[256,3456]{1,0:T(8,128)(2,1)}) custom-call(bf16[1024,5120]{1,0:T(8,128)(2,1)} %shard_map.46.z_ref, bf16[5120,3456]{1,0:T(8,128)(2,1)} %all-gather.5.cloned.1.call-done.refs_0_.refs_1_.refs_2_.refs_3_, bf16[5120,3456]{1,0:T(8,128)(2,1)} %all-gather.5.cloned.1.call-done.refs_0_.refs_1_.refs_2_.refs_3_, ...), custom_call_target="tpu_custom_call" | custom-call | flops 18119393280 | bytes 35389440 | tf_op jit(solution)/shard_map/pallas_call | solution.py:66
  408.7 37.9 %collective-permute-done.13.refs_5_ = bf16[256,3456]{1,0:T(8,128)(2,1)S(1)} collective-permute-done((bf16[256,3456]{1,0:T(8,128)(2,1)}, bf16[256,3456]{1,0:T(8,128)(2,1)S(1)}, u32[]{:S(2)}, u32[]{:S(2)}) %collective-permute-start.13) | collective-permute-done | bytes 1769504 | tf_op jit(solution)/shard_map/ppermute | solution.py:149
  446.6 27.4 %shard_map.52 = (bf16[256,3456]{1,0:T(8,128)(2,1)}, bf16[256,3456]{1,0:T(8,128)(2,1)}) custom-call(bf16[1024,5120]{1,0:T(8,128)(2,1)} %shard_map.46.z_ref, bf16[5120,3456]{1,0:T(8,128)(2,1)} %all-gather.5.cloned.1.call-done.refs_0_.refs_1_.refs_2_.refs_3_, bf16[5120,3456]{1,0:T(8,128)(2,1)} %all-gather.5.cloned.1.call-done.refs_0_.refs_1_.refs_2_.refs_3_, ...), custom_call_target="tpu_custom_call" | custom-call | flops 18119393280 | bytes 35389440 | tf_op jit(solution)/shard_map/pallas_call | solution.py:66
  474.0 10.5 %collective-permute-done.22.refs_2_.refs_5_ = bf16[256,3456]{1,0:T(8,128)(2,1)} collective-permute-done((bf16[256,3456]{1,0:T(8,128)(2,1)}, bf16[256,3456]{1,0:T(8,128)(2,1)}, u32[]{:S(2)}, u32[]{:S(2)}) %collective-permute-start.22) | collective-permute-done | bytes 1769504 | tf_op jit(solution)/shard_map/ppermute | solution.py:149
  486.1 31.4 %collective-permute-done.14.refs_6_ = bf16[256,3456]{1,0:T(8,128)(2,1)} collective-permute-done((bf16[256,3456]{1,0:T(8,128)(2,1)S(1)}, bf16[256,3456]{1,0:T(8,128)(2,1)}, u32[]{:S(2)}, u32[]{:S(2)}) %collective-permute-start.14) | collective-permute-done | bytes 1769504 | tf_op jit(solution)/shard_map/ppermute | solution.py:146
  517.8 37.6 %collective-permute-done.15.refs_7_ = bf16[256,3456]{1,0:T(8,128)(2,1)} collective-permute-done((bf16[256,3456]{1,0:T(8,128)(2,1)S(1)}, bf16[256,3456]{1,0:T(8,128)(2,1)}, u32[]{:S(2)}, u32[]{:S(2)}) %collective-permute-start.15) | collective-permute-done | bytes 1769504 | tf_op jit(solution)/shard_map/ppermute | solution.py:146
  555.4 26.6 %shard_map.56 = bf16[512,1024]{1,0:T(8,128)(2,1)} custom-call(s32[4]{0:T(128)} %pad_add_fusion.meta, bf16[256,3456]{1,0:T(8,128)(2,1)} %get-tuple-element.17.refs_0_, bf16[256,3456]{1,0:T(8,128)(2,1)} %get-tuple-element.18.refs_1_, bf16[256,3456]{1,0:T(8,128)(2,1)} %copy-done.3, bf16[256,3456]{1,0:T(8,128)(2,1)} %collective-permute-done.7.refs_3_, ...), custom_call_target="tpu_custom_call" | custom-call | flops 14495514624 | bytes 28311552 | tf_op jit(solution)/shard_map/pallas_call | solution.py:119
  582.1 11.3 %collective-permute-done.17.refs_1_.refs_2_ = bf16[256,3456]{1,0:T(8,128)(2,1)} collective-permute-done((bf16[256,3456]{1,0:T(8,128)(2,1)}, bf16[256,3456]{1,0:T(8,128)(2,1)}, u32[]{:S(2)}, u32[]{:S(2)}) %collective-permute-start.17) | collective-permute-done | bytes 1769504 | tf_op jit(solution)/shard_map/ppermute | solution.py:146
  593.4 37.9 %collective-permute-done.21.refs_1_.refs_3_ = bf16[256,3456]{1,0:T(8,128)(2,1)} collective-permute-done((bf16[256,3456]{1,0:T(8,128)(2,1)}, bf16[256,3456]{1,0:T(8,128)(2,1)}, u32[]{:S(2)}, u32[]{:S(2)}) %collective-permute-start.21) | collective-permute-done | bytes 1769504 | tf_op jit(solution)/shard_map/ppermute | solution.py:146
  631.3 37.9 %collective-permute-done.19.refs_3_.refs_6_ = bf16[256,3456]{1,0:T(8,128)(2,1)} collective-permute-done((bf16[256,3456]{1,0:T(8,128)(2,1)}, bf16[256,3456]{1,0:T(8,128)(2,1)}, u32[]{:S(2)}, u32[]{:S(2)}) %collective-permute-start.19) | collective-permute-done | bytes 1769504 | tf_op jit(solution)/shard_map/ppermute | solution.py:146
  669.2 37.9 %collective-permute-done.23.refs_3_.refs_7_ = bf16[256,3456]{1,0:T(8,128)(2,1)} collective-permute-done((bf16[256,3456]{1,0:T(8,128)(2,1)}, bf16[256,3456]{1,0:T(8,128)(2,1)}, u32[]{:S(2)}, u32[]{:S(2)}) %collective-permute-start.23) | collective-permute-done | bytes 1769504 | tf_op jit(solution)/shard_map/ppermute | solution.py:146
  707.1 32.3 %shard_map.58 = bf16[512,1280]{1,0:T(8,128)(2,1)} custom-call(s32[4]{0:T(128)} %pad_add_fusion.meta, bf16[256,3456]{1,0:T(8,128)(2,1)} %get-tuple-element.23.refs_0_, bf16[256,3456]{1,0:T(8,128)(2,1)} %get-tuple-element.25.refs_0_.refs_1_, bf16[256,3456]{1,0:T(8,128)(2,1)} %collective-permute-done.17.refs_1_.refs_2_, ...), custom_call_target="tpu_custom_call" | custom-call | flops 18119393280 | bytes 35389440 | tf_op jit(solution)/shard_map/pallas_call | solution.py:119
  739.5 29.8 %shard_map.51 = bf16[512,1280]{1,0:T(8,128)(2,1)} custom-call(s32[4]{0:T(128)} %pad_add_fusion.meta, bf16[256,3456]{1,0:T(8,128)(2,1)} %get-tuple-element.17.refs_0_, bf16[256,3456]{1,0:T(8,128)(2,1)} %get-tuple-element.18.refs_1_, bf16[256,3456]{1,0:T(8,128)(2,1)} %copy-done.3, bf16[256,3456]{1,0:T(8,128)(2,1)} %collective-permute-done.7.refs_3_, ...), custom_call_target="tpu_custom_call" | custom-call | flops 18119393280 | bytes 35389440 | tf_op jit(solution)/shard_map/pallas_call | solution.py:119
  770.9 19.6 %shard_map.54 = bf16[256,1280]{1,0:T(8,128)(2,1)} custom-call(s32[4]{0:T(128)} %pad_add_fusion.meta, bf16[256,3456]{1,0:T(8,128)(2,1)} %get-tuple-element.23.refs_0_, bf16[256,3456]{1,0:T(8,128)(2,1)} %collective-permute-done.17.refs_1_.refs_2_, bf16[256,3456]{1,0:T(8,128)(2,1)} %collective-permute-done.18.refs_2_.refs_4_, ...), custom_call_target="tpu_custom_call" | custom-call | flops 9059696640 | bytes 35389440 | tf_op jit(solution)/shard_map/pallas_call | solution.py:119
  791.6 19.5 %shard_map.55 = bf16[256,1280]{1,0:T(8,128)(2,1)} custom-call(s32[4]{0:T(128)} %pad_add_fusion.meta, bf16[256,3456]{1,0:T(8,128)(2,1)} %get-tuple-element.25.refs_0_.refs_1_, bf16[256,3456]{1,0:T(8,128)(2,1)} %collective-permute-done.21.refs_1_.refs_3_, bf16[256,3456]{1,0:T(8,128)(2,1)} %collective-permute-done.22.refs_2_.refs_5_, ...), custom_call_target="tpu_custom_call" | custom-call | flops 9059696640 | bytes 35389440 | tf_op jit(solution)/shard_map/pallas_call | solution.py:119
  812.7 12.6 %shard_map.57 = bf16[512,256]{1,0:T(8,128)(2,1)} custom-call(s32[4]{0:T(128)} %pad_add_fusion.meta, bf16[256,3456]{1,0:T(8,128)(2,1)} %get-tuple-element.17.refs_0_, bf16[256,3456]{1,0:T(8,128)(2,1)} %get-tuple-element.18.refs_1_, bf16[256,3456]{1,0:T(8,128)(2,1)} %copy-done.3, bf16[256,3456]{1,0:T(8,128)(2,1)} %collective-permute-done.7.refs_3_, ...), custom_call_target="tpu_custom_call" | custom-call | flops 3623878656 | bytes 7077888 | tf_op jit(solution)/shard_map/pallas_call | solution.py:119
  828.3 2.3 copy-done.4
  (81 shorter events, 26.2 us)
Async XLA Ops:
  6.5 299.1 %all-gather.5.cloned.1.call-start = ((), (), s32[]{:S(2)}) async-start(), calls=%async_computation | async-start | bytes 39813120 | tf_op jit(solution)/shard_map/all_gather | solution.py:152
  7.3 510.5 %all-gather.9.cloned.1.call-start = ((), (), s32[]{:S(2)}) async-start(), calls=%async_computation.2 | async-start | bytes 31850496 | tf_op jit(solution)/shard_map/all_gather | solution.py:152
  7.4 100.9 %collective-permute-start.11 = (bf16[1728,1280]{1,0:T(8,128)(2,1)}, bf16[1728,1280]{1,0:T(8,128)(2,1)}, u32[]{:S(2)}, u32[]{:S(2)}) collective-permute-start(bf16[1728,1280]{1,0:T(8,128)(2,1)} %param.7), channel_id=1, source_target_pairs={{0,24},{8,16},{16,8},{24,0},{1,25},{9,17},{17,9},{25,1},{2,26},{10... | collective-permute-start | bytes 13271048 | tf_op jit(solution)/shard_map/ppermute | solution.py:149
  108.3 473.8 %all-gather.11.cloned.1.call-start = ((), (), s32[]{:S(2)}) async-start(), calls=%async_computation.3 | async-start | bytes 7962624 | tf_op jit(solution)/shard_map/all_gather | solution.py:152
  109.1 630.3 %all-gather.7.cloned.1.call-start = ((), (), s32[]{:S(2)}) async-start(), calls=%async_computation.1 | async-start | bytes 39813120 | tf_op jit(solution)/shard_map/all_gather | solution.py:152
  109.8 63.9 %copy-start.8 = (f32[1,1280]{1,0:T(1,128)S(1)}, f32[1,1280]{1,0:T(1,128)}, u32[]{:S(2)}) copy-start(f32[1,1280]{1,0:T(1,128)} %reshape.3.refs_4_.in_ref) | copy-start | bytes 15364
  114.2 191.4 %copy-start = (bf16[1024,1280]{1,0:T(8,128)(2,1)}, bf16[1024,1280]{1,0:T(8,128)(2,1)S(1)}, u32[]{:S(2)}) copy-start(bf16[1024,1280]{1,0:T(8,128)(2,1)S(1)} %get-tuple-element.30.refs_0_.refs_16_.refs_24_) | copy-start | bytes 7864324
  114.2 57.3 %collective-permute-start = (bf16[1024,1280]{1,0:T(8,128)(2,1)S(1)}, bf16[1024,1280]{1,0:T(8,128)(2,1)}, u32[]{:S(2)}, u32[]{:S(2)}) collective-permute-start(bf16[1024,1280]{1,0:T(8,128)(2,1)S(1)} %get-tuple-element.30.refs_0_.refs_16_.refs_24_), channel_id=1, source_target_pairs={{0,8},{8,0},{16,24},{24,16},{1,9},{9,1},{17,25},{25,17},{2,10},{10... | collective-permute-start | bytes 7864328 | tf_op jit(solution)/shard_map/ppermute | solution.py:146
  114.2 175.0 %collective-permute-start.1 = (bf16[1024,1280]{1,0:T(8,128)(2,1)}, bf16[1024,1280]{1,0:T(8,128)(2,1)}, u32[]{:S(2)}, u32[]{:S(2)}) collective-permute-start(bf16[1024,1280]{1,0:T(8,128)(2,1)} %get-tuple-element.29.refs_0_), channel_id=1, source_target_pairs={{0,24},{8,16},{16,8},{24,0},{1,25},{9,17},{17,9},{25,1},{2,26},{10... | collective-permute-start | bytes 7864328 | tf_op jit(solution)/shard_map/ppermute | solution.py:149
  116.6 174.6 %collective-permute-start.8 = (bf16[1024,1280]{1,0:T(8,128)(2,1)}, bf16[1024,1280]{1,0:T(8,128)(2,1)}, u32[]{:S(2)}, u32[]{:S(2)}) collective-permute-start(bf16[1024,1280]{1,0:T(8,128)(2,1)} %get-tuple-element.29.refs_0_), channel_id=1, source_target_pairs={{0,8},{8,0},{16,24},{24,16},{1,9},{9,1},{17,25},{25,17},{2,10},{10... | collective-permute-start | bytes 7864328 | tf_op jit(solution)/shard_map/ppermute | solution.py:146
  117.5 173.7 %collective-permute-start.9 = (bf16[1024,1280]{1,0:T(8,128)(2,1)S(1)}, bf16[1024,1280]{1,0:T(8,128)(2,1)}, u32[]{:S(2)}, u32[]{:S(2)}) collective-permute-start(bf16[1024,1280]{1,0:T(8,128)(2,1)S(1)} %get-tuple-element.30.refs_0_.refs_16_.refs_24_), channel_id=1, source_target_pairs={{0,24},{8,16},{16,8},{24,0},{1,25},{9,17},{17,9},{25,1},{2,26},{10... | collective-permute-start | bytes 7864328 | tf_op jit(solution)/shard_map/ppermute | solution.py:149
  171.6 119.6 %collective-permute-start.10 = (bf16[1024,1280]{1,0:T(8,128)(2,1)}, bf16[1024,1280]{1,0:T(8,128)(2,1)}, u32[]{:S(2)}, u32[]{:S(2)}) collective-permute-start(bf16[1024,1280]{1,0:T(8,128)(2,1)} %collective-permute-done.refs_1_), channel_id=1, source_target_pairs={{0,24},{8,16},{16,8},{24,0},{1,25},{9,17},{17,9},{25,1},{2,26},{10... | collective-permute-start | bytes 7864328 | tf_op jit(solution)/shard_map/ppermute | solution.py:149
  173.7 111.8 %collective-permute-start.4 = (f32[1,1280]{1,0:T(1,128)S(1)}, f32[1,1280]{1,0:T(1,128)S(1)}, u32[]{:S(2)}, u32[]{:S(2)}) collective-permute-start(f32[1,1280]{1,0:T(1,128)S(1)} %copy-done.8), channel_id=1, source_target_pairs={{0,24},{8,16},{16,8},{24,0},{1,25},{9,17},{17,9},{25,1},{2,26},{10... | collective-permute-start | bytes 15368 | tf_op jit(solution)/shard_map/ppermute | solution.py:149
  285.5 2.9 collective-permute-start.3
  288.3 2.9 collective-permute-start.5
  289.2 75.0 %collective-permute-start.2 = (bf16[1024,1280]{1,0:T(8,128)(2,1)}, bf16[1024,1280]{1,0:T(8,128)(2,1)}, u32[]{:S(2)}, u32[]{:S(2)}) collective-permute-start(bf16[1024,1280]{1,0:T(8,128)(2,1)} %collective-permute-done.1.refs_2_.refs_16_.refs_12_), channel_id=1, source_target_pairs={{0,8},{8,0},{16,24},{24,16},{1,9},{9,1},{17,25},{25,17},{2,10},{10... | collective-permute-start | bytes 7864328 | tf_op jit(solution)/shard_map/ppermute | solution.py:146
  332.5 73.5 %collective-permute-start.18 = (bf16[256,3456]{1,0:T(8,128)(2,1)}, bf16[256,3456]{1,0:T(8,128)(2,1)}, u32[]{:S(2)}, u32[]{:S(2)}) collective-permute-start(bf16[256,3456]{1,0:T(8,128)(2,1)} %get-tuple-element.24), channel_id=1, source_target_pairs={{0,24},{8,16},{16,8},{24,0},{1,25},{9,17},{17,9},{25,1},{2,26},{10... | collective-permute-start | bytes 5308424 | tf_op jit(solution)/shard_map/ppermute | solution.py:149
  361.5 47.2 %collective-permute-start.12 = (bf16[256,3456]{1,0:T(8,128)(2,1)}, bf16[256,3456]{1,0:T(8,128)(2,1)S(1)}, u32[]{:S(2)}, u32[]{:S(2)}) collective-permute-start(bf16[256,3456]{1,0:T(8,128)(2,1)} %get-tuple-element.20), channel_id=1, source_target_pairs={{0,24},{8,16},{16,8},{24,0},{1,25},{9,17},{17,9},{25,1},{2,26},{10... | collective-permute-start | bytes 5308424 | tf_op jit(solution)/shard_map/ppermute | solution.py:149
  362.1 84.6 %collective-permute-start.13 = (bf16[256,3456]{1,0:T(8,128)(2,1)}, bf16[256,3456]{1,0:T(8,128)(2,1)S(1)}, u32[]{:S(2)}, u32[]{:S(2)}) collective-permute-start(bf16[256,3456]{1,0:T(8,128)(2,1)} %get-tuple-element.21), channel_id=1, source_target_pairs={{0,24},{8,16},{16,8},{24,0},{1,25},{9,17},{17,9},{25,1},{2,26},{10... | collective-permute-start | bytes 5308424 | tf_op jit(solution)/shard_map/ppermute | solution.py:149
  378.5 106.0 %collective-permute-start.22 = (bf16[256,3456]{1,0:T(8,128)(2,1)}, bf16[256,3456]{1,0:T(8,128)(2,1)}, u32[]{:S(2)}, u32[]{:S(2)}) collective-permute-start(bf16[256,3456]{1,0:T(8,128)(2,1)} %get-tuple-element.26), channel_id=1, source_target_pairs={{0,24},{8,16},{16,8},{24,0},{1,25},{9,17},{17,9},{25,1},{2,26},{10... | collective-permute-start | bytes 5308424 | tf_op jit(solution)/shard_map/ppermute | solution.py:149
  405.9 78.6 %collective-permute-start.6 = (bf16[256,3456]{1,0:T(8,128)(2,1)}, bf16[256,3456]{1,0:T(8,128)(2,1)S(1)}, u32[]{:S(2)}, u32[]{:S(2)}) collective-permute-start(bf16[256,3456]{1,0:T(8,128)(2,1)} %get-tuple-element.17.refs_0_), channel_id=1, source_target_pairs={{0,8},{8,0},{16,24},{24,16},{1,9},{9,1},{17,25},{25,17},{2,10},{10... | collective-permute-start | bytes 5308424 | tf_op jit(solution)/shard_map/ppermute | solution.py:146
  406.0 80.1 %collective-permute-start.7 = (bf16[256,3456]{1,0:T(8,128)(2,1)}, bf16[256,3456]{1,0:T(8,128)(2,1)}, u32[]{:S(2)}, u32[]{:S(2)}) collective-permute-start(bf16[256,3456]{1,0:T(8,128)(2,1)} %get-tuple-element.18.refs_1_), channel_id=1, source_target_pairs={{0,8},{8,0},{16,24},{24,16},{1,9},{9,1},{17,25},{25,17},{2,10},{10... | collective-permute-start | bytes 5308424 | tf_op jit(solution)/shard_map/ppermute | solution.py:146
  408.7 65.3 %copy-start.1 = (bf16[256,3456]{1,0:T(8,128)(2,1)}, bf16[256,3456]{1,0:T(8,128)(2,1)S(1)}, u32[]{:S(2)}) copy-start(bf16[256,3456]{1,0:T(8,128)(2,1)S(1)} %collective-permute-done.12.refs_4_) | copy-start | bytes 5308420
  408.7 108.8 %collective-permute-start.14 = (bf16[256,3456]{1,0:T(8,128)(2,1)S(1)}, bf16[256,3456]{1,0:T(8,128)(2,1)}, u32[]{:S(2)}, u32[]{:S(2)}) collective-permute-start(bf16[256,3456]{1,0:T(8,128)(2,1)S(1)} %collective-permute-done.12.refs_4_), channel_id=1, source_target_pairs={{0,8},{8,0},{16,24},{24,16},{1,9},{9,1},{17,25},{25,17},{2,10},{10... | collective-permute-start | bytes 5308424 | tf_op jit(solution)/shard_map/ppermute | solution.py:146
  446.6 108.8 %collective-permute-start.15 = (bf16[256,3456]{1,0:T(8,128)(2,1)S(1)}, bf16[256,3456]{1,0:T(8,128)(2,1)}, u32[]{:S(2)}, u32[]{:S(2)}) collective-permute-start(bf16[256,3456]{1,0:T(8,128)(2,1)S(1)} %collective-permute-done.13.refs_5_), channel_id=1, source_target_pairs={{0,8},{8,0},{16,24},{24,16},{1,9},{9,1},{17,25},{25,17},{2,10},{10... | collective-permute-start | bytes 5308424 | tf_op jit(solution)/shard_map/ppermute | solution.py:146
  484.5 108.8 %collective-permute-start.17 = (bf16[256,3456]{1,0:T(8,128)(2,1)}, bf16[256,3456]{1,0:T(8,128)(2,1)}, u32[]{:S(2)}, u32[]{:S(2)}) collective-permute-start(bf16[256,3456]{1,0:T(8,128)(2,1)} %get-tuple-element.23.refs_0_), channel_id=1, source_target_pairs={{0,8},{8,0},{16,24},{24,16},{1,9},{9,1},{17,25},{25,17},{2,10},{10... | collective-permute-start | bytes 5308424 | tf_op jit(solution)/shard_map/ppermute | solution.py:146
  484.6 146.7 %collective-permute-start.21 = (bf16[256,3456]{1,0:T(8,128)(2,1)}, bf16[256,3456]{1,0:T(8,128)(2,1)}, u32[]{:S(2)}, u32[]{:S(2)}) collective-permute-start(bf16[256,3456]{1,0:T(8,128)(2,1)} %get-tuple-element.25.refs_0_.refs_1_), channel_id=1, source_target_pairs={{0,8},{8,0},{16,24},{24,16},{1,9},{9,1},{17,25},{25,17},{2,10},{10... | collective-permute-start | bytes 5308424 | tf_op jit(solution)/shard_map/ppermute | solution.py:146
  486.0 183.2 %collective-permute-start.19 = (bf16[256,3456]{1,0:T(8,128)(2,1)}, bf16[256,3456]{1,0:T(8,128)(2,1)}, u32[]{:S(2)}, u32[]{:S(2)}) collective-permute-start(bf16[256,3456]{1,0:T(8,128)(2,1)} %collective-permute-done.18.refs_2_.refs_4_), channel_id=1, source_target_pairs={{0,8},{8,0},{16,24},{24,16},{1,9},{9,1},{17,25},{25,17},{2,10},{10... | collective-permute-start | bytes 5308424 | tf_op jit(solution)/shard_map/ppermute | solution.py:146
  517.5 189.6 %collective-permute-start.23 = (bf16[256,3456]{1,0:T(8,128)(2,1)}, bf16[256,3456]{1,0:T(8,128)(2,1)}, u32[]{:S(2)}, u32[]{:S(2)}) collective-permute-start(bf16[256,3456]{1,0:T(8,128)(2,1)} %collective-permute-done.22.refs_2_.refs_5_), channel_id=1, source_target_pairs={{0,8},{8,0},{16,24},{24,16},{1,9},{9,1},{17,25},{25,17},{2,10},{10... | collective-permute-start | bytes 5308424 | tf_op jit(solution)/shard_map/ppermute | solution.py:146
  769.3 56.1 %collective-permute-start.16 = (bf16[512,1280]{1,0:T(8,128)(2,1)}, bf16[512,1280]{1,0:T(8,128)(2,1)}, u32[]{:S(2)}, u32[]{:S(2)}) collective-permute-start(bf16[512,1280]{1,0:T(8,128)(2,1)} %shard_map.51), channel_id=1, source_target_pairs={{0,24},{8,16},{16,8},{24,0},{1,25},{9,17},{17,9},{25,1},{2,26},{10... | collective-permute-start | bytes 3932168 | tf_op jit(solution)/shard_map/ppermute | solution.py:149
  790.5 36.8 %collective-permute-start.20 = (bf16[256,1280]{1,0:T(8,128)(2,1)}, bf16[256,1280]{1,0:T(8,128)(2,1)S(1)}, u32[]{:S(2)}, u32[]{:S(2)}) collective-permute-start(bf16[256,1280]{1,0:T(8,128)(2,1)} %shard_map.54), channel_id=1, source_target_pairs={{0,24},{8,16},{16,8},{24,0},{1,25},{9,17},{17,9},{25,1},{2,26},{10... | collective-permute-start | bytes 1966088 | tf_op jit(solution)/shard_map/ppermute | solution.py:149
  811.2 16.2 %collective-permute-start.24 = (bf16[256,1280]{1,0:T(8,128)(2,1)}, bf16[256,1280]{1,0:T(8,128)(2,1)S(1)}, u32[]{:S(2)}, u32[]{:S(2)}) collective-permute-start(bf16[256,1280]{1,0:T(8,128)(2,1)} %shard_map.55), channel_id=1, source_target_pairs={{0,24},{8,16},{16,8},{24,0},{1,25},{9,17},{17,9},{25,1},{2,26},{10... | collective-permute-start | bytes 1966088 | tf_op jit(solution)/shard_map/ppermute | solution.py:149
  (10 other events, 89.7 us)
Sparse Core Ops, SparseCore 0:
  8.9 167.2 all-gather.4
  177.8 130.1 all-gather.8
  309.6 42.5 all-gather.10
  353.6 162.9 all-gather.6

commit v4 on v3

--- a/solution.py
+++ b/solution.py
@@ -1,3 +1,5 @@
+import functools
+
 import jax
 import jax.numpy as jnp
 from jax import lax
@@ -75,61 +77,56 @@
     )(z, *[w] * UP_SPLIT)
 
 
-def down_kernel(meta, *refs):
-    n_w = 4 * DOWN_SPLIT
-    x_ref, y_ref = refs[-2], refs[-1]
-    pieces = y_ref.shape[0] // refs[0].shape[0]
-    hs, ws = refs[:4 * pieces], refs[4 * pieces:-2]
+def down_kernel(n_owner, pieces, final, with_part, meta, *refs):
+    refs = list(refs)
+    y_ref = refs.pop()
+    x_ref = refs.pop() if final else None
+    part_ref = refs.pop() if with_part else None
+    hs, ws = refs[:n_owner * pieces], refs[n_owner * pieces:]
     depth = ws[0].shape[0]
-
-    def product(ws):
-        branch = None
-        for j in range(4):
-            for s in range(DOWN_SPLIT):
-                parts = [h[:, s * depth:(s + 1) * depth] for h in hs[j * pieces:(j + 1) * pieces]]
-                lhs = parts[0] if pieces == 1 else jnp.concatenate(parts, axis=0)
-                term = jnp.dot(lhs, ws[j * DOWN_SPLIT + s][...], preferred_element_type=jnp.float32)
-                branch = term if branch is None else branch + term
-        y_ref[...] = (x_ref[...].astype(jnp.float32) + branch).astype(jnp.bfloat16)
-
-    if len(ws) == n_w:
-        product(ws)
-    else:
-        first = pl.program_id(0) < FIRST_COLS // DOWN_TILE
-        pl.when(first)(lambda: product(ws[:n_w]))
-        pl.when(jnp.logical_not(first))(lambda: product(ws[n_w:]))
-
-
-def down(meta, at, step, hs, ws, x, x_col):
+    branch = part_ref[...] if with_part else None
+    for j in range(n_owner):
+        for s in range(DOWN_SPLIT):
+            parts = [h[:, s * depth:(s + 1) * depth] for h in hs[j * pieces:(j + 1) * pieces]]
+            lhs = parts[0] if pieces == 1 else jnp.concatenate(parts, axis=0)
+            term = jnp.dot(lhs, ws[j * DOWN_SPLIT + s][...], preferred_element_type=jnp.float32)
+            branch = term if branch is None else branch + term
+    if final:
+        branch = x_ref[...].astype(jnp.float32) + branch
+    y_ref[...] = branch.astype(y_ref.dtype)
+
+
+def down(meta, at, step, hs, owners, w, part=None, x=None, x_col=0):
     pieces = len(hs[0])
     hid = hs[0][0].shape[1]
     rows = step * pieces
-    cols = sum(w.shape[1] for w in ws)
-    w_specs, operands, start = [], [], 0
-    for w in ws:
-        tiles = w.shape[1] // DOWN_TILE
-        for j in range(4):
-            for s in range(DOWN_SPLIT):
-                def index(n, m, j=j, s=s, start=start, tiles=tiles):
-                    return (m[j] * DOWN_SPLIT + s, jnp.clip(n - start, 0, tiles - 1))
-
-                w_specs.append(pl.BlockSpec((hid // DOWN_SPLIT, DOWN_TILE), index))
-                operands.append(w)
-        start += tiles
+    cols = w.shape[1]
+    n_owner = len(owners)
+    once = pl.Buffered(buffer_count=1)
+    specs = [pl.BlockSpec((step, hid), lambda n, m: (0, 0), pipeline_mode=once)] * (n_owner * pieces)
+    specs += [
+        pl.BlockSpec((hid // DOWN_SPLIT, DOWN_TILE), lambda n, m, j=j, s=s: (m[j] * DOWN_SPLIT + s, n))
+        for j in owners for s in range(DOWN_SPLIT)
+    ]
+    operands = [h for owner in hs for h in owner] + [w] * (n_owner * DOWN_SPLIT)
+    if part is not None:
+        specs.append(pl.BlockSpec((rows, DOWN_TILE), lambda n, m: (at, n)))
+        operands.append(part)
+    if x is not None:
+        specs.append(pl.BlockSpec((rows, DOWN_TILE), lambda n, m: (at, x_col // DOWN_TILE + n)))
+        operands.append(x)
     return pl.pallas_call(
-        down_kernel,
+        functools.partial(down_kernel, n_owner, pieces, x is not None, part is not None),
         grid_spec=pltpu.PrefetchScalarGridSpec(
             num_scalar_prefetch=1,
             grid=(cols // DOWN_TILE,),
-            in_specs=[pl.BlockSpec((step, hid), lambda n, m: (0, 0))] * (4 * pieces)
-            + w_specs
-            + [pl.BlockSpec((rows, DOWN_TILE), lambda n, m: (at, x_col // DOWN_TILE + n))],
+            in_specs=specs,
             out_specs=pl.BlockSpec((rows, DOWN_TILE), lambda n, m: (0, n)),
         ),
-        out_shape=jax.ShapeDtypeStruct((rows, cols), jnp.bfloat16),
+        out_shape=jax.ShapeDtypeStruct((rows, cols), jnp.float32 if x is None else jnp.bfloat16),
         compiler_params=pltpu.CompilerParams(vmem_limit_bytes=VMEM_LIMIT),
-        cost_estimate=pl.CostEstimate(flops=8 * rows * hid * cols, bytes_accessed=8 * hid * cols, transcendentals=0),
-    )(meta, *[h for owner in hs for h in owner], *operands, x)
+        cost_estimate=pl.CostEstimate(flops=2 * n_owner * rows * hid * cols, bytes_accessed=2 * n_owner * hid * cols, transcendentals=0),
+    )(meta, *operands)
 
 
 def copy_kernel(in_ref, out_ref):
@@ -195,20 +192,22 @@
             h_far += [far(h_other[c]) for c in (2 * p, 2 * p + 1)]
         h_opp = [near(h) for h in h_far]
 
-        def call(chunks, ws, x, x_col):
-            hs = [[h[c] for c in chunks] for h in (h_mine, h_near, h_far, h_opp)]
-            return down(meta, chunks[0] // len(chunks), step, hs, ws, x, x_col)
-
+        pieces = (h_mine, h_near, h_far, h_opp)
+
+        def call(chunks, owners, w, **rest):
+            return down(meta, chunks[0] // len(chunks), step, [[pieces[j][c] for c in chunks] for j in owners], owners, w, **rest)
+
+        every = tuple(range(CHUNKS))
         y = jnp.zeros((rows, width), jnp.bfloat16)
+        far_part = call(every, (0, 1), far_panel)
         for chunks in ((0, 1), (2,), (3,)):
-            part = far(call(chunks, [far_panel], b1, 0))
-            y = lax.dynamic_update_slice(y, part, ((1 - side) * half + chunks[0] * step, 0))
-        part = call((0, 1), [own_first], x_mine, 0)
-        y = lax.dynamic_update_slice(y, part, (side * half, 0))
-        part = call((0, 1), [own_last], x_mine, FIRST_COLS)
-        y = lax.dynamic_update_slice(y, part, (side * half, FIRST_COLS))
-        part = call((2, 3), [own_first, own_last], x_mine, 0)
-        y = lax.dynamic_update_slice(y, part, (side * half + 2 * step, 0))
+            done = call(chunks, (2, 3), far_panel, part=far_part, x=b1)
+            y = lax.dynamic_update_slice(y, far(done), ((1 - side) * half + chunks[0] * step, 0))
+        own_part = call(every, (0, 1, 2), own_first)
+        done = call(every, (3,), own_first, part=own_part, x=x_mine)
+        y = lax.dynamic_update_slice(y, done, (side * half, 0))
+        done = call(every, (0, 1, 2, 3), own_last, x=x_mine, x_col=FIRST_COLS)
+        y = lax.dynamic_update_slice(y, done, (side * half, FIRST_COLS))
         return y
 
     return jax.shard_map(local_block, mesh=mesh, in_specs=(tok_spec, P("col"), P("row", "col"), P("row", "col")), out_specs=tok_spec, check_vma=False)

time: 845 us -> 786 us (0.930)
  waiting for transfers between devices: 501 us -> 440 us
    ppermute x13, waiting for transfers between devices: 251 us -> 85.7 us  [near(): return lax.ppermute(v, 'col', near_pairs)]
    ppermute x12, waiting for transfers between devices: 248 us -> 353 us  [far(): return lax.ppermute(v, 'col', far_pairs)]
    pallas_call x6 -> x7, Pallas kernels: 140 us -> 142 us  [down(): pl.pallas_call(functools.partial(down_kernel, n_owner, pieces, x is not N...]
  transfers between devices with their start and end apart: 29 -> 29, of which waited for: 14 -> 12; matrix products, arithmetic and copies ran while one was open for 2% -> 2% of each run, Pallas kernels for 30% -> 30%
where the time goes in v4:
time: 786 us; the launch traced here: 779 us
  waiting for transfers between devices  440 us (56%)
  Pallas kernels  280 us (36%)
  starting transfers between devices  28.7 us (4%)
  local copies, waits for them, and re-layouts  15.9 us (2%)
  between operations  13.4 us (2%)
    ppermute x12, waiting for transfers between devices, far(): return lax.ppermute(v, 'col', far_pairs)  353 us
    pallas_call x7, Pallas kernels, down(): pl.pallas_call(functools.partial(down_kernel, n_owner, pieces, x is not N...  142 us
    pallas_call x4, Pallas kernels, up(): pl.pallas_call(up_kernel, grid=(pl.cdiv(hid, UP_TILE),), in_specs=[pl.Blo...  109 us
    ppermute x13, waiting for transfers between devices, near(): return lax.ppermute(v, 'col', near_pairs)  85.7 us
    pallas_call x2, Pallas kernels, norm(): pl.pallas_call(norm_kernel, grid_spec=pltpu.PrefetchScalarGridSpec(num_sc...  27.8 us
    ppermute x12, starting transfers between devices, far(): return lax.ppermute(v, 'col', far_pairs)  21.5 us
  transfers between devices with their start and end apart: 29, of which 12 were waited for; matrix products, arithmetic and copies ran while one was open for 2% of the time, Pallas kernels for 30%

profile of v4, /device:TPU:97, one launch (start us, length us, event | category | flops | bytes accessed | tf_op | source)
XLA Modules:
  0.0 779.2 jit_solution(4121260531027981727)
XLA Ops:
  7.4 5.3 collective-permute-start.4
  12.7 4.2 slice.6
  16.8 2.1 slice.7
  20.9 87.4 %collective-permute-done.4 = bf16[1728,1280]{1,0:T(8,128)(2,1)} collective-permute-done((bf16[1728,1280]{1,0:T(8,128)(2,1)}, bf16[1728,1280]{1,0:T(8,128)(2,1)}, u32[]{:S(2)}, u32[]{:S(2)}) %collective-permute-start.4) | collective-permute-done | bytes 4423712 | tf_op jit(solution)/shard_map/ppermute | solution.py:146
  109.8 4.4 constant_dynamic-slice_fusion
  114.2 2.4 collective-permute-start.12
  116.6 56.4 %collective-permute-done.12.refs_2_.refs_9_.refs_7_ = bf16[1024,1280]{1,0:T(8,128)(2,1)} collective-permute-done((bf16[1024,1280]{1,0:T(8,128)(2,1)}, bf16[1024,1280]{1,0:T(8,128)(2,1)}, u32[]{:S(2)}, u32[]{:S(2)}) %collective-permute-start.12) | collective-permute-done | bytes 2621472 | tf_op jit(solution)/shard_map/ppermute | solution.py:146
  174.4 2.1 collective-permute-start.1
  179.2 108.6 %collective-permute-done.6.refs_6_ = f32[1,1280]{1,0:T(1,128)S(1)} collective-permute-done((f32[1,1280]{1,0:T(1,128)S(1)}, f32[1,1280]{1,0:T(1,128)S(1)}, u32[]{:S(2)}, u32[]{:S(2)}) %collective-permute-start.6) | collective-permute-done | bytes 5152 | tf_op jit(solution)/shard_map/ppermute | solution.py:146
  287.9 2.9 collective-permute-done.5.refs_5_
  291.3 2.3 collective-permute-done.7.refs_7_
  294.2 13.7 %shard_map.49.z_ref = bf16[1024,5120]{1,0:T(8,128)(2,1)} custom-call(s32[4]{0:T(128)} %pad_add_fusion.meta, bf16[1024,1280]{1,0:T(8,128)(2,1)} %copy-done, bf16[1024,1280]{1,0:T(8,128)(2,1)} %collective-permute-done.2.refs_1_, bf16[1024,1280]{1,0:T(8,128)(2,1)} %collective-permute-done.12.refs_2_.refs_9_.refs_7_, ...), custom_call_target="tpu_custom_call" | custom-call | flops 335544320 | bytes 20971520 | tf_op jit(solution)/shard_map/pallas_call | solution.py:39
  307.9 14.0 %shard_map.47.z_ref = bf16[1024,5120]{1,0:T(8,128)(2,1)} custom-call(s32[4]{0:T(128)} %pad_add_fusion.meta, bf16[1024,1280]{1,0:T(8,128)(2,1)} %get-tuple-element.30.refs_0_, bf16[1024,1280]{1,0:T(8,128)(2,1)} %collective-permute-done.refs_1_, bf16[1024,1280]{1,0:T(8,128)(2,1)} %collective-permute-done.1.refs_2_, ...), custom_call_target="tpu_custom_call" | custom-call | flops 335544320 | bytes 20971520 | tf_op jit(solution)/shard_map/pallas_call | solution.py:39
  322.0 26.9 %shard_map.50 = (bf16[256,3456]{1,0:T(8,128)(2,1)}, bf16[256,3456]{1,0:T(8,128)(2,1)}) custom-call(bf16[1024,5120]{1,0:T(8,128)(2,1)} %shard_map.49.z_ref, bf16[5120,3456]{1,0:T(8,128)(2,1)} %all-gather.5.cloned.1.call-done.refs_0_.refs_1_.refs_2_.refs_3_, bf16[5120,3456]{1,0:T(8,128)(2,1)} %all-gather.5.cloned.1.call-done.refs_0_.refs_1_.refs_2_.refs_3_, ...), custom_call_target="tpu_custom_call" | custom-call | flops 18119393280 | bytes 35389440 | tf_op jit(solution)/shard_map/pallas_call | solution.py:68
  350.4 28.5 %shard_map.51 = (bf16[256,3456]{1,0:T(8,128)(2,1)}, bf16[256,3456]{1,0:T(8,128)(2,1)}) custom-call(bf16[1024,5120]{1,0:T(8,128)(2,1)} %shard_map.49.z_ref, bf16[5120,3456]{1,0:T(8,128)(2,1)} %all-gather.5.cloned.1.call-done.refs_0_.refs_1_.refs_2_.refs_3_, bf16[5120,3456]{1,0:T(8,128)(2,1)} %all-gather.5.cloned.1.call-done.refs_0_.refs_1_.refs_2_.refs_3_, ...), custom_call_target="tpu_custom_call" | custom-call | flops 18119393280 | bytes 35389440 | tf_op jit(solution)/shard_map/pallas_call | solution.py:68
  378.9 26.7 %shard_map.48 = (bf16[256,3456]{1,0:T(8,128)(2,1)}, bf16[256,3456]{1,0:T(8,128)(2,1)}) custom-call(bf16[1024,5120]{1,0:T(8,128)(2,1)} %shard_map.47.z_ref, bf16[5120,3456]{1,0:T(8,128)(2,1)} %all-gather.5.cloned.1.call-done.refs_0_.refs_1_.refs_2_.refs_3_, bf16[5120,3456]{1,0:T(8,128)(2,1)} %all-gather.5.cloned.1.call-done.refs_0_.refs_1_.refs_2_.refs_3_, ...), custom_call_target="tpu_custom_call" | custom-call | flops 18119393280 | bytes 35389440 | tf_op jit(solution)/shard_map/pallas_call | solution.py:68
  408.3 26.9 %shard_map.54 = (bf16[256,3456]{1,0:T(8,128)(2,1)}, bf16[256,3456]{1,0:T(8,128)(2,1)}) custom-call(bf16[1024,5120]{1,0:T(8,128)(2,1)} %shard_map.47.z_ref, bf16[5120,3456]{1,0:T(8,128)(2,1)} %all-gather.5.cloned.1.call-done.refs_0_.refs_1_.refs_2_.refs_3_, bf16[5120,3456]{1,0:T(8,128)(2,1)} %all-gather.5.cloned.1.call-done.refs_0_.refs_1_.refs_2_.refs_3_, ...), custom_call_target="tpu_custom_call" | custom-call | flops 18119393280 | bytes 35389440 | tf_op jit(solution)/shard_map/pallas_call | solution.py:68
  438.0 22.4 %collective-permute-done.16.refs_6_ = bf16[256,3456]{1,0:T(8,128)(2,1)} collective-permute-done((bf16[256,3456]{1,0:T(8,128)(2,1)}, bf16[256,3456]{1,0:T(8,128)(2,1)}, u32[]{:S(2)}, u32[]{:S(2)}) %collective-permute-start.16) | collective-permute-done | bytes 1769504 | tf_op jit(solution)/shard_map/ppermute | solution.py:143
  461.9 17.3 %collective-permute-done.9.refs_1_.refs_9_ = bf16[256,3456]{1,0:T(8,128)(2,1)} collective-permute-done((bf16[256,3456]{1,0:T(8,128)(2,1)}, bf16[256,3456]{1,0:T(8,128)(2,1)}, u32[]{:S(2)}, u32[]{:S(2)}) %collective-permute-start.9) | collective-permute-done | bytes 1769504 | tf_op jit(solution)/shard_map/ppermute | solution.py:146
  480.1 37.1 %collective-permute-done.19.refs_0_.refs_10_ = bf16[256,3456]{1,0:T(8,128)(2,1)} collective-permute-done((bf16[256,3456]{1,0:T(8,128)(2,1)}, bf16[256,3456]{1,0:T(8,128)(2,1)}, u32[]{:S(2)}, u32[]{:S(2)}) %collective-permute-start.19) | collective-permute-done | bytes 1769504 | tf_op jit(solution)/shard_map/ppermute | solution.py:146
  518.0 37.1 %collective-permute-done.22.refs_0_.refs_11_ = bf16[256,3456]{1,0:T(8,128)(2,1)} collective-permute-done((bf16[256,3456]{1,0:T(8,128)(2,1)}, bf16[256,3456]{1,0:T(8,128)(2,1)}, u32[]{:S(2)}, u32[]{:S(2)}) %collective-permute-start.22) | collective-permute-done | bytes 1769504 | tf_op jit(solution)/shard_map/ppermute | solution.py:146
  555.9 35.0 %shard_map.57.refs_6_ = f32[1024,1024]{1,0:T(8,128)} custom-call(s32[4]{0:T(128)} %pad_add_fusion.meta, bf16[256,3456]{1,0:T(8,128)(2,1)} %get-tuple-element.21.refs_0_, bf16[256,3456]{1,0:T(8,128)(2,1)} %get-tuple-element.22.refs_1_, bf16[256,3456]{1,0:T(8,128)(2,1)} %get-tuple-element.23.refs_2_, bf16[256,3456]{1,0:T(8,128)(2,1)} %get-tuple-element.24.refs_3_, ...), custom_call_target="tpu_custom_call" | custom-call | flops 21743271936 | bytes 21233664 | tf_op jit(solution)/shard_map/pallas_call | solution.py:118
  591.0 20.2 %collective-permute-done.20.refs_1_.refs_2_.refs_14_ = bf16[256,3456]{1,0:T(8,128)(2,1)} collective-permute-done((bf16[256,3456]{1,0:T(8,128)(2,1)}, bf16[256,3456]{1,0:T(8,128)(2,1)}, u32[]{:S(2)}, u32[]{:S(2)}) %collective-permute-start.20) | collective-permute-done | bytes 1769504 | tf_op jit(solution)/shard_map/ppermute | solution.py:143
  611.3 37.9 %collective-permute-done.23.refs_1_.refs_3_.refs_15_ = bf16[256,3456]{1,0:T(8,128)(2,1)} collective-permute-done((bf16[256,3456]{1,0:T(8,128)(2,1)}, bf16[256,3456]{1,0:T(8,128)(2,1)}, u32[]{:S(2)}, u32[]{:S(2)}) %collective-permute-start.23) | collective-permute-done | bytes 1769504 | tf_op jit(solution)/shard_map/ppermute | solution.py:143
  649.2 20.6 %shard_map.59 = bf16[1024,256]{1,0:T(8,128)(2,1)} custom-call(s32[4]{0:T(128)} %pad_add_fusion.meta, bf16[256,3456]{1,0:T(8,128)(2,1)} %get-tuple-element.21.refs_0_, bf16[256,3456]{1,0:T(8,128)(2,1)} %get-tuple-element.22.refs_1_, bf16[256,3456]{1,0:T(8,128)(2,1)} %get-tuple-element.23.refs_2_, bf16[256,3456]{1,0:T(8,128)(2,1)} %get-tuple-element.24.refs_3_, ...), custom_call_target="tpu_custom_call" | custom-call | flops 7247757312 | bytes 7077888 | tf_op jit(solution)/shard_map/pallas_call | solution.py:118
  669.8 28.5 %shard_map.52.refs_8_.refs_6_ = f32[1024,1280]{1,0:T(8,128)} custom-call(s32[4]{0:T(128)} %pad_add_fusion.meta, bf16[256,3456]{1,0:T(8,128)(2,1)} %get-tuple-element.21.refs_0_, bf16[256,3456]{1,0:T(8,128)(2,1)} %get-tuple-element.22.refs_1_, bf16[256,3456]{1,0:T(8,128)(2,1)} %get-tuple-element.23.refs_2_, bf16[256,3456]{1,0:T(8,128)(2,1)} %get-tuple-element.24.refs_3_, ...), custom_call_target="tpu_custom_call" | custom-call | flops 18119393280 | bytes 17694720 | tf_op jit(solution)/shard_map/pallas_call | solution.py:118
  698.3 17.4 %shard_map.53 = bf16[512,1280]{1,0:T(8,128)(2,1)} custom-call(s32[4]{0:T(128)} %pad_add_fusion.meta, bf16[256,3456]{1,0:T(8,128)(2,1)} %collective-permute-done.8.refs_0_.refs_8_, bf16[256,3456]{1,0:T(8,128)(2,1)} %collective-permute-done.9.refs_1_.refs_9_, bf16[256,3456]{1,0:T(8,128)(2,1)} %collective-permute-done.10.refs_2_.refs_0_.refs_12_, ...), custom_call_target="tpu_custom_call" | custom-call | flops 9059696640 | bytes 17694720 | tf_op jit(solution)/shard_map/pallas_call | solution.py:118
  716.7 13.1 %shard_map.56 = bf16[256,1280]{1,0:T(8,128)(2,1)} custom-call(s32[4]{0:T(128)} %pad_add_fusion.meta, bf16[256,3456]{1,0:T(8,128)(2,1)} %collective-permute-done.22.refs_0_.refs_11_, bf16[256,3456]{1,0:T(8,128)(2,1)} %collective-permute-done.23.refs_1_.refs_3_.refs_15_, ...), custom_call_target="tpu_custom_call" | custom-call | flops 4529848320 | bytes 17694720 | tf_op jit(solution)/shard_map/pallas_call | solution.py:118
  731.5 13.1 %shard_map.55 = bf16[256,1280]{1,0:T(8,128)(2,1)} custom-call(s32[4]{0:T(128)} %pad_add_fusion.meta, bf16[256,3456]{1,0:T(8,128)(2,1)} %collective-permute-done.19.refs_0_.refs_10_, bf16[256,3456]{1,0:T(8,128)(2,1)} %collective-permute-done.20.refs_1_.refs_2_.refs_14_, ...), custom_call_target="tpu_custom_call" | custom-call | flops 4529848320 | bytes 17694720 | tf_op jit(solution)/shard_map/pallas_call | solution.py:118
  745.5 14.3 %shard_map.58 = bf16[1024,1024]{1,0:T(8,128)(2,1)} custom-call(s32[4]{0:T(128)} %pad_add_fusion.meta, bf16[256,3456]{1,0:T(8,128)(2,1)} %collective-permute-done.10.refs_2_.refs_0_.refs_12_, bf16[256,3456]{1,0:T(8,128)(2,1)} %collective-permute-done.11.refs_3_.refs_1_.refs_13_, bf16[256,3456]{1,0:T(8,128)(2,1)} %collective-permute-done.20.refs_1_.refs_2_.refs_14_, ...), custom_call_target="tpu_custom_call" | custom-call | flops 7247757312 | bytes 7077888 | tf_op jit(solution)/shard_map/pallas_call | solution.py:118
  760.3 8.7 %collective-permute-done.21 = bf16[256,1280]{1,0:T(8,128)(2,1)S(1)} collective-permute-done((bf16[256,1280]{1,0:T(8,128)(2,1)}, bf16[256,1280]{1,0:T(8,128)(2,1)S(1)}, u32[]{:S(2)}, u32[]{:S(2)}) %collective-permute-start.21) | collective-permute-done | bytes 655392 | tf_op jit(solution)/shard_map/ppermute | solution.py:146
  769.5 2.3 copy-done.4
  (77 shorter events, 25.9 us)
Async XLA Ops:
  6.5 315.4 %all-gather.5.cloned.1.call-start = ((), (), s32[]{:S(2)}) async-start(), calls=%async_computation | async-start | bytes 39813120 | tf_op jit(solution)/shard_map/all_gather | solution.py:149
  7.3 548.6 %all-gather.9.cloned.1.call-start = ((), (), s32[]{:S(2)}) async-start(), calls=%async_computation.2 | async-start | bytes 31850496 | tf_op jit(solution)/shard_map/all_gather | solution.py:149
  7.4 100.9 %collective-permute-start.4 = (bf16[1728,1280]{1,0:T(8,128)(2,1)}, bf16[1728,1280]{1,0:T(8,128)(2,1)}, u32[]{:S(2)}, u32[]{:S(2)}) collective-permute-start(bf16[1728,1280]{1,0:T(8,128)(2,1)} %param.7), channel_id=1, source_target_pairs={{0,24},{8,16},{16,8},{24,0},{1,25},{9,17},{17,9},{25,1},{2,26},{10... | collective-permute-start | bytes 13271048 | tf_op jit(solution)/shard_map/ppermute | solution.py:146
  108.3 482.7 %all-gather.11.cloned.1.call-start = ((), (), s32[]{:S(2)}) async-start(), calls=%async_computation.3 | async-start | bytes 7962624 | tf_op jit(solution)/shard_map/all_gather | solution.py:149
  109.1 560.7 %all-gather.7.cloned.1.call-start = ((), (), s32[]{:S(2)}) async-start(), calls=%async_computation.1 | async-start | bytes 39813120 | tf_op jit(solution)/shard_map/all_gather | solution.py:149
  114.2 179.4 %copy-start = (bf16[1024,1280]{1,0:T(8,128)(2,1)}, bf16[1024,1280]{1,0:T(8,128)(2,1)S(1)}, u32[]{:S(2)}) copy-start(bf16[1024,1280]{1,0:T(8,128)(2,1)S(1)} %get-tuple-element.29.refs_0_.refs_7_.refs_24_) | copy-start | bytes 7864324
  114.2 58.8 %collective-permute-start.12 = (bf16[1024,1280]{1,0:T(8,128)(2,1)}, bf16[1024,1280]{1,0:T(8,128)(2,1)}, u32[]{:S(2)}, u32[]{:S(2)}) collective-permute-start(bf16[1024,1280]{1,0:T(8,128)(2,1)} %get-tuple-element.30.refs_0_), channel_id=1, source_target_pairs={{0,24},{8,16},{16,8},{24,0},{1,25},{9,17},{17,9},{25,1},{2,26},{10... | collective-permute-start | bytes 7864328 | tf_op jit(solution)/shard_map/ppermute | solution.py:146
  116.6 60.0 %collective-permute-start.2 = (bf16[1024,1280]{1,0:T(8,128)(2,1)S(1)}, bf16[1024,1280]{1,0:T(8,128)(2,1)}, u32[]{:S(2)}, u32[]{:S(2)}) collective-permute-start(bf16[1024,1280]{1,0:T(8,128)(2,1)S(1)} %get-tuple-element.29.refs_0_.refs_7_.refs_24_), channel_id=1, source_target_pairs={{0,8},{8,0},{16,24},{24,16},{1,9},{9,1},{17,25},{25,17},{2,10},{10... | collective-permute-start | bytes 7864328 | tf_op jit(solution)/shard_map/ppermute | solution.py:143
  173.0 120.6 %collective-permute-start.13 = (bf16[1024,1280]{1,0:T(8,128)(2,1)}, bf16[1024,1280]{1,0:T(8,128)(2,1)}, u32[]{:S(2)}, u32[]{:S(2)}) collective-permute-start(bf16[1024,1280]{1,0:T(8,128)(2,1)} %collective-permute-done.12.refs_2_.refs_9_.refs_7_), channel_id=1, source_target_pairs={{0,8},{8,0},{16,24},{24,16},{1,9},{9,1},{17,25},{25,17},{2,10},{10... | collective-permute-start | bytes 7864328 | tf_op jit(solution)/shard_map/ppermute | solution.py:143
  173.0 135.0 %collective-permute-start = (bf16[1024,1280]{1,0:T(8,128)(2,1)}, bf16[1024,1280]{1,0:T(8,128)(2,1)}, u32[]{:S(2)}, u32[]{:S(2)}) collective-permute-start(bf16[1024,1280]{1,0:T(8,128)(2,1)} %get-tuple-element.30.refs_0_), channel_id=1, source_target_pairs={{0,8},{8,0},{16,24},{24,16},{1,9},{9,1},{17,25},{25,17},{2,10},{10... | collective-permute-start | bytes 7864328 | tf_op jit(solution)/shard_map/ppermute | solution.py:143
  174.4 133.5 %collective-permute-start.1 = (bf16[1024,1280]{1,0:T(8,128)(2,1)S(1)}, bf16[1024,1280]{1,0:T(8,128)(2,1)}, u32[]{:S(2)}, u32[]{:S(2)}) collective-permute-start(bf16[1024,1280]{1,0:T(8,128)(2,1)S(1)} %get-tuple-element.29.refs_0_.refs_7_.refs_24_), channel_id=1, source_target_pairs={{0,24},{8,16},{16,8},{24,0},{1,25},{9,17},{17,9},{25,1},{2,26},{10... | collective-permute-start | bytes 7864328 | tf_op jit(solution)/shard_map/ppermute | solution.py:146
  176.5 131.4 %collective-permute-start.3 = (bf16[1024,1280]{1,0:T(8,128)(2,1)}, bf16[1024,1280]{1,0:T(8,128)(2,1)}, u32[]{:S(2)}, u32[]{:S(2)}) collective-permute-start(bf16[1024,1280]{1,0:T(8,128)(2,1)} %collective-permute-done.2.refs_1_), channel_id=1, source_target_pairs={{0,24},{8,16},{16,8},{24,0},{1,25},{9,17},{17,9},{25,1},{2,26},{10... | collective-permute-start | bytes 7864328 | tf_op jit(solution)/shard_map/ppermute | solution.py:146
  177.1 110.7 %collective-permute-start.6 = (f32[1,1280]{1,0:T(1,128)S(1)}, f32[1,1280]{1,0:T(1,128)S(1)}, u32[]{:S(2)}, u32[]{:S(2)}) collective-permute-start(f32[1,1280]{1,0:T(1,128)S(1)} %copy-done.6), channel_id=1, source_target_pairs={{0,24},{8,16},{16,8},{24,0},{1,25},{9,17},{17,9},{25,1},{2,26},{10... | collective-permute-start | bytes 15368 | tf_op jit(solution)/shard_map/ppermute | solution.py:146
  287.9 2.9 collective-permute-start.5
  290.7 2.9 collective-permute-start.7
  348.9 86.3 %collective-permute-start.14 = (bf16[256,3456]{1,0:T(8,128)(2,1)}, bf16[256,3456]{1,0:T(8,128)(2,1)S(1)}, u32[]{:S(2)}, u32[]{:S(2)}) collective-permute-start(bf16[256,3456]{1,0:T(8,128)(2,1)} %get-tuple-element.21.refs_0_), channel_id=1, source_target_pairs={{0,8},{8,0},{16,24},{24,16},{1,9},{9,1},{17,25},{25,17},{2,10},{10... | collective-permute-start | bytes 5308424 | tf_op jit(solution)/shard_map/ppermute | solution.py:143
  348.9 87.6 %collective-permute-start.15 = (bf16[256,3456]{1,0:T(8,128)(2,1)}, bf16[256,3456]{1,0:T(8,128)(2,1)S(1)}, u32[]{:S(2)}, u32[]{:S(2)}) collective-permute-start(bf16[256,3456]{1,0:T(8,128)(2,1)} %get-tuple-element.22.refs_1_), channel_id=1, source_target_pairs={{0,8},{8,0},{16,24},{24,16},{1,9},{9,1},{17,25},{25,17},{2,10},{10... | collective-permute-start | bytes 5308424 | tf_op jit(solution)/shard_map/ppermute | solution.py:143
  378.9 81.6 %collective-permute-start.16 = (bf16[256,3456]{1,0:T(8,128)(2,1)}, bf16[256,3456]{1,0:T(8,128)(2,1)}, u32[]{:S(2)}, u32[]{:S(2)}) collective-permute-start(bf16[256,3456]{1,0:T(8,128)(2,1)} %get-tuple-element.23.refs_2_), channel_id=1, source_target_pairs={{0,8},{8,0},{16,24},{24,16},{1,9},{9,1},{17,25},{25,17},{2,10},{10... | collective-permute-start | bytes 5308424 | tf_op jit(solution)/shard_map/ppermute | solution.py:143
  405.6 54.9 %collective-permute-start.8 = (bf16[256,3456]{1,0:T(8,128)(2,1)}, bf16[256,3456]{1,0:T(8,128)(2,1)}, u32[]{:S(2)}, u32[]{:S(2)}) collective-permute-start(bf16[256,3456]{1,0:T(8,128)(2,1)} %get-tuple-element.18), channel_id=1, source_target_pairs={{0,24},{8,16},{16,8},{24,0},{1,25},{9,17},{17,9},{25,1},{2,26},{10... | collective-permute-start | bytes 5308424 | tf_op jit(solution)/shard_map/ppermute | solution.py:146
  406.4 72.8 %collective-permute-start.9 = (bf16[256,3456]{1,0:T(8,128)(2,1)}, bf16[256,3456]{1,0:T(8,128)(2,1)}, u32[]{:S(2)}, u32[]{:S(2)}) collective-permute-start(bf16[256,3456]{1,0:T(8,128)(2,1)} %get-tuple-element.19), channel_id=1, source_target_pairs={{0,24},{8,16},{16,8},{24,0},{1,25},{9,17},{17,9},{25,1},{2,26},{10... | collective-permute-start | bytes 5308424 | tf_op jit(solution)/shard_map/ppermute | solution.py:146
  435.2 120.7 %copy-start.1 = (bf16[256,3456]{1,0:T(8,128)(2,1)}, bf16[256,3456]{1,0:T(8,128)(2,1)S(1)}, u32[]{:S(2)}) copy-start(bf16[256,3456]{1,0:T(8,128)(2,1)S(1)} %collective-permute-done.14.refs_4_) | copy-start | bytes 5308420
  435.2 81.9 %collective-permute-start.19 = (bf16[256,3456]{1,0:T(8,128)(2,1)}, bf16[256,3456]{1,0:T(8,128)(2,1)}, u32[]{:S(2)}, u32[]{:S(2)}) collective-permute-start(bf16[256,3456]{1,0:T(8,128)(2,1)} %get-tuple-element.25), channel_id=1, source_target_pairs={{0,24},{8,16},{16,8},{24,0},{1,25},{9,17},{17,9},{25,1},{2,26},{10... | collective-permute-start | bytes 5308424 | tf_op jit(solution)/shard_map/ppermute | solution.py:146
  436.5 119.5 %copy-start.2 = (bf16[256,3456]{1,0:T(8,128)(2,1)}, bf16[256,3456]{1,0:T(8,128)(2,1)S(1)}, u32[]{:S(2)}) copy-start(bf16[256,3456]{1,0:T(8,128)(2,1)S(1)} %collective-permute-done.15.refs_5_) | copy-start | bytes 5308420
  436.5 118.6 %collective-permute-start.22 = (bf16[256,3456]{1,0:T(8,128)(2,1)}, bf16[256,3456]{1,0:T(8,128)(2,1)}, u32[]{:S(2)}, u32[]{:S(2)}) collective-permute-start(bf16[256,3456]{1,0:T(8,128)(2,1)} %get-tuple-element.26), channel_id=1, source_target_pairs={{0,24},{8,16},{16,8},{24,0},{1,25},{9,17},{17,9},{25,1},{2,26},{10... | collective-permute-start | bytes 5308424 | tf_op jit(solution)/shard_map/ppermute | solution.py:146
  460.4 95.5 %collective-permute-start.17 = (bf16[256,3456]{1,0:T(8,128)(2,1)}, bf16[256,3456]{1,0:T(8,128)(2,1)}, u32[]{:S(2)}, u32[]{:S(2)}) collective-permute-start(bf16[256,3456]{1,0:T(8,128)(2,1)} %get-tuple-element.24.refs_3_), channel_id=1, source_target_pairs={{0,8},{8,0},{16,24},{24,16},{1,9},{9,1},{17,25},{25,17},{2,10},{10... | collective-permute-start | bytes 5308424 | tf_op jit(solution)/shard_map/ppermute | solution.py:143
  460.6 130.5 %collective-permute-start.10 = (bf16[256,3456]{1,0:T(8,128)(2,1)}, bf16[256,3456]{1,0:T(8,128)(2,1)}, u32[]{:S(2)}, u32[]{:S(2)}) collective-permute-start(bf16[256,3456]{1,0:T(8,128)(2,1)} %collective-permute-done.8.refs_0_.refs_8_), channel_id=1, source_target_pairs={{0,8},{8,0},{16,24},{24,16},{1,9},{9,1},{17,25},{25,17},{2,10},{10... | collective-permute-start | bytes 5308424 | tf_op jit(solution)/shard_map/ppermute | solution.py:143
  479.2 111.8 %collective-permute-start.11 = (bf16[256,3456]{1,0:T(8,128)(2,1)}, bf16[256,3456]{1,0:T(8,128)(2,1)}, u32[]{:S(2)}, u32[]{:S(2)}) collective-permute-start(bf16[256,3456]{1,0:T(8,128)(2,1)} %collective-permute-done.9.refs_1_.refs_9_), channel_id=1, source_target_pairs={{0,8},{8,0},{16,24},{24,16},{1,9},{9,1},{17,25},{25,17},{2,10},{10... | collective-permute-start | bytes 5308424 | tf_op jit(solution)/shard_map/ppermute | solution.py:143
  517.1 94.1 %collective-permute-start.20 = (bf16[256,3456]{1,0:T(8,128)(2,1)}, bf16[256,3456]{1,0:T(8,128)(2,1)}, u32[]{:S(2)}, u32[]{:S(2)}) collective-permute-start(bf16[256,3456]{1,0:T(8,128)(2,1)} %collective-permute-done.19.refs_0_.refs_10_), channel_id=1, source_target_pairs={{0,8},{8,0},{16,24},{24,16},{1,9},{9,1},{17,25},{25,17},{2,10},{10... | collective-permute-start | bytes 5308424 | tf_op jit(solution)/shard_map/ppermute | solution.py:143
  555.1 94.1 %collective-permute-start.23 = (bf16[256,3456]{1,0:T(8,128)(2,1)}, bf16[256,3456]{1,0:T(8,128)(2,1)}, u32[]{:S(2)}, u32[]{:S(2)}) collective-permute-start(bf16[256,3456]{1,0:T(8,128)(2,1)} %collective-permute-done.22.refs_0_.refs_11_), channel_id=1, source_target_pairs={{0,8},{8,0},{16,24},{24,16},{1,9},{9,1},{17,25},{25,17},{2,10},{10... | collective-permute-start | bytes 5308424 | tf_op jit(solution)/shard_map/ppermute | solution.py:143
  715.7 44.1 %collective-permute-start.18 = (bf16[512,1280]{1,0:T(8,128)(2,1)}, bf16[512,1280]{1,0:T(8,128)(2,1)S(1)}, u32[]{:S(2)}, u32[]{:S(2)}) collective-permute-start(bf16[512,1280]{1,0:T(8,128)(2,1)} %shard_map.53), channel_id=1, source_target_pairs={{0,24},{8,16},{16,8},{24,0},{1,25},{9,17},{17,9},{25,1},{2,26},{10... | collective-permute-start | bytes 3932168 | tf_op jit(solution)/shard_map/ppermute | solution.py:146
  729.8 39.3 %collective-permute-start.24 = (bf16[256,1280]{1,0:T(8,128)(2,1)}, bf16[256,1280]{1,0:T(8,128)(2,1)S(1)}, u32[]{:S(2)}, u32[]{:S(2)}) collective-permute-start(bf16[256,1280]{1,0:T(8,128)(2,1)} %shard_map.56), channel_id=1, source_target_pairs={{0,24},{8,16},{16,8},{24,0},{1,25},{9,17},{17,9},{25,1},{2,26},{10... | collective-permute-start | bytes 1966088 | tf_op jit(solution)/shard_map/ppermute | solution.py:146
  744.5 24.5 %collective-permute-start.21 = (bf16[256,1280]{1,0:T(8,128)(2,1)}, bf16[256,1280]{1,0:T(8,128)(2,1)S(1)}, u32[]{:S(2)}, u32[]{:S(2)}) collective-permute-start(bf16[256,1280]{1,0:T(8,128)(2,1)} %shard_map.55), channel_id=1, source_target_pairs={{0,24},{8,16},{16,8},{24,0},{1,25},{9,17},{17,9},{25,1},{2,26},{10... | collective-permute-start | bytes 1966088 | tf_op jit(solution)/shard_map/ppermute | solution.py:146
  (8 other events, 102.4 us)
Sparse Core Ops, SparseCore 0:
  8.9 167.2 all-gather.4
  177.8 130.1 all-gather.8
  309.6 42.5 all-gather.10
  353.6 162.9 all-gather.6

commit v5 on v4

--- a/solution.py
+++ b/solution.py
@@ -10,7 +10,7 @@
 
 LN_EPS = 1e-5
 CHUNKS = 4
-FIRST_COLS = 1024
+FIRST_COLS = 768
 NORM_ROWS = 128
 VMEM_LIMIT = 58 * 1024 * 1024
 UP_SPLIT, UP_TILE = 4, 512
@@ -33,15 +33,15 @@
         z_ref[:, pl.ds(pl.multiple_of(meta[j] * width, 128), width)] = piece.astype(jnp.bfloat16)
 
 
-def norm(meta, blocks, gammas):
-    rows, width = blocks[0].shape
+def norm(meta, at, rows, blocks, gammas):
+    width = blocks[0].shape[1]
     d_model = width * 4
     return pl.pallas_call(
         norm_kernel,
         grid_spec=pltpu.PrefetchScalarGridSpec(
             num_scalar_prefetch=1,
             grid=(rows // NORM_ROWS,),
-            in_specs=[pl.BlockSpec((NORM_ROWS, width), lambda i, m: (i, 0))] * 4
+            in_specs=[pl.BlockSpec((NORM_ROWS, width), lambda i, m: (at * (rows // NORM_ROWS) + i, 0))] * 4
             + [pl.BlockSpec((1, width), lambda i, m: (0, 0))] * 4,
             out_specs=pl.BlockSpec((NORM_ROWS, d_model), lambda i, m: (i, 0)),
         ),
@@ -96,7 +96,7 @@
     y_ref[...] = branch.astype(y_ref.dtype)
 
 
-def down(meta, at, step, hs, owners, w, part=None, x=None, x_col=0):
+def down(meta, at, step, hs, owners, w, part=None, part_at=0, x=None, x_col=0):
     pieces = len(hs[0])
     hid = hs[0][0].shape[1]
     rows = step * pieces
@@ -110,7 +110,7 @@
     ]
     operands = [h for owner in hs for h in owner] + [w] * (n_owner * DOWN_SPLIT)
     if part is not None:
-        specs.append(pl.BlockSpec((rows, DOWN_TILE), lambda n, m: (at, n)))
+        specs.append(pl.BlockSpec((rows, DOWN_TILE), lambda n, m: (part_at, n)))
         operands.append(part)
     if x is not None:
         specs.append(pl.BlockSpec((rows, DOWN_TILE), lambda n, m: (at, x_col // DOWN_TILE + n)))
@@ -182,13 +182,13 @@
         own_last = gather(w_last)
 
         h_mine, h_near, h_other, h_far = [], [], [], []
-        z_mine = norm(meta, [x_mine, a1, b1, a2], gammas)
-        z_other = norm(meta, [x_other, a3, b2, b3], other_gammas)
+        z_mine = norm(meta, 0, half, [x_mine, a1, b1, a2], gammas)
         for p in range(CHUNKS // 2):
             h_mine += up(p, step, z_mine, w_in_panel)
             h_near += [near(h_mine[c]) for c in (2 * p, 2 * p + 1)]
         for p in range(CHUNKS // 2):
-            h_other += up(p, step, z_other, w_in_panel)
+            z_other = norm(meta, p, 2 * step, [x_other, a3, b2, b3], other_gammas)
+            h_other += up(0, step, z_other, w_in_panel)
             h_far += [far(h_other[c]) for c in (2 * p, 2 * p + 1)]
         h_opp = [near(h) for h in h_far]
 
@@ -201,11 +201,12 @@
         y = jnp.zeros((rows, width), jnp.bfloat16)
         far_part = call(every, (0, 1), far_panel)
         for chunks in ((0, 1), (2,), (3,)):
-            done = call(chunks, (2, 3), far_panel, part=far_part, x=b1)
+            done = call(chunks, (2, 3), far_panel, part=far_part, part_at=chunks[0] // len(chunks), x=b1)
             y = lax.dynamic_update_slice(y, far(done), ((1 - side) * half + chunks[0] * step, 0))
-        own_part = call(every, (0, 1, 2), own_first)
-        done = call(every, (3,), own_first, part=own_part, x=x_mine)
-        y = lax.dynamic_update_slice(y, done, (side * half, 0))
+        for pair in ((0, 1), (2, 3)):
+            own_part = call(pair, (0, 1, 2), own_first)
+            done = call(pair, (3,), own_first, part=own_part, x=x_mine)
+            y = lax.dynamic_update_slice(y, done, (side * half + pair[0] * step, 0))
         done = call(every, (0, 1, 2, 3), own_last, x=x_mine, x_col=FIRST_COLS)
         y = lax.dynamic_update_slice(y, done, (side * half, FIRST_COLS))
         return y

time: 786 us -> 830 us (1.056)
  waiting for transfers between devices: 440 us -> 472 us
  Pallas kernels: 280 us -> 294 us
    ppermute x13, waiting for transfers between devices: 85.7 us -> 248 us  [near(): return lax.ppermute(v, 'col', near_pairs)]
    ppermute x12, waiting for transfers between devices: 353 us -> 221 us  [far(): return lax.ppermute(v, 'col', far_pairs)]
    pallas_call x7 -> x9, Pallas kernels: 142 us -> 154 us  [down(): pl.pallas_call(functools.partial(down_kernel, n_owner, pieces, x is not N...]
    pallas_call x2 -> x3, Pallas kernels: 27.8 us -> 30.2 us  [norm(): pl.pallas_call(norm_kernel, grid_spec=pltpu.PrefetchScalarGridSpec(num_sc...]
  transfers between devices with their start and end apart: 29 -> 29, of which waited for: 12 -> 14; matrix products, arithmetic and copies ran while one was open for 2% -> 2% of each run, Pallas kernels for 30% -> 30%
where the time goes in v5:
time: 830 us; the launch traced here: 823 us
  waiting for transfers between devices  472 us (57%)
  Pallas kernels  294 us (35%)
  starting transfers between devices  26.7 us (3%)
  local copies, waits for them, and re-layouts  16 us (2%)
  between operations  13.6 us (2%)
    ppermute x13, waiting for transfers between devices, near(): return lax.ppermute(v, 'col', near_pairs)  248 us
    ppermute x12, waiting for transfers between devices, far(): return lax.ppermute(v, 'col', far_pairs)  221 us
    pallas_call x9, Pallas kernels, down(): pl.pallas_call(functools.partial(down_kernel, n_owner, pieces, x is not N...  154 us
    pallas_call x4, Pallas kernels, up(): pl.pallas_call(up_kernel, grid=(pl.cdiv(hid, UP_TILE),), in_specs=[pl.Blo...  109 us
    pallas_call x3, Pallas kernels, norm(): pl.pallas_call(norm_kernel, grid_spec=pltpu.PrefetchScalarGridSpec(num_sc...  30.2 us
    ppermute x12, starting transfers between devices, far(): return lax.ppermute(v, 'col', far_pairs)  21.6 us
  transfers between devices with their start and end apart: 29, of which 14 were waited for; matrix products, arithmetic and copies ran while one was open for 2% of the time, Pallas kernels for 30%

profile of v5, /device:TPU:97, one launch (start us, length us, event | category | flops | bytes accessed | tf_op | source)
XLA Modules:
  0.0 823.1 jit_solution(14829047564916049261)
XLA Ops:
  7.4 5.3 collective-permute-start.4
  12.7 3.4 slice.6
  16.1 2.8 slice.7
  20.8 87.5 %collective-permute-done.4 = bf16[1728,1280]{1,0:T(8,128)(2,1)} collective-permute-done((bf16[1728,1280]{1,0:T(8,128)(2,1)}, bf16[1728,1280]{1,0:T(8,128)(2,1)}, u32[]{:S(2)}, u32[]{:S(2)}) %collective-permute-start.4) | collective-permute-done | bytes 4423712 | tf_op jit(solution)/shard_map/ppermute | solution.py:146
  109.8 4.4 constant_dynamic-slice_fusion
  118.1 53.5 %collective-permute-done.2.refs_1_ = bf16[1024,1280]{1,0:T(8,128)(2,1)} collective-permute-done((bf16[1024,1280]{1,0:T(8,128)(2,1)S(1)}, bf16[1024,1280]{1,0:T(8,128)(2,1)}, u32[]{:S(2)}, u32[]{:S(2)}) %collective-permute-start.2) | collective-permute-done | bytes 2621472 | tf_op jit(solution)/shard_map/ppermute | solution.py:143
  175.1 110.4 %collective-permute-done.6.refs_6_ = f32[1,1280]{1,0:T(1,128)S(1)} collective-permute-done((f32[1,1280]{1,0:T(1,128)S(1)}, f32[1,1280]{1,0:T(1,128)S(1)}, u32[]{:S(2)}, u32[]{:S(2)}) %collective-permute-start.6) | collective-permute-done | bytes 5152 | tf_op jit(solution)/shard_map/ppermute | solution.py:146
  291.3 8.4 %shard_map.54.z_ref = bf16[512,5120]{1,0:T(8,128)(2,1)} custom-call(s32[4]{0:T(128)} %pad_add_fusion.meta, bf16[1024,1280]{1,0:T(8,128)(2,1)} %get-tuple-element.30.refs_0_, bf16[1024,1280]{1,0:T(8,128)(2,1)} %collective-permute-done.refs_1_, bf16[1024,1280]{1,0:T(8,128)(2,1)} %collective-permute-done.1.refs_2_, ...), custom_call_target="tpu_custom_call" | custom-call | flops 167772160 | bytes 10485760 | tf_op jit(solution)/shard_map/pallas_call | solution.py:39
  299.7 8.0 shard_map.47.z_ref
  307.7 13.8 %shard_map.49.z_ref = bf16[1024,5120]{1,0:T(8,128)(2,1)} custom-call(s32[4]{0:T(128)} %pad_add_fusion.meta, bf16[1024,1280]{1,0:T(8,128)(2,1)} %copy-done, bf16[1024,1280]{1,0:T(8,128)(2,1)} %collective-permute-done.2.refs_1_, bf16[1024,1280]{1,0:T(8,128)(2,1)} %collective-permute-done.12.refs_2_.refs_9_.refs_7_, ...), custom_call_target="tpu_custom_call" | custom-call | flops 335544320 | bytes 20971520 | tf_op jit(solution)/shard_map/pallas_call | solution.py:39
  321.5 26.8 %shard_map.55 = (bf16[256,3456]{1,0:T(8,128)(2,1)}, bf16[256,3456]{1,0:T(8,128)(2,1)}) custom-call(bf16[512,5120]{1,0:T(8,128)(2,1)} %shard_map.54.z_ref, bf16[5120,3456]{1,0:T(8,128)(2,1)} %all-gather.5.cloned.1.call-done.refs_0_.refs_1_.refs_2_.refs_3_, bf16[5120,3456]{1,0:T(8,128)(2,1)} %all-gather.5.cloned.1.call-done.refs_0_.refs_1_.refs_2_.refs_3_, ...), custom_call_target="tpu_custom_call" | custom-call | flops 18119393280 | bytes 35389440 | tf_op jit(solution)/shard_map/pallas_call | solution.py:68
  351.0 28.6 %shard_map.50 = (bf16[256,3456]{1,0:T(8,128)(2,1)}, bf16[256,3456]{1,0:T(8,128)(2,1)}) custom-call(bf16[1024,5120]{1,0:T(8,128)(2,1)} %shard_map.49.z_ref, bf16[5120,3456]{1,0:T(8,128)(2,1)} %all-gather.5.cloned.1.call-done.refs_0_.refs_1_.refs_2_.refs_3_, bf16[5120,3456]{1,0:T(8,128)(2,1)} %all-gather.5.cloned.1.call-done.refs_0_.refs_1_.refs_2_.refs_3_, ...), custom_call_target="tpu_custom_call" | custom-call | flops 18119393280 | bytes 35389440 | tf_op jit(solution)/shard_map/pallas_call | solution.py:68
  379.6 26.8 %shard_map.51 = (bf16[256,3456]{1,0:T(8,128)(2,1)}, bf16[256,3456]{1,0:T(8,128)(2,1)}) custom-call(bf16[1024,5120]{1,0:T(8,128)(2,1)} %shard_map.49.z_ref, bf16[5120,3456]{1,0:T(8,128)(2,1)} %all-gather.5.cloned.1.call-done.refs_0_.refs_1_.refs_2_.refs_3_, bf16[5120,3456]{1,0:T(8,128)(2,1)} %all-gather.5.cloned.1.call-done.refs_0_.refs_1_.refs_2_.refs_3_, ...), custom_call_target="tpu_custom_call" | custom-call | flops 18119393280 | bytes 35389440 | tf_op jit(solution)/shard_map/pallas_call | solution.py:68
  407.9 26.9 %shard_map.48 = (bf16[256,3456]{1,0:T(8,128)(2,1)}, bf16[256,3456]{1,0:T(8,128)(2,1)}) custom-call(bf16[512,5120]{1,0:T(8,128)(2,1)} %shard_map.47.z_ref, bf16[5120,3456]{1,0:T(8,128)(2,1)} %all-gather.5.cloned.1.call-done.refs_0_.refs_1_.refs_2_.refs_3_, bf16[5120,3456]{1,0:T(8,128)(2,1)} %all-gather.5.cloned.1.call-done.refs_0_.refs_1_.refs_2_.refs_3_, ...), custom_call_target="tpu_custom_call" | custom-call | flops 18119393280 | bytes 35389440 | tf_op jit(solution)/shard_map/pallas_call | solution.py:68
  437.9 15.9 %collective-permute-done.16.refs_6_.refs_2_ = bf16[256,3456]{1,0:T(8,128)(2,1)} collective-permute-done((bf16[256,3456]{1,0:T(8,128)(2,1)}, bf16[256,3456]{1,0:T(8,128)(2,1)}, u32[]{:S(2)}, u32[]{:S(2)}) %collective-permute-start.16) | collective-permute-done | bytes 1769504 | tf_op jit(solution)/shard_map/ppermute | solution.py:143
  454.0 37.6 %collective-permute-done.17.refs_7_.refs_3_ = bf16[256,3456]{1,0:T(8,128)(2,1)} collective-permute-done((bf16[256,3456]{1,0:T(8,128)(2,1)}, bf16[256,3456]{1,0:T(8,128)(2,1)}, u32[]{:S(2)}, u32[]{:S(2)}) %collective-permute-start.17) | collective-permute-done | bytes 1769504 | tf_op jit(solution)/shard_map/ppermute | solution.py:143
  493.1 16.3 %collective-permute-done.9.refs_1_.refs_5_.refs_9_ = bf16[256,3456]{1,0:T(8,128)(2,1)} collective-permute-done((bf16[256,3456]{1,0:T(8,128)(2,1)}, bf16[256,3456]{1,0:T(8,128)(2,1)}, u32[]{:S(2)}, u32[]{:S(2)}) %collective-permute-start.9) | collective-permute-done | bytes 1769504 | tf_op jit(solution)/shard_map/ppermute | solution.py:146
  509.4 17.6 %shard_map.60.refs_4_ = f32[512,768]{1,0:T(8,128)} custom-call(s32[4]{0:T(128)} %pad_add_fusion.meta, bf16[256,3456]{1,0:T(8,128)(2,1)} %get-tuple-element.23.refs_2_.refs_0_, bf16[256,3456]{1,0:T(8,128)(2,1)} %get-tuple-element.24.refs_3_.refs_1_, bf16[256,3456]{1,0:T(8,128)(2,1)} %collective-permute-done.16.refs_6_.refs_2_, ...), custom_call_target="tpu_custom_call" | custom-call | flops 8153726976 | bytes 15925248 | tf_op jit(solution)/shard_map/pallas_call | solution.py:118
  527.0 2.6 collective-permute-done.15.refs_5_.refs_3_
  529.6 17.1 %shard_map.58.refs_4_ = f32[512,768]{1,0:T(8,128)} custom-call(s32[4]{0:T(128)} %pad_add_fusion.meta, bf16[256,3456]{1,0:T(8,128)(2,1)} %get-tuple-element.21.refs_0_, bf16[256,3456]{1,0:T(8,128)(2,1)} %get-tuple-element.22.refs_1_, bf16[256,3456]{1,0:T(8,128)(2,1)} %copy-done.3, bf16[256,3456]{1,0:T(8,128)(2,1)} %collective-permute-done.15.refs_5_.refs_3_, ...), custom_call_target="tpu_custom_call" | custom-call | flops 8153726976 | bytes 15925248 | tf_op jit(solution)/shard_map/pallas_call | solution.py:118
  546.7 20.8 %collective-permute-done.20.refs_1_.refs_0_.refs_14_ = bf16[256,3456]{1,0:T(8,128)(2,1)} collective-permute-done((bf16[256,3456]{1,0:T(8,128)(2,1)S(1)}, bf16[256,3456]{1,0:T(8,128)(2,1)}, u32[]{:S(2)}, u32[]{:S(2)}) %collective-permute-start.20) | collective-permute-done | bytes 1769504 | tf_op jit(solution)/shard_map/ppermute | solution.py:143
  567.5 37.9 %collective-permute-done.23.refs_1_.refs_15_ = bf16[256,3456]{1,0:T(8,128)(2,1)} collective-permute-done((bf16[256,3456]{1,0:T(8,128)(2,1)S(1)}, bf16[256,3456]{1,0:T(8,128)(2,1)}, u32[]{:S(2)}, u32[]{:S(2)}) %collective-permute-start.23) | collective-permute-done | bytes 1769504 | tf_op jit(solution)/shard_map/ppermute | solution.py:143
  605.4 37.9 %collective-permute-done.10.refs_2_.refs_0_.refs_12_ = bf16[256,3456]{1,0:T(8,128)(2,1)} collective-permute-done((bf16[256,3456]{1,0:T(8,128)(2,1)}, bf16[256,3456]{1,0:T(8,128)(2,1)}, u32[]{:S(2)}, u32[]{:S(2)}) %collective-permute-start.10) | collective-permute-done | bytes 1769504 | tf_op jit(solution)/shard_map/ppermute | solution.py:143
  643.4 37.9 %collective-permute-done.11.refs_3_.refs_1_.refs_13_ = bf16[256,3456]{1,0:T(8,128)(2,1)} collective-permute-done((bf16[256,3456]{1,0:T(8,128)(2,1)}, bf16[256,3456]{1,0:T(8,128)(2,1)}, u32[]{:S(2)}, u32[]{:S(2)}) %collective-permute-start.11) | collective-permute-done | bytes 1769504 | tf_op jit(solution)/shard_map/ppermute | solution.py:143
  681.3 29.7 %shard_map.62 = bf16[1024,512]{1,0:T(8,128)(2,1)} custom-call(s32[4]{0:T(128)} %pad_add_fusion.meta, bf16[256,3456]{1,0:T(8,128)(2,1)} %get-tuple-element.21.refs_0_, bf16[256,3456]{1,0:T(8,128)(2,1)} %get-tuple-element.22.refs_1_, bf16[256,3456]{1,0:T(8,128)(2,1)} %get-tuple-element.23.refs_2_.refs_0_, bf16[256,3456]{1,0:T(8,128)(2,1)} %get-tuple-element.24.refs_3_.refs_1_, ...), custom_call_target="tpu_custom_call" | custom-call | flops 14495514624 | bytes 14155776 | tf_op jit(solution)/shard_map/pallas_call | solution.py:118
  711.0 28.8 %shard_map.52.refs_8_.refs_6_ = f32[1024,1280]{1,0:T(8,128)} custom-call(s32[4]{0:T(128)} %pad_add_fusion.meta, bf16[256,3456]{1,0:T(8,128)(2,1)} %get-tuple-element.21.refs_0_, bf16[256,3456]{1,0:T(8,128)(2,1)} %get-tuple-element.22.refs_1_, bf16[256,3456]{1,0:T(8,128)(2,1)} %get-tuple-element.23.refs_2_.refs_0_, ...), custom_call_target="tpu_custom_call" | custom-call | flops 18119393280 | bytes 17694720 | tf_op jit(solution)/shard_map/pallas_call | solution.py:118
  739.8 17.4 %shard_map.53 = bf16[512,1280]{1,0:T(8,128)(2,1)} custom-call(s32[4]{0:T(128)} %pad_add_fusion.meta, bf16[256,3456]{1,0:T(8,128)(2,1)} %collective-permute-done.8.refs_0_.refs_4_.refs_8_, bf16[256,3456]{1,0:T(8,128)(2,1)} %collective-permute-done.9.refs_1_.refs_5_.refs_9_, bf16[256,3456]{1,0:T(8,128)(2,1)} %collective-permute-done.10.refs_2_.refs_0_.refs_12_, ...), custom_call_target="tpu_custom_call" | custom-call | flops 9059696640 | bytes 17694720 | tf_op jit(solution)/shard_map/pallas_call | solution.py:118
  758.9 8.5 %shard_map.61 = bf16[512,768]{1,0:T(8,128)(2,1)} custom-call(s32[4]{0:T(128)} %pad_add_fusion.meta, bf16[256,3456]{1,0:T(8,128)(2,1)} %collective-permute-done.20.refs_1_.refs_0_.refs_14_, bf16[256,3456]{1,0:T(8,128)(2,1)} %collective-permute-done.23.refs_1_.refs_15_, ...), custom_call_target="tpu_custom_call" | custom-call | flops 2717908992 | bytes 5308416 | tf_op jit(solution)/shard_map/pallas_call | solution.py:118
  767.4 13.1 %shard_map.56 = bf16[256,1280]{1,0:T(8,128)(2,1)} custom-call(s32[4]{0:T(128)} %pad_add_fusion.meta, bf16[256,3456]{1,0:T(8,128)(2,1)} %copy-done.2, bf16[256,3456]{1,0:T(8,128)(2,1)} %collective-permute-done.20.refs_1_.refs_0_.refs_14_, ...), custom_call_target="tpu_custom_call" | custom-call | flops 4529848320 | bytes 17694720 | tf_op jit(solution)/shard_map/pallas_call | solution.py:118
  781.4 13.1 %shard_map.57 = bf16[256,1280]{1,0:T(8,128)(2,1)} custom-call(s32[4]{0:T(128)} %pad_add_fusion.meta, bf16[256,3456]{1,0:T(8,128)(2,1)} %copy-done.1, bf16[256,3456]{1,0:T(8,128)(2,1)} %collective-permute-done.23.refs_1_.refs_15_, ...), custom_call_target="tpu_custom_call" | custom-call | flops 4529848320 | bytes 17694720 | tf_op jit(solution)/shard_map/pallas_call | solution.py:118
  796.2 8.5 %shard_map.59 = bf16[512,768]{1,0:T(8,128)(2,1)} custom-call(s32[4]{0:T(128)} %pad_add_fusion.meta, bf16[256,3456]{1,0:T(8,128)(2,1)} %collective-permute-done.10.refs_2_.refs_0_.refs_12_, bf16[256,3456]{1,0:T(8,128)(2,1)} %collective-permute-done.11.refs_3_.refs_1_.refs_13_, ...), custom_call_target="tpu_custom_call" | custom-call | flops 2717908992 | bytes 5308416 | tf_op jit(solution)/shard_map/pallas_call | solution.py:118
  805.3 7.3 collective-permute-done.24
  (85 shorter events, 34.9 us)
Async XLA Ops:
  6.5 314.9 %all-gather.5.cloned.1.call-start = ((), (), s32[]{:S(2)}) async-start(), calls=%async_computation | async-start | bytes 39813120 | tf_op jit(solution)/shard_map/all_gather | solution.py:149
  7.3 502.1 %all-gather.9.cloned.1.call-start = ((), (), s32[]{:S(2)}) async-start(), calls=%async_computation.2 | async-start | bytes 23887872 | tf_op jit(solution)/shard_map/all_gather | solution.py:149
  7.4 100.9 %collective-permute-start.4 = (bf16[1728,1280]{1,0:T(8,128)(2,1)}, bf16[1728,1280]{1,0:T(8,128)(2,1)}, u32[]{:S(2)}, u32[]{:S(2)}) collective-permute-start(bf16[1728,1280]{1,0:T(8,128)(2,1)} %param.7), channel_id=1, source_target_pairs={{0,24},{8,16},{16,8},{24,0},{1,25},{9,17},{17,9},{25,1},{2,26},{10... | collective-permute-start | bytes 13271048 | tf_op jit(solution)/shard_map/ppermute | solution.py:146
  108.3 438.4 %all-gather.11.cloned.1.call-start = ((), (), s32[]{:S(2)}) async-start(), calls=%async_computation.3 | async-start | bytes 15925248 | tf_op jit(solution)/shard_map/all_gather | solution.py:149
  109.1 601.9 %all-gather.7.cloned.1.call-start = ((), (), s32[]{:S(2)}) async-start(), calls=%async_computation.1 | async-start | bytes 39813120 | tf_op jit(solution)/shard_map/all_gather | solution.py:149
  114.2 185.5 %copy-start = (bf16[1024,1280]{1,0:T(8,128)(2,1)}, bf16[1024,1280]{1,0:T(8,128)(2,1)S(1)}, u32[]{:S(2)}) copy-start(bf16[1024,1280]{1,0:T(8,128)(2,1)S(1)} %get-tuple-element.29.refs_0_.refs_5_.refs_24_) | copy-start | bytes 7864324
  114.2 57.3 %collective-permute-start.2 = (bf16[1024,1280]{1,0:T(8,128)(2,1)S(1)}, bf16[1024,1280]{1,0:T(8,128)(2,1)}, u32[]{:S(2)}, u32[]{:S(2)}) collective-permute-start(bf16[1024,1280]{1,0:T(8,128)(2,1)S(1)} %get-tuple-element.29.refs_0_.refs_5_.refs_24_), channel_id=1, source_target_pairs={{0,8},{8,0},{16,24},{24,16},{1,9},{9,1},{17,25},{25,17},{2,10},{10... | collective-permute-start | bytes 7864328 | tf_op jit(solution)/shard_map/ppermute | solution.py:143
  114.2 59.4 %collective-permute-start.12 = (bf16[1024,1280]{1,0:T(8,128)(2,1)}, bf16[1024,1280]{1,0:T(8,128)(2,1)}, u32[]{:S(2)}, u32[]{:S(2)}) collective-permute-start(bf16[1024,1280]{1,0:T(8,128)(2,1)} %get-tuple-element.30.refs_0_), channel_id=1, source_target_pairs={{0,24},{8,16},{16,8},{24,0},{1,25},{9,17},{17,9},{25,1},{2,26},{10... | collective-permute-start | bytes 7864328 | tf_op jit(solution)/shard_map/ppermute | solution.py:146
  116.6 174.1 %collective-permute-start = (bf16[1024,1280]{1,0:T(8,128)(2,1)}, bf16[1024,1280]{1,0:T(8,128)(2,1)}, u32[]{:S(2)}, u32[]{:S(2)}) collective-permute-start(bf16[1024,1280]{1,0:T(8,128)(2,1)} %get-tuple-element.30.refs_0_), channel_id=1, source_target_pairs={{0,8},{8,0},{16,24},{24,16},{1,9},{9,1},{17,25},{25,17},{2,10},{10... | collective-permute-start | bytes 7864328 | tf_op jit(solution)/shard_map/ppermute | solution.py:143
  117.4 173.2 %collective-permute-start.1 = (bf16[1024,1280]{1,0:T(8,128)(2,1)S(1)}, bf16[1024,1280]{1,0:T(8,128)(2,1)}, u32[]{:S(2)}, u32[]{:S(2)}) collective-permute-start(bf16[1024,1280]{1,0:T(8,128)(2,1)S(1)} %get-tuple-element.29.refs_0_.refs_5_.refs_24_), channel_id=1, source_target_pairs={{0,24},{8,16},{16,8},{24,0},{1,25},{9,17},{17,9},{25,1},{2,26},{10... | collective-permute-start | bytes 7864328 | tf_op jit(solution)/shard_map/ppermute | solution.py:146
  171.6 119.1 %collective-permute-start.3 = (bf16[1024,1280]{1,0:T(8,128)(2,1)}, bf16[1024,1280]{1,0:T(8,128)(2,1)}, u32[]{:S(2)}, u32[]{:S(2)}) collective-permute-start(bf16[1024,1280]{1,0:T(8,128)(2,1)} %collective-permute-done.2.refs_1_), channel_id=1, source_target_pairs={{0,24},{8,16},{16,8},{24,0},{1,25},{9,17},{17,9},{25,1},{2,26},{10... | collective-permute-start | bytes 7864328 | tf_op jit(solution)/shard_map/ppermute | solution.py:146
  173.7 134.0 %collective-permute-start.13 = (bf16[1024,1280]{1,0:T(8,128)(2,1)}, bf16[1024,1280]{1,0:T(8,128)(2,1)}, u32[]{:S(2)}, u32[]{:S(2)}) collective-permute-start(bf16[1024,1280]{1,0:T(8,128)(2,1)} %collective-permute-done.12.refs_2_.refs_9_.refs_7_), channel_id=1, source_target_pairs={{0,8},{8,0},{16,24},{24,16},{1,9},{9,1},{17,25},{25,17},{2,10},{10... | collective-permute-start | bytes 7864328 | tf_op jit(solution)/shard_map/ppermute | solution.py:143
  173.7 111.8 %collective-permute-start.6 = (f32[1,1280]{1,0:T(1,128)S(1)}, f32[1,1280]{1,0:T(1,128)S(1)}, u32[]{:S(2)}, u32[]{:S(2)}) collective-permute-start(f32[1,1280]{1,0:T(1,128)S(1)} %copy-done.11), channel_id=1, source_target_pairs={{0,24},{8,16},{16,8},{24,0},{1,25},{9,17},{17,9},{25,1},{2,26},{10... | collective-permute-start | bytes 15368 | tf_op jit(solution)/shard_map/ppermute | solution.py:146
  285.4 2.5 collective-permute-start.5
  287.9 2.8 collective-permute-start.7
  348.3 86.5 %collective-permute-start.19 = (bf16[256,3456]{1,0:T(8,128)(2,1)}, bf16[256,3456]{1,0:T(8,128)(2,1)S(1)}, u32[]{:S(2)}, u32[]{:S(2)}) collective-permute-start(bf16[256,3456]{1,0:T(8,128)(2,1)} %get-tuple-element.25), channel_id=1, source_target_pairs={{0,24},{8,16},{16,8},{24,0},{1,25},{9,17},{17,9},{25,1},{2,26},{10... | collective-permute-start | bytes 5308424 | tf_op jit(solution)/shard_map/ppermute | solution.py:146
  350.4 86.6 %collective-permute-start.22 = (bf16[256,3456]{1,0:T(8,128)(2,1)}, bf16[256,3456]{1,0:T(8,128)(2,1)S(1)}, u32[]{:S(2)}, u32[]{:S(2)}) collective-permute-start(bf16[256,3456]{1,0:T(8,128)(2,1)} %get-tuple-element.26), channel_id=1, source_target_pairs={{0,24},{8,16},{16,8},{24,0},{1,25},{9,17},{17,9},{25,1},{2,26},{10... | collective-permute-start | bytes 5308424 | tf_op jit(solution)/shard_map/ppermute | solution.py:146
  379.6 58.0 %collective-permute-start.14 = (bf16[256,3456]{1,0:T(8,128)(2,1)}, bf16[256,3456]{1,0:T(8,128)(2,1)S(1)}, u32[]{:S(2)}, u32[]{:S(2)}) collective-permute-start(bf16[256,3456]{1,0:T(8,128)(2,1)} %get-tuple-element.21.refs_0_), channel_id=1, source_target_pairs={{0,8},{8,0},{16,24},{24,16},{1,9},{9,1},{17,25},{25,17},{2,10},{10... | collective-permute-start | bytes 5308424 | tf_op jit(solution)/shard_map/ppermute | solution.py:143
  406.4 47.4 %collective-permute-start.16 = (bf16[256,3456]{1,0:T(8,128)(2,1)}, bf16[256,3456]{1,0:T(8,128)(2,1)}, u32[]{:S(2)}, u32[]{:S(2)}) collective-permute-start(bf16[256,3456]{1,0:T(8,128)(2,1)} %get-tuple-element.23.refs_2_.refs_0_), channel_id=1, source_target_pairs={{0,8},{8,0},{16,24},{24,16},{1,9},{9,1},{17,25},{25,17},{2,10},{10... | collective-permute-start | bytes 5308424 | tf_op jit(solution)/shard_map/ppermute | solution.py:143
  407.8 83.9 %collective-permute-start.17 = (bf16[256,3456]{1,0:T(8,128)(2,1)}, bf16[256,3456]{1,0:T(8,128)(2,1)}, u32[]{:S(2)}, u32[]{:S(2)}) collective-permute-start(bf16[256,3456]{1,0:T(8,128)(2,1)} %get-tuple-element.24.refs_3_.refs_1_), channel_id=1, source_target_pairs={{0,8},{8,0},{16,24},{24,16},{1,9},{9,1},{17,25},{25,17},{2,10},{10... | collective-permute-start | bytes 5308424 | tf_op jit(solution)/shard_map/ppermute | solution.py:143
  434.8 74.6 %copy-start.2 = (bf16[256,3456]{1,0:T(8,128)(2,1)}, bf16[256,3456]{1,0:T(8,128)(2,1)S(1)}, u32[]{:S(2)}) copy-start(bf16[256,3456]{1,0:T(8,128)(2,1)S(1)} %collective-permute-done.19.refs_0_.refs_4_.refs_10_) | copy-start | bytes 5308420
  434.8 57.1 %collective-permute-start.8 = (bf16[256,3456]{1,0:T(8,128)(2,1)}, bf16[256,3456]{1,0:T(8,128)(2,1)}, u32[]{:S(2)}, u32[]{:S(2)}) collective-permute-start(bf16[256,3456]{1,0:T(8,128)(2,1)} %get-tuple-element.18), channel_id=1, source_target_pairs={{0,24},{8,16},{16,8},{24,0},{1,25},{9,17},{17,9},{25,1},{2,26},{10... | collective-permute-start | bytes 5308424 | tf_op jit(solution)/shard_map/ppermute | solution.py:146
  437.0 72.4 %copy-start.1 = (bf16[256,3456]{1,0:T(8,128)(2,1)}, bf16[256,3456]{1,0:T(8,128)(2,1)S(1)}, u32[]{:S(2)}) copy-start(bf16[256,3456]{1,0:T(8,128)(2,1)S(1)} %collective-permute-done.22.refs_0_.refs_5_.refs_11_) | copy-start | bytes 5308420
  437.0 72.4 %collective-permute-start.9 = (bf16[256,3456]{1,0:T(8,128)(2,1)}, bf16[256,3456]{1,0:T(8,128)(2,1)}, u32[]{:S(2)}, u32[]{:S(2)}) collective-permute-start(bf16[256,3456]{1,0:T(8,128)(2,1)} %get-tuple-element.19), channel_id=1, source_target_pairs={{0,24},{8,16},{16,8},{24,0},{1,25},{9,17},{17,9},{25,1},{2,26},{10... | collective-permute-start | bytes 5308424 | tf_op jit(solution)/shard_map/ppermute | solution.py:146
  437.6 92.0 %collective-permute-start.15 = (bf16[256,3456]{1,0:T(8,128)(2,1)}, bf16[256,3456]{1,0:T(8,128)(2,1)}, u32[]{:S(2)}, u32[]{:S(2)}) collective-permute-start(bf16[256,3456]{1,0:T(8,128)(2,1)} %get-tuple-element.22.refs_1_), channel_id=1, source_target_pairs={{0,8},{8,0},{16,24},{24,16},{1,9},{9,1},{17,25},{25,17},{2,10},{10... | collective-permute-start | bytes 5308424 | tf_op jit(solution)/shard_map/ppermute | solution.py:143
  453.8 113.8 %collective-permute-start.20 = (bf16[256,3456]{1,0:T(8,128)(2,1)S(1)}, bf16[256,3456]{1,0:T(8,128)(2,1)}, u32[]{:S(2)}, u32[]{:S(2)}) collective-permute-start(bf16[256,3456]{1,0:T(8,128)(2,1)S(1)} %collective-permute-done.19.refs_0_.refs_4_.refs_10_), channel_id=1, source_target_pairs={{0,8},{8,0},{16,24},{24,16},{1,9},{9,1},{17,25},{25,17},{2,10},{10... | collective-permute-start | bytes 5308424 | tf_op jit(solution)/shard_map/ppermute | solution.py:143
  491.7 113.8 %collective-permute-start.23 = (bf16[256,3456]{1,0:T(8,128)(2,1)S(1)}, bf16[256,3456]{1,0:T(8,128)(2,1)}, u32[]{:S(2)}, u32[]{:S(2)}) collective-permute-start(bf16[256,3456]{1,0:T(8,128)(2,1)S(1)} %collective-permute-done.22.refs_0_.refs_5_.refs_11_), channel_id=1, source_target_pairs={{0,8},{8,0},{16,24},{24,16},{1,9},{9,1},{17,25},{25,17},{2,10},{10... | collective-permute-start | bytes 5308424 | tf_op jit(solution)/shard_map/ppermute | solution.py:143
  492.0 151.4 %collective-permute-start.10 = (bf16[256,3456]{1,0:T(8,128)(2,1)}, bf16[256,3456]{1,0:T(8,128)(2,1)}, u32[]{:S(2)}, u32[]{:S(2)}) collective-permute-start(bf16[256,3456]{1,0:T(8,128)(2,1)} %collective-permute-done.8.refs_0_.refs_4_.refs_8_), channel_id=1, source_target_pairs={{0,8},{8,0},{16,24},{24,16},{1,9},{9,1},{17,25},{25,17},{2,10},{10... | collective-permute-start | bytes 5308424 | tf_op jit(solution)/shard_map/ppermute | solution.py:143
  509.4 171.9 %collective-permute-start.11 = (bf16[256,3456]{1,0:T(8,128)(2,1)}, bf16[256,3456]{1,0:T(8,128)(2,1)}, u32[]{:S(2)}, u32[]{:S(2)}) collective-permute-start(bf16[256,3456]{1,0:T(8,128)(2,1)} %collective-permute-done.9.refs_1_.refs_5_.refs_9_), channel_id=1, source_target_pairs={{0,8},{8,0},{16,24},{24,16},{1,9},{9,1},{17,25},{25,17},{2,10},{10... | collective-permute-start | bytes 5308424 | tf_op jit(solution)/shard_map/ppermute | solution.py:143
  757.2 47.6 %collective-permute-start.18 = (bf16[512,1280]{1,0:T(8,128)(2,1)}, bf16[512,1280]{1,0:T(8,128)(2,1)S(1)}, u32[]{:S(2)}, u32[]{:S(2)}) collective-permute-start(bf16[512,1280]{1,0:T(8,128)(2,1)} %shard_map.53), channel_id=1, source_target_pairs={{0,24},{8,16},{16,8},{24,0},{1,25},{9,17},{17,9},{25,1},{2,26},{10... | collective-permute-start | bytes 3932168 | tf_op jit(solution)/shard_map/ppermute | solution.py:146
  780.5 24.8 %collective-permute-start.21 = (bf16[256,1280]{1,0:T(8,128)(2,1)}, bf16[256,1280]{1,0:T(8,128)(2,1)S(1)}, u32[]{:S(2)}, u32[]{:S(2)}) collective-permute-start(bf16[256,1280]{1,0:T(8,128)(2,1)} %shard_map.56), channel_id=1, source_target_pairs={{0,24},{8,16},{16,8},{24,0},{1,25},{9,17},{17,9},{25,1},{2,26},{10... | collective-permute-start | bytes 1966088 | tf_op jit(solution)/shard_map/ppermute | solution.py:146
  794.5 18.2 %collective-permute-start.24 = (bf16[256,1280]{1,0:T(8,128)(2,1)}, bf16[256,1280]{1,0:T(8,128)(2,1)S(1)}, u32[]{:S(2)}, u32[]{:S(2)}) collective-permute-start(bf16[256,1280]{1,0:T(8,128)(2,1)} %shard_map.57), channel_id=1, source_target_pairs={{0,24},{8,16},{16,8},{24,0},{1,25},{9,17},{17,9},{25,1},{2,26},{10... | collective-permute-start | bytes 1966088 | tf_op jit(solution)/shard_map/ppermute | solution.py:146
  (10 other events, 119.4 us)
Sparse Core Ops, SparseCore 0:
  8.9 167.2 all-gather.4
  177.8 100.1 all-gather.8
  279.6 72.1 all-gather.10
  353.2 163.3 all-gather.6
